TPU v7x, 256 devices: a whole 4x4x8 slice. The times are simulated.
256 devices in a mesh: tm: 16 (over z, core), space: 16 (over y, x).
Axes of the slice: x: 4, y: 4, z: 8, core: 2. Of those that a mesh axis runs over, the one named last changes fastest.
Arguments:
- residual: float32 [64, 32, 128, 128], P('tm', 'space'), may hold values from -6 to 6
- absorption: float32 [32, 128, 128], P('space'), may hold values from 0.05 to 1
- counts: int32 [64], replicated, may hold values from 1 to 6
Outputs:
- preconditioned: float32 [64, 32, 128, 128], P('tm', 'space')
Inputs may be any that keep to these rules, and one draw needn't show every extreme that they name: counts[k] is the number of minimal-residual steps of frequency k.
All inputs are finite; a program needn't handle non-finite values.
Results may differ from a plain program's by a relative error of at most 0.00022.
Values sent between devices are 32-bit elements; how exact they have to be, the bound alone decides.
No kernel may reach another device: no remote copies, remote signals or barrier semaphores. Data moves between devices by JAX's collectives and lax.ppermute only.
A program may use at most 64 MiB of HBM per device.

v0:
```python
import math

import jax
import jax.numpy as jnp
from jax import lax
from jax.sharding import PartitionSpec as P

L = 64


wrap_factor = 0.1
step_size = 1.0
norm_floor = 1e-06
highest = lax.Precision.HIGHEST


def with_halo(cells, sides, width):
    for axis, dim in sides:
        count = lax.axis_size(axis)
        ends = count - 1
        head = lax.slice_in_dim(cells, 0, width, axis=dim)
        tail = lax.slice_in_dim(cells, cells.shape[dim] - width, cells.shape[dim], axis=dim)
        cells = jnp.concatenate(
            [
                lax.ppermute(tail, axis, [(i, (i + 1) % count) for i in range(ends)]),
                cells,
                lax.ppermute(head, axis, [((i + 1) % count, i) for i in range(ends)]),
            ],
            axis=dim,
        )
    return cells


def copy_for_each(shard, axis):
    copies = jnp.broadcast_to(shard, (lax.axis_size(axis), *shard.shape))
    return lax.all_to_all(copies, axis, split_axis=0, concat_axis=0, tiled=True)


def taken_together(shard, axis):
    return copy_for_each(shard, axis).sum(axis=0)


def packed_total(arrays, axis):
    vector, at, finished = (jnp.concatenate([a.reshape(-1) for a in arrays]), 0, [])
    so_far = taken_together(vector, axis)
    for a in arrays:
        finished.append(so_far[at : at + a.size].reshape(a.shape))
        at += a.size
    return tuple(finished)


def shifts(frequency):
    angles = frequency.astype(jnp.float32) * (2.0 * math.pi / L)
    decay_rate = wrap_factor ** (1.0 / L)
    shift_re = (1.0 - decay_rate * jnp.cos(angles)) / step_size
    shift_im = decay_rate * jnp.sin(angles) / step_size
    return (shift_re, shift_im)


def near_sum(padded):
    interior = padded[..., 1:-1, :, :]
    widths = [(0, 0)] * (interior.ndim - 2) + [(1, 1), (1, 1)]
    padded_xy = jnp.pad(interior, widths)
    summed = padded[..., 2:, :, :] + padded[..., :-2, :, :]
    summed = summed + padded_xy[..., 2:, 1:-1] + padded_xy[..., :-2, 1:-1]
    summed = summed + padded_xy[..., 1:-1, 2:] + padded_xy[..., 1:-1, :-2]
    return summed


def advance(carried, dir_re, dir_im, img_re, img_im, coef_re, coef_im):
    sol_re, sol_im, res_re, res_im = carried
    sol_re = sol_re + coef_re * dir_re - coef_im * dir_im
    sol_im = sol_im + coef_re * dir_im + coef_im * dir_re
    res_re = res_re - (coef_re * img_re - coef_im * img_im)
    res_im = res_im - (coef_re * img_im + coef_im * img_re)
    return (sol_re, sol_im, res_re, res_im)


def solve_together(spectrum, absorption, frequencies, step_counts, longest):
    shift_re, shift_im = shifts(frequencies)
    shift_re = shift_re[:, None, None, None]
    shift_im = shift_im[:, None, None, None]
    diag_re = shift_re + 6.0 + absorption[None]
    magnitude = diag_re * diag_re + shift_im * shift_im
    inv_re = diag_re / magnitude
    inv_im = -shift_im / magnitude

    def iterate(iteration, carried):
        res_re, res_im = (carried[2], carried[3])
        dir_re = inv_re * res_re - inv_im * res_im
        dir_im = inv_re * res_im + inv_im * res_re
        padded = with_halo(jnp.stack([dir_re, dir_im], axis=1), (("space", 2),), 1)
        nearby = near_sum(padded)
        img_re = diag_re * dir_re - shift_im * dir_im - nearby[:, 0]
        img_im = diag_re * dir_im + shift_im * dir_re - nearby[:, 1]
        totals = packed_total(
            (
                jnp.sum(img_re * res_re + img_im * res_im, axis=(1, 2, 3)),
                jnp.sum(img_re * res_im - img_im * res_re, axis=(1, 2, 3)),
                jnp.sum(img_re * img_re + img_im * img_im, axis=(1, 2, 3)),
            ),
            "space",
        )
        active = iteration < step_counts
        denominator = totals[2] + norm_floor
        coef_re = jnp.where(active, totals[0] / denominator, 0.0)[:, None, None, None]
        coef_im = jnp.where(active, totals[1] / denominator, 0.0)[:, None, None, None]
        return advance(carried, dir_re, dir_im, img_re, img_im, coef_re, coef_im)

    blank = jnp.zeros_like(spectrum[:, 0])
    finished = lax.fori_loop(0, longest, iterate, (blank, blank, spectrum[:, 0], spectrum[:, 1]))
    return jnp.stack([finished[0], finished[1]], axis=1)


def slot_order():
    return jnp.arange(L, dtype=jnp.int32)


def phase_table(left, right):
    return (left[:, None] * right[None, :] % L).astype(jnp.float32) * (2.0 * math.pi / L)


def body(residual, absorption, counts):
    per_device = residual.shape[0]
    decay_rate = wrap_factor ** (1.0 / L)
    first_step = lax.axis_index("tm") * per_device
    times_here = first_step + jnp.arange(per_device, dtype=jnp.int32)
    scaled = residual * jnp.power(decay_rate, times_here.astype(jnp.float32))[:, None, None, None]
    slot_freqs = slot_order()
    own_freqs = lax.dynamic_slice_in_dim(slot_freqs, first_step, per_device)
    own_counts = counts[own_freqs]
    longest = jnp.max(counts)
    all_times = jnp.arange(L, dtype=jnp.int32)
    series = lax.all_to_all(scaled, "tm", split_axis=2, concat_axis=0, tiled=True)
    phases = phase_table(slot_freqs, all_times)
    real_part = jnp.einsum("sn,nzxy->szxy", jnp.cos(phases), series, precision=highest)
    imag_part = -jnp.einsum("sn,nzxy->szxy", jnp.sin(phases), series, precision=highest)
    spectrum = lax.all_to_all(
        jnp.stack([real_part, imag_part], axis=1), "tm", split_axis=0, concat_axis=3, tiled=True
    )
    solved = solve_together(spectrum, absorption, own_freqs, own_counts, longest)
    gathered = lax.all_to_all(solved, "tm", split_axis=3, concat_axis=0, tiled=True)
    phases = phase_table(all_times, slot_freqs)
    values = jnp.einsum("ns,szxy->nzxy", jnp.cos(phases), gathered[:, 0], precision=highest)
    values = values - jnp.einsum(
        "ns,szxy->nzxy", jnp.sin(phases), gathered[:, 1], precision=highest
    )
    weight = jnp.power(decay_rate, -all_times.astype(jnp.float32)) / L
    values = values * weight[:, None, None, None]
    return lax.all_to_all(values, "tm", split_axis=0, concat_axis=2, tiled=True)


def solution(mesh):
    in_specs = (P("tm", "space", None, None), P("space", None, None), P())
    out_specs = P("tm", "space", None, None)
    return jax.shard_map(body, mesh=mesh, in_specs=in_specs, out_specs=out_specs, check_vma=False)
```

profile of v0, /device:TPU:1, one launch (start us, length us, event | category | flops | bytes accessed | tf_op | source)
XLA Modules:
  0.0 341.6 jit_solution(1226429195683885706)
XLA Ops:
  1.5 27.0 %all_to_all.84 = f32[4,2,128,128]{3,0,1,2:T(4,128)S(1)} all-to-all(f32[4,2,128,128]{3,0,1,2:T(4,128)S(1)} %copy.60), channel_id=1, replica_groups=mesh['tm'=16,'space'=16] {'tm'}, dimensions={2} | all-to-all | bytes 1048576 | tf_op jit(solution)/shard_map/all_to_all | solution.py:134
  31.8 3.7 %all-to-all-start.2 = ((f32[64,2,2,8,128]{4,3,2,1,0:T(8,128)}), f32[64,2,2,8,128]{4,3,2,1,0:T(8,128)S(1)}, u32[]{:S(2)}, u32[]{:S(2)}) async-start(f32[64,2,2,8,128]{4,3,2,1,0:T(8,128)} %copy.62), calls=%async_computation.2 | async-start | bytes 2097152 | tf_op jit(solution)/shard_map/all_to_all | solution.py:138
  37.0 25.8 %all-to-all-done.2 = f32[64,2,2,8,128]{4,3,2,1,0:T(8,128)S(1)} async-done(((f32[64,2,2,8,128]{4,3,2,1,0:T(8,128)}), f32[64,2,2,8,128]{4,3,2,1,0:T(8,128)S(1)}, u32[]{:S(2)}, u32[]{:S(2)}) %all-to-all-start.2) | async-done | bytes 1048608 | tf_op jit(solution)/shard_map/all_to_all | solution.py:138
  64.7 204.2 %while.20 = (s32[]{:T(128)}, f32[4,2,128,128]{3,2,1,0:T(8,128)}, f32[4,2,128,128]{3,2,1,0:T(8,128)}, f32[4,2,128,128]{3,2,1,0:T(8,128)S(1)}, f32[4,2,128,128]{3,...) while((s32[]{:T(128)}, f32[4,2,128,128]{3,2,1,0:T(8,128)}, ...), condition=%wide.region_6.7_spmd.clone.clone, body=%wide.region_1.6_spmd.clone.clone.sunk | while | flops 9175258 | bytes 25447364 | solution.py:111
  65.8 3.2 collective-permute-start
  70.3 9.4 %collective-permute-done = f32[4,2,1,128,128]{4,3,2,0,1:T(8,128)S(1)} collective-permute-done((f32[4,2,1,128,128]{4,3,2,0,1:T(8,128)S(1)}, f32[4,2,1,128,128]{4,3,2,0,1:T(8,128)S(1)}, u32[]{:S(2)}, u32[]{:S(2)}) %collective-permute-start) | collective-permute-done | bytes 524320 | tf_op jit(solution)/shard_map/while/body/ppermute | solution.py:25
  79.8 4.1 %collective-permute-done.1 = f32[4,2,1,128,128]{4,3,2,0,1:T(8,128)S(1)} collective-permute-done((f32[4,2,1,128,128]{4,3,2,0,1:T(8,128)S(1)}, f32[4,2,1,128,128]{4,3,2,0,1:T(8,128)S(1)}, u32[]{:S(2)}, u32[]{:S(2)}) %collective-permute-start.1) | collective-permute-done | bytes 524320 | tf_op jit(solution)/shard_map/while/body/ppermute | solution.py:27
  85.9 8.3 %all-to-all-start = ((f32[16,1,12]{2,1,0:T(1,128)}), f32[16,1,12]{2,1,0:T(1,128)S(1)}, u32[]{:S(2)}, u32[]{:S(2)}) async-start(f32[16,1,12]{2,1,0:T(1,128)} %broadcast_in_dim.42), calls=%async_computation | async-start | bytes 16384 | tf_op jit(solution)/shard_map/while/body/all_to_all | solution.py:36
  94.2 6.4 %all-to-all-done = f32[16,1,12]{2,1,0:T(1,128)S(1)} async-done(((f32[16,1,12]{2,1,0:T(1,128)}), f32[16,1,12]{2,1,0:T(1,128)S(1)}, u32[]{:S(2)}, u32[]{:S(2)}) %all-to-all-start) | async-done | bytes 800 | tf_op jit(solution)/shard_map/while/body/all_to_all | solution.py:36
  108.1 8.1 %collective-permute-done = f32[4,2,1,128,128]{4,3,2,0,1:T(8,128)S(1)} collective-permute-done((f32[4,2,1,128,128]{4,3,2,0,1:T(8,128)S(1)}, f32[4,2,1,128,128]{4,3,2,0,1:T(8,128)S(1)}, u32[]{:S(2)}, u32[]{:S(2)}) %collective-permute-start) | collective-permute-done | bytes 524320 | tf_op jit(solution)/shard_map/while/body/ppermute | solution.py:25
  116.2 3.9 %collective-permute-done.1 = f32[4,2,1,128,128]{4,3,2,0,1:T(8,128)S(1)} collective-permute-done((f32[4,2,1,128,128]{4,3,2,0,1:T(8,128)S(1)}, f32[4,2,1,128,128]{4,3,2,0,1:T(8,128)S(1)}, u32[]{:S(2)}, u32[]{:S(2)}) %collective-permute-start.1) | collective-permute-done | bytes 524320 | tf_op jit(solution)/shard_map/while/body/ppermute | solution.py:27
  122.1 7.8 %all-to-all-start = ((f32[16,1,12]{2,1,0:T(1,128)}), f32[16,1,12]{2,1,0:T(1,128)S(1)}, u32[]{:S(2)}, u32[]{:S(2)}) async-start(f32[16,1,12]{2,1,0:T(1,128)} %broadcast_in_dim.42), calls=%async_computation | async-start | bytes 16384 | tf_op jit(solution)/shard_map/while/body/all_to_all | solution.py:36
  129.9 6.4 %all-to-all-done = f32[16,1,12]{2,1,0:T(1,128)S(1)} async-done(((f32[16,1,12]{2,1,0:T(1,128)}), f32[16,1,12]{2,1,0:T(1,128)S(1)}, u32[]{:S(2)}, u32[]{:S(2)}) %all-to-all-start) | async-done | bytes 800 | tf_op jit(solution)/shard_map/while/body/all_to_all | solution.py:36
  143.8 5.7 %collective-permute-done = f32[4,2,1,128,128]{4,3,2,0,1:T(8,128)S(1)} collective-permute-done((f32[4,2,1,128,128]{4,3,2,0,1:T(8,128)S(1)}, f32[4,2,1,128,128]{4,3,2,0,1:T(8,128)S(1)}, u32[]{:S(2)}, u32[]{:S(2)}) %collective-permute-start) | collective-permute-done | bytes 524320 | tf_op jit(solution)/shard_map/while/body/ppermute | solution.py:25
  149.5 3.9 %collective-permute-done.1 = f32[4,2,1,128,128]{4,3,2,0,1:T(8,128)S(1)} collective-permute-done((f32[4,2,1,128,128]{4,3,2,0,1:T(8,128)S(1)}, f32[4,2,1,128,128]{4,3,2,0,1:T(8,128)S(1)}, u32[]{:S(2)}, u32[]{:S(2)}) %collective-permute-start.1) | collective-permute-done | bytes 524320 | tf_op jit(solution)/shard_map/while/body/ppermute | solution.py:27
  155.3 7.8 %all-to-all-start = ((f32[16,1,12]{2,1,0:T(1,128)}), f32[16,1,12]{2,1,0:T(1,128)S(1)}, u32[]{:S(2)}, u32[]{:S(2)}) async-start(f32[16,1,12]{2,1,0:T(1,128)} %broadcast_in_dim.42), calls=%async_computation | async-start | bytes 16384 | tf_op jit(solution)/shard_map/while/body/all_to_all | solution.py:36
  163.2 6.4 %all-to-all-done = f32[16,1,12]{2,1,0:T(1,128)S(1)} async-done(((f32[16,1,12]{2,1,0:T(1,128)}), f32[16,1,12]{2,1,0:T(1,128)S(1)}, u32[]{:S(2)}, u32[]{:S(2)}) %all-to-all-start) | async-done | bytes 800 | tf_op jit(solution)/shard_map/while/body/all_to_all | solution.py:36
  177.0 4.7 %collective-permute-done = f32[4,2,1,128,128]{4,3,2,0,1:T(8,128)S(1)} collective-permute-done((f32[4,2,1,128,128]{4,3,2,0,1:T(8,128)S(1)}, f32[4,2,1,128,128]{4,3,2,0,1:T(8,128)S(1)}, u32[]{:S(2)}, u32[]{:S(2)}) %collective-permute-start) | collective-permute-done | bytes 524320 | tf_op jit(solution)/shard_map/while/body/ppermute | solution.py:25
  181.7 3.8 %collective-permute-done.1 = f32[4,2,1,128,128]{4,3,2,0,1:T(8,128)S(1)} collective-permute-done((f32[4,2,1,128,128]{4,3,2,0,1:T(8,128)S(1)}, f32[4,2,1,128,128]{4,3,2,0,1:T(8,128)S(1)}, u32[]{:S(2)}, u32[]{:S(2)}) %collective-permute-start.1) | collective-permute-done | bytes 524320 | tf_op jit(solution)/shard_map/while/body/ppermute | solution.py:27
  187.6 7.5 %all-to-all-start = ((f32[16,1,12]{2,1,0:T(1,128)}), f32[16,1,12]{2,1,0:T(1,128)S(1)}, u32[]{:S(2)}, u32[]{:S(2)}) async-start(f32[16,1,12]{2,1,0:T(1,128)} %broadcast_in_dim.42), calls=%async_computation | async-start | bytes 16384 | tf_op jit(solution)/shard_map/while/body/all_to_all | solution.py:36
  195.1 6.4 %all-to-all-done = f32[16,1,12]{2,1,0:T(1,128)S(1)} async-done(((f32[16,1,12]{2,1,0:T(1,128)}), f32[16,1,12]{2,1,0:T(1,128)S(1)}, u32[]{:S(2)}, u32[]{:S(2)}) %all-to-all-start) | async-done | bytes 800 | tf_op jit(solution)/shard_map/while/body/all_to_all | solution.py:36
  209.0 4.7 %collective-permute-done = f32[4,2,1,128,128]{4,3,2,0,1:T(8,128)S(1)} collective-permute-done((f32[4,2,1,128,128]{4,3,2,0,1:T(8,128)S(1)}, f32[4,2,1,128,128]{4,3,2,0,1:T(8,128)S(1)}, u32[]{:S(2)}, u32[]{:S(2)}) %collective-permute-start) | collective-permute-done | bytes 524320 | tf_op jit(solution)/shard_map/while/body/ppermute | solution.py:25
  213.6 3.8 %collective-permute-done.1 = f32[4,2,1,128,128]{4,3,2,0,1:T(8,128)S(1)} collective-permute-done((f32[4,2,1,128,128]{4,3,2,0,1:T(8,128)S(1)}, f32[4,2,1,128,128]{4,3,2,0,1:T(8,128)S(1)}, u32[]{:S(2)}, u32[]{:S(2)}) %collective-permute-start.1) | collective-permute-done | bytes 524320 | tf_op jit(solution)/shard_map/while/body/ppermute | solution.py:27
  219.5 7.5 %all-to-all-start = ((f32[16,1,12]{2,1,0:T(1,128)}), f32[16,1,12]{2,1,0:T(1,128)S(1)}, u32[]{:S(2)}, u32[]{:S(2)}) async-start(f32[16,1,12]{2,1,0:T(1,128)} %broadcast_in_dim.42), calls=%async_computation | async-start | bytes 16384 | tf_op jit(solution)/shard_map/while/body/all_to_all | solution.py:36
  227.0 6.4 %all-to-all-done = f32[16,1,12]{2,1,0:T(1,128)S(1)} async-done(((f32[16,1,12]{2,1,0:T(1,128)}), f32[16,1,12]{2,1,0:T(1,128)S(1)}, u32[]{:S(2)}, u32[]{:S(2)}) %all-to-all-start) | async-done | bytes 800 | tf_op jit(solution)/shard_map/while/body/all_to_all | solution.py:36
  240.9 4.7 %collective-permute-done = f32[4,2,1,128,128]{4,3,2,0,1:T(8,128)S(1)} collective-permute-done((f32[4,2,1,128,128]{4,3,2,0,1:T(8,128)S(1)}, f32[4,2,1,128,128]{4,3,2,0,1:T(8,128)S(1)}, u32[]{:S(2)}, u32[]{:S(2)}) %collective-permute-start) | collective-permute-done | bytes 524320 | tf_op jit(solution)/shard_map/while/body/ppermute | solution.py:25
  245.6 3.8 %collective-permute-done.1 = f32[4,2,1,128,128]{4,3,2,0,1:T(8,128)S(1)} collective-permute-done((f32[4,2,1,128,128]{4,3,2,0,1:T(8,128)S(1)}, f32[4,2,1,128,128]{4,3,2,0,1:T(8,128)S(1)}, u32[]{:S(2)}, u32[]{:S(2)}) %collective-permute-start.1) | collective-permute-done | bytes 524320 | tf_op jit(solution)/shard_map/while/body/ppermute | solution.py:27
  251.4 7.5 %all-to-all-start = ((f32[16,1,12]{2,1,0:T(1,128)}), f32[16,1,12]{2,1,0:T(1,128)S(1)}, u32[]{:S(2)}, u32[]{:S(2)}) async-start(f32[16,1,12]{2,1,0:T(1,128)} %broadcast_in_dim.42), calls=%async_computation | async-start | bytes 16384 | tf_op jit(solution)/shard_map/while/body/all_to_all | solution.py:36
  258.9 6.4 %all-to-all-done = f32[16,1,12]{2,1,0:T(1,128)S(1)} async-done(((f32[16,1,12]{2,1,0:T(1,128)}), f32[16,1,12]{2,1,0:T(1,128)S(1)}, u32[]{:S(2)}, u32[]{:S(2)}) %all-to-all-start) | async-done | bytes 800 | tf_op jit(solution)/shard_map/while/body/all_to_all | solution.py:36
  272.4 17.8 %all-to-all-start.3 = ((f32[4,2,2,128,128]{4,2,0,1,3:T(2,128)}), f32[4,2,2,128,128]{4,2,0,1,3:T(2,128)S(1)}, u32[]{:S(2)}, u32[]{:S(2)}) async-start(f32[4,2,2,128,128]{4,2,0,1,3:T(2,128)} %pad_maximum_fusion.7), calls=%async_computation.3 | async-start | bytes 2097152 | tf_op jit(solution)/shard_map/all_to_all | solution.py:142
  290.2 28.0 %all-to-all-done.3 = f32[4,2,2,128,128]{4,2,0,1,3:T(2,128)S(1)} async-done(((f32[4,2,2,128,128]{4,2,0,1,3:T(2,128)}), f32[4,2,2,128,128]{4,2,0,1,3:T(2,128)S(1)}, u32[]{:S(2)}, u32[]{:S(2)}) %all-to-all-start.3) | async-done | bytes 1048608 | tf_op jit(solution)/shard_map/all_to_all | solution.py:142
  320.3 20.4 %all_to_all.85 = f32[64,2,8,128]{3,2,1,0:T(8,128)S(1)} all-to-all(f32[64,2,8,128]{3,2,1,0:T(8,128)S(1)} %copy.67), channel_id=1, replica_groups=mesh['tm'=16,'space'=16] {'tm'}, dimensions={0} | all-to-all | bytes 1048576 | tf_op jit(solution)/shard_map/all_to_all | solution.py:150
  (102 shorter events, 64.6 us)
Async XLA Ops:
  31.8 3.9 %copy-start = (s32[64]{0:T(128)S(1)}, s32[64]{0:T(128)}, u32[]{:S(2)}) copy-start(s32[64]{0:T(128)} %param.7) | copy-start | bytes 772
  31.8 31.0 %all-to-all-start.2 = ((f32[64,2,2,8,128]{4,3,2,1,0:T(8,128)}), f32[64,2,2,8,128]{4,3,2,1,0:T(8,128)S(1)}, u32[]{:S(2)}, u32[]{:S(2)}) async-start(f32[64,2,2,8,128]{4,3,2,1,0:T(8,128)} %copy.62), calls=%async_computation.2 | async-start | bytes 2097152 | tf_op jit(solution)/shard_map/all_to_all | solution.py:138
  63.0 1.7 copy-start.1
  65.8 14.0 %collective-permute-start = (f32[4,2,1,128,128]{4,3,2,0,1:T(8,128)S(1)}, f32[4,2,1,128,128]{4,3,2,0,1:T(8,128)S(1)}, u32[]{:S(2)}, u32[]{:S(2)}) collective-permute-start(f32[4,2,1,128,128]{4,3,2,0,1:T(8,128)S(1)} %get-tuple-element.368), channel_id=1, source_target_pairs={{0,1},{1,2},{2,3},{3,4},{4,5},{5,6},{6,7},{7,8},{8,9},{9,10},{10,1... | collective-permute-start | bytes 1572872 | tf_op jit(solution)/shard_map/while/body/ppermute | solution.py:25
  68.9 15.0 %collective-permute-start.1 = (f32[4,2,1,128,128]{4,3,2,0,1:T(8,128)S(1)}, f32[4,2,1,128,128]{4,3,2,0,1:T(8,128)S(1)}, u32[]{:S(2)}, u32[]{:S(2)}) collective-permute-start(f32[4,2,1,128,128]{4,3,2,0,1:T(8,128)S(1)} %get-tuple-element.369), channel_id=1, source_target_pairs={{1,0},{2,1},{3,2},{4,3},{5,4},{6,5},{7,6},{8,7},{9,8},{10,9},{11,1... | collective-permute-start | bytes 1572872 | tf_op jit(solution)/shard_map/while/body/ppermute | solution.py:27
  85.9 14.7 %all-to-all-start = ((f32[16,1,12]{2,1,0:T(1,128)}), f32[16,1,12]{2,1,0:T(1,128)S(1)}, u32[]{:S(2)}, u32[]{:S(2)}) async-start(f32[16,1,12]{2,1,0:T(1,128)} %broadcast_in_dim.42), calls=%async_computation | async-start | bytes 16384 | tf_op jit(solution)/shard_map/while/body/all_to_all | solution.py:36
  104.6 11.6 %collective-permute-start = (f32[4,2,1,128,128]{4,3,2,0,1:T(8,128)S(1)}, f32[4,2,1,128,128]{4,3,2,0,1:T(8,128)S(1)}, u32[]{:S(2)}, u32[]{:S(2)}) collective-permute-start(f32[4,2,1,128,128]{4,3,2,0,1:T(8,128)S(1)} %get-tuple-element.368), channel_id=1, source_target_pairs={{0,1},{1,2},{2,3},{3,4},{4,5},{5,6},{6,7},{7,8},{8,9},{9,10},{10,1... | collective-permute-start | bytes 1572872 | tf_op jit(solution)/shard_map/while/body/ppermute | solution.py:25
  106.7 13.4 %collective-permute-start.1 = (f32[4,2,1,128,128]{4,3,2,0,1:T(8,128)S(1)}, f32[4,2,1,128,128]{4,3,2,0,1:T(8,128)S(1)}, u32[]{:S(2)}, u32[]{:S(2)}) collective-permute-start(f32[4,2,1,128,128]{4,3,2,0,1:T(8,128)S(1)} %get-tuple-element.369), channel_id=1, source_target_pairs={{1,0},{2,1},{3,2},{4,3},{5,4},{6,5},{7,6},{8,7},{9,8},{10,9},{11,1... | collective-permute-start | bytes 1572872 | tf_op jit(solution)/shard_map/while/body/ppermute | solution.py:27
  122.1 14.3 %all-to-all-start = ((f32[16,1,12]{2,1,0:T(1,128)}), f32[16,1,12]{2,1,0:T(1,128)S(1)}, u32[]{:S(2)}, u32[]{:S(2)}) async-start(f32[16,1,12]{2,1,0:T(1,128)} %broadcast_in_dim.42), calls=%async_computation | async-start | bytes 16384 | tf_op jit(solution)/shard_map/while/body/all_to_all | solution.py:36
  140.3 9.2 %collective-permute-start = (f32[4,2,1,128,128]{4,3,2,0,1:T(8,128)S(1)}, f32[4,2,1,128,128]{4,3,2,0,1:T(8,128)S(1)}, u32[]{:S(2)}, u32[]{:S(2)}) collective-permute-start(f32[4,2,1,128,128]{4,3,2,0,1:T(8,128)S(1)} %get-tuple-element.368), channel_id=1, source_target_pairs={{0,1},{1,2},{2,3},{3,4},{4,5},{5,6},{6,7},{7,8},{8,9},{9,10},{10,1... | collective-permute-start | bytes 1572872 | tf_op jit(solution)/shard_map/while/body/ppermute | solution.py:25
  142.4 11.0 %collective-permute-start.1 = (f32[4,2,1,128,128]{4,3,2,0,1:T(8,128)S(1)}, f32[4,2,1,128,128]{4,3,2,0,1:T(8,128)S(1)}, u32[]{:S(2)}, u32[]{:S(2)}) collective-permute-start(f32[4,2,1,128,128]{4,3,2,0,1:T(8,128)S(1)} %get-tuple-element.369), channel_id=1, source_target_pairs={{1,0},{2,1},{3,2},{4,3},{5,4},{6,5},{7,6},{8,7},{9,8},{10,9},{11,1... | collective-permute-start | bytes 1572872 | tf_op jit(solution)/shard_map/while/body/ppermute | solution.py:27
  155.3 14.3 %all-to-all-start = ((f32[16,1,12]{2,1,0:T(1,128)}), f32[16,1,12]{2,1,0:T(1,128)S(1)}, u32[]{:S(2)}, u32[]{:S(2)}) async-start(f32[16,1,12]{2,1,0:T(1,128)} %broadcast_in_dim.42), calls=%async_computation | async-start | bytes 16384 | tf_op jit(solution)/shard_map/while/body/all_to_all | solution.py:36
  173.6 8.2 %collective-permute-start = (f32[4,2,1,128,128]{4,3,2,0,1:T(8,128)S(1)}, f32[4,2,1,128,128]{4,3,2,0,1:T(8,128)S(1)}, u32[]{:S(2)}, u32[]{:S(2)}) collective-permute-start(f32[4,2,1,128,128]{4,3,2,0,1:T(8,128)S(1)} %get-tuple-element.368), channel_id=1, source_target_pairs={{0,1},{1,2},{2,3},{3,4},{4,5},{5,6},{6,7},{7,8},{8,9},{9,10},{10,1... | collective-permute-start | bytes 1572872 | tf_op jit(solution)/shard_map/while/body/ppermute | solution.py:25
  175.6 9.9 %collective-permute-start.1 = (f32[4,2,1,128,128]{4,3,2,0,1:T(8,128)S(1)}, f32[4,2,1,128,128]{4,3,2,0,1:T(8,128)S(1)}, u32[]{:S(2)}, u32[]{:S(2)}) collective-permute-start(f32[4,2,1,128,128]{4,3,2,0,1:T(8,128)S(1)} %get-tuple-element.369), channel_id=1, source_target_pairs={{1,0},{2,1},{3,2},{4,3},{5,4},{6,5},{7,6},{8,7},{9,8},{10,9},{11,1... | collective-permute-start | bytes 1572872 | tf_op jit(solution)/shard_map/while/body/ppermute | solution.py:27
  187.6 14.0 %all-to-all-start = ((f32[16,1,12]{2,1,0:T(1,128)}), f32[16,1,12]{2,1,0:T(1,128)S(1)}, u32[]{:S(2)}, u32[]{:S(2)}) async-start(f32[16,1,12]{2,1,0:T(1,128)} %broadcast_in_dim.42), calls=%async_computation | async-start | bytes 16384 | tf_op jit(solution)/shard_map/while/body/all_to_all | solution.py:36
  205.5 8.2 %collective-permute-start = (f32[4,2,1,128,128]{4,3,2,0,1:T(8,128)S(1)}, f32[4,2,1,128,128]{4,3,2,0,1:T(8,128)S(1)}, u32[]{:S(2)}, u32[]{:S(2)}) collective-permute-start(f32[4,2,1,128,128]{4,3,2,0,1:T(8,128)S(1)} %get-tuple-element.368), channel_id=1, source_target_pairs={{0,1},{1,2},{2,3},{3,4},{4,5},{5,6},{6,7},{7,8},{8,9},{9,10},{10,1... | collective-permute-start | bytes 1572872 | tf_op jit(solution)/shard_map/while/body/ppermute | solution.py:25
  207.6 9.9 %collective-permute-start.1 = (f32[4,2,1,128,128]{4,3,2,0,1:T(8,128)S(1)}, f32[4,2,1,128,128]{4,3,2,0,1:T(8,128)S(1)}, u32[]{:S(2)}, u32[]{:S(2)}) collective-permute-start(f32[4,2,1,128,128]{4,3,2,0,1:T(8,128)S(1)} %get-tuple-element.369), channel_id=1, source_target_pairs={{1,0},{2,1},{3,2},{4,3},{5,4},{6,5},{7,6},{8,7},{9,8},{10,9},{11,1... | collective-permute-start | bytes 1572872 | tf_op jit(solution)/shard_map/while/body/ppermute | solution.py:27
  219.5 14.0 %all-to-all-start = ((f32[16,1,12]{2,1,0:T(1,128)}), f32[16,1,12]{2,1,0:T(1,128)S(1)}, u32[]{:S(2)}, u32[]{:S(2)}) async-start(f32[16,1,12]{2,1,0:T(1,128)} %broadcast_in_dim.42), calls=%async_computation | async-start | bytes 16384 | tf_op jit(solution)/shard_map/while/body/all_to_all | solution.py:36
  237.4 8.2 %collective-permute-start = (f32[4,2,1,128,128]{4,3,2,0,1:T(8,128)S(1)}, f32[4,2,1,128,128]{4,3,2,0,1:T(8,128)S(1)}, u32[]{:S(2)}, u32[]{:S(2)}) collective-permute-start(f32[4,2,1,128,128]{4,3,2,0,1:T(8,128)S(1)} %get-tuple-element.368), channel_id=1, source_target_pairs={{0,1},{1,2},{2,3},{3,4},{4,5},{5,6},{6,7},{7,8},{8,9},{9,10},{10,1... | collective-permute-start | bytes 1572872 | tf_op jit(solution)/shard_map/while/body/ppermute | solution.py:25
  239.5 9.9 %collective-permute-start.1 = (f32[4,2,1,128,128]{4,3,2,0,1:T(8,128)S(1)}, f32[4,2,1,128,128]{4,3,2,0,1:T(8,128)S(1)}, u32[]{:S(2)}, u32[]{:S(2)}) collective-permute-start(f32[4,2,1,128,128]{4,3,2,0,1:T(8,128)S(1)} %get-tuple-element.369), channel_id=1, source_target_pairs={{1,0},{2,1},{3,2},{4,3},{5,4},{6,5},{7,6},{8,7},{9,8},{10,9},{11,1... | collective-permute-start | bytes 1572872 | tf_op jit(solution)/shard_map/while/body/ppermute | solution.py:27
  251.4 14.0 %all-to-all-start = ((f32[16,1,12]{2,1,0:T(1,128)}), f32[16,1,12]{2,1,0:T(1,128)S(1)}, u32[]{:S(2)}, u32[]{:S(2)}) async-start(f32[16,1,12]{2,1,0:T(1,128)} %broadcast_in_dim.42), calls=%async_computation | async-start | bytes 16384 | tf_op jit(solution)/shard_map/while/body/all_to_all | solution.py:36
  272.4 45.9 %all-to-all-start.3 = ((f32[4,2,2,128,128]{4,2,0,1,3:T(2,128)}), f32[4,2,2,128,128]{4,2,0,1,3:T(2,128)S(1)}, u32[]{:S(2)}, u32[]{:S(2)}) async-start(f32[4,2,2,128,128]{4,2,0,1,3:T(2,128)} %pad_maximum_fusion.7), calls=%async_computation.3 | async-start | bytes 2097152 | tf_op jit(solution)/shard_map/all_to_all | solution.py:142
where the time goes:
time: 343 us; the launch traced here: 342 us
  waiting for transfers between devices  153 us (45%)
  starting transfers between devices  89.2 us (26%)
  blocking collectives  47.4 us (14%)
  other arithmetic  32 us (9%)
  local copies, waits for them, and re-layouts  11.6 us (3%)
  loops' own time  5.21 us (2%)
    all_to_all x6, starting transfers between devices, copy_for_each(): return lax.all_to_all(copies, axis, split_axis=0, concat_axis=0, tiled=True)  46.4 us
    all_to_all x6, waiting for transfers between devices, copy_for_each(): return lax.all_to_all(copies, axis, split_axis=0, concat_axis=0, tiled=True)  38.6 us
    ppermute x6, waiting for transfers between devices, with_halo(): lax.ppermute(tail, axis, [(i, (i + 1) % count) for i in range(ends)])  37.3 us
    all_to_all x1, waiting for transfers between devices, body(): lax.all_to_all(solved, 'tm', split_axis=3, concat_axis=0, tiled=True)  28 us
    all_to_all x1, blocking collectives, body(): lax.all_to_all(scaled, 'tm', split_axis=2, concat_axis=0, tiled=True)  27 us
    all_to_all x1, waiting for transfers between devices, body(): lax.all_to_all(jnp.stack([real_part, imag_part], axis=1), 'tm', split_axi...  25.8 us
    ppermute x6, waiting for transfers between devices, with_halo(): lax.ppermute(head, axis, [((i + 1) % count, i) for i in range(ends)])  23.4 us
    all_to_all x1, blocking collectives, body(): return lax.all_to_all(values, 'tm', split_axis=0, concat_axis=2, tiled=True)  20.4 us
  transfers between devices with their start and end apart: 20, of which 20 were waited for; matrix products, arithmetic and copies ran while one was open for 1% of the time, Pallas kernels for 0%

commit v1 on v0

--- a/solution.py
+++ b/solution.py
@@ -2,16 +2,29 @@
 
 import jax
 import jax.numpy as jnp
+import numpy as np
 from jax import lax
+from jax.experimental import pallas as pl
+from jax.experimental.pallas import tpu as pltpu
+from jax.sharding import Mesh
 from jax.sharding import PartitionSpec as P
 
 L = 64
-
+STEPS = 6
+NZ = 32
+PAIRS = L // 2
+TM = ("z", "core")
+SPACE = ("y", "x")
+SLOTS = ("core", "y", "x")
 
 wrap_factor = 0.1
 step_size = 1.0
 norm_floor = 1e-06
 highest = lax.Precision.HIGHEST
+decay = wrap_factor ** (1.0 / L)
+
+gram_rounding = 2.5e-7
+error_allowed = 5e-4
 
 
 def with_halo(cells, sides, width):
@@ -89,7 +102,7 @@
         res_re, res_im = (carried[2], carried[3])
         dir_re = inv_re * res_re - inv_im * res_im
         dir_im = inv_re * res_im + inv_im * res_re
-        padded = with_halo(jnp.stack([dir_re, dir_im], axis=1), (("space", 2),), 1)
+        padded = with_halo(jnp.stack([dir_re, dir_im], axis=1), ((SPACE, 2),), 1)
         nearby = near_sum(padded)
         img_re = diag_re * dir_re - shift_im * dir_im - nearby[:, 0]
         img_im = diag_re * dir_im + shift_im * dir_re - nearby[:, 1]
@@ -99,7 +112,7 @@
                 jnp.sum(img_re * res_im - img_im * res_re, axis=(1, 2, 3)),
                 jnp.sum(img_re * img_re + img_im * img_im, axis=(1, 2, 3)),
             ),
-            "space",
+            SPACE,
         )
         active = iteration < step_counts
         denominator = totals[2] + norm_floor
@@ -120,10 +133,10 @@
     return (left[:, None] * right[None, :] % L).astype(jnp.float32) * (2.0 * math.pi / L)
 
 
-def body(residual, absorption, counts):
+def stepwise(residual, absorption, counts):
     per_device = residual.shape[0]
     decay_rate = wrap_factor ** (1.0 / L)
-    first_step = lax.axis_index("tm") * per_device
+    first_step = lax.axis_index(TM) * per_device
     times_here = first_step + jnp.arange(per_device, dtype=jnp.int32)
     scaled = residual * jnp.power(decay_rate, times_here.astype(jnp.float32))[:, None, None, None]
     slot_freqs = slot_order()
@@ -131,15 +144,15 @@
     own_counts = counts[own_freqs]
     longest = jnp.max(counts)
     all_times = jnp.arange(L, dtype=jnp.int32)
-    series = lax.all_to_all(scaled, "tm", split_axis=2, concat_axis=0, tiled=True)
+    series = lax.all_to_all(scaled, TM, split_axis=2, concat_axis=0, tiled=True)
     phases = phase_table(slot_freqs, all_times)
     real_part = jnp.einsum("sn,nzxy->szxy", jnp.cos(phases), series, precision=highest)
     imag_part = -jnp.einsum("sn,nzxy->szxy", jnp.sin(phases), series, precision=highest)
     spectrum = lax.all_to_all(
-        jnp.stack([real_part, imag_part], axis=1), "tm", split_axis=0, concat_axis=3, tiled=True
+        jnp.stack([real_part, imag_part], axis=1), TM, split_axis=0, concat_axis=3, tiled=True
     )
     solved = solve_together(spectrum, absorption, own_freqs, own_counts, longest)
-    gathered = lax.all_to_all(solved, "tm", split_axis=3, concat_axis=0, tiled=True)
+    gathered = lax.all_to_all(solved, TM, split_axis=3, concat_axis=0, tiled=True)
     phases = phase_table(all_times, slot_freqs)
     values = jnp.einsum("ns,szxy->nzxy", jnp.cos(phases), gathered[:, 0], precision=highest)
     values = values - jnp.einsum(
@@ -147,10 +160,386 @@
     )
     weight = jnp.power(decay_rate, -all_times.astype(jnp.float32)) / L
     values = values * weight[:, None, None, None]
-    return lax.all_to_all(values, "tm", split_axis=0, concat_axis=2, tiled=True)
+    return lax.all_to_all(values, TM, split_axis=0, concat_axis=2, tiled=True)
+
+
+def real_transform(x):
+    n = len(x)
+    if n == 2:
+        return [(x[0] + x[1], None), (x[0] - x[1], None)]
+    even, odd = real_transform(x[0::2]), real_transform(x[1::2])
+    out = [None] * (n // 2 + 1)
+    out[0] = (even[0][0] + odd[0][0], None)
+    out[n // 2] = (even[0][0] - odd[0][0], None)
+    out[n // 4] = (even[n // 4][0], -odd[n // 4][0])
+    for k in range(1, n // 4):
+        cos, sin = math.cos(2 * math.pi * k / n), math.sin(2 * math.pi * k / n)
+        (er, ei), (cr, ci) = even[k], odd[k]
+        tr, ti = cos * cr + sin * ci, cos * ci - sin * cr
+        out[k] = (er + tr, ei + ti)
+        out[n // 2 - k] = (er - tr, ti - ei)
+    return out
+
+
+def real_inverse(spectrum):
+    n = 2 * (len(spectrum) - 1)
+    first, last = spectrum[0][0], spectrum[n // 2][0]
+    if n == 2:
+        return [first + last, first - last]
+    even, odd = [None] * (n // 4 + 1), [None] * (n // 4 + 1)
+    even[0], odd[0] = (first + last, None), (first - last, None)
+    mid_re, mid_im = spectrum[n // 4]
+    even[n // 4], odd[n // 4] = (mid_re + mid_re, None), (-(mid_im + mid_im), None)
+    for k in range(1, n // 4):
+        cos, sin = math.cos(2 * math.pi * k / n), math.sin(2 * math.pi * k / n)
+        (ar, ai), (br, bi) = spectrum[k], spectrum[n // 2 - k]
+        even[k] = (ar + br, ai - bi)
+        tr, ti = ar - br, ai + bi
+        odd[k] = (cos * tr - sin * ti, cos * ti + sin * tr)
+    halves = real_inverse(even), real_inverse(odd)
+    return [halves[i % 2][i // 2] for i in range(n)]
+
+
+def forward_kernel(x_ref, out_ref):
+    for zz in range(2):
+        spectrum = real_transform([x_ref[n, zz] * decay**n for n in range(L)])
+        out_ref[0, 0, zz] = spectrum[0][0]
+        out_ref[0, 1, zz] = spectrum[PAIRS][0]
+        for k in range(1, PAIRS):
+            out_ref[k, 0, zz] = spectrum[k][0]
+            out_ref[k, 1, zz] = spectrum[k][1]
+
+
+def inverse_kernel(s_ref, out_ref):
+    for zz in range(2):
+        ends = [s_ref[0, part, zz] for part in range(2)]
+        spectrum = [(ends[0] + ends[0], None)]
+        spectrum += [(s_ref[k, 0, zz], s_ref[k, 1, zz]) for k in range(1, PAIRS)]
+        spectrum += [(ends[1] + ends[1], None)]
+        values = real_inverse(spectrum)
+        for n in range(L):
+            out_ref[n, zz] = values[n] * (decay ** (-n) / (2 * L))
+
+
+same = [(i, j) for i in range(STEPS + 1) for j in range(i, STEPS + 1)]
+cross = [(i, j) for i in range(STEPS + 1) for j in range(i + 1, STEPS + 1)]
+entry = {(kind, i, j): None for kind, ij in (("re", same), ("im", same), ("x", cross)) for i, j in ij}
+for at, name in enumerate(entry):
+    entry[name] = at
+
+
+def tree_sum(terms):
+    while len(terms) > 1:
+        terms = [sum(terms[i : i + 2][1:], terms[i]) for i in range(0, len(terms), 2)]
+    return terms[0]
+
+
+def basis_kernel(at_ref, shift_ref, own_ref, left_ref, right_ref, abs_ref, v_ref, inv_ref, gram_ref, u, edge, edge_inv, last, sums):
+    slot, z = at_ref[0], at_ref[1]
+    shift_a, shift_b, shift_im = (shift_ref[slot, i] for i in range(3))
+    lanes = lax.broadcasted_iota(jnp.int32, (8, 128), 1)
+    first_lane, last_lane = lanes == 0, lanes == 127
+    blank = jnp.zeros((8, 128), jnp.float32)
+
+    for part in range(2):
+        for row in range(0, 48, 8):
+            u[part, 0, pl.ds(row, 8), :] = blank
+            u[part, NZ + 1, pl.ds(row, 8), :] = blank
+
+    def prepare(sp, _):
+        for part in range(2):
+            for zz in range(2):
+                u[part, 2 * sp + zz + 1, pl.ds(0, 8), :] = blank
+                u[part, 2 * sp + zz + 1, pl.ds(40, 8), :] = blank
+        for tile in range(4):
+            inside = True
+            if tile == 0:
+                inside = z > 0
+            if tile == 3:
+                inside = z < lax.axis_size("z") - 1
+            for zz in range(2):
+                base = abs_ref[tile // 2, sp, zz, tile % 2]
+                da, db = (shift_a + 6.0) + base, (shift_b + 6.0) + base
+                ra, rb = 1.0 / (da * da + shift_im * shift_im), 1.0 / (db * db + shift_im * shift_im)
+                found = (da * ra, db * rb, -shift_im * ra)
+                for i in range(3):
+                    if tile in (1, 2):
+                        inv_ref[i, tile - 1, sp, zz] = found[i]
+                    else:
+                        edge_inv[i, tile // 3, sp, zz] = jnp.where(inside, found[i], 0.0)
+        return 0
+
+    lax.fori_loop(0, NZ // 2, prepare, 0)
+
+    for j in range(STEPS):
+        def scaled(sp, _, j=j):
+            for tile in range(4):
+                for zz in range(2):
+                    if tile in (1, 2):
+                        a, b, c = (inv_ref[i, tile - 1, sp, zz] for i in range(3))
+                        re, im = ((own_ref[tile - 1, sp, part, zz] if j == 0 else v_ref[j - 1, part, tile - 1, sp, zz]) for part in range(2))
+                    else:
+                        a, b, c = (edge_inv[i, tile // 3, sp, zz] for i in range(3))
+                        side = (left_ref, None, None, right_ref)[tile]
+                        re, im = ((side[sp, part, zz] if j == 0 else edge[part, tile // 3, sp, zz]) for part in range(2))
+                    u[0, 2 * sp + zz + 1, pl.ds(8 + 8 * tile, 8), :] = a * re - c * im
+                    u[1, 2 * sp + zz + 1, pl.ds(8 + 8 * tile, 8), :] = b * im + c * re
+            return 0
+
+        lax.fori_loop(0, NZ // 2, scaled, 0)
+
+        def spread(sp, _, j=j):
+            for tile in range(4) if j < STEPS - 1 else (1, 2):
+                for zz in range(2):
+                    for part in range(2):
+                        layer, row = 2 * sp + zz + 1, 8 + 8 * tile
+                        here = u[part, layer, pl.ds(row, 8), :]
+                        total = u[part, layer - 1, pl.ds(row, 8), :] + u[part, layer + 1, pl.ds(row, 8), :]
+                        total = total + (u[part, layer, pl.ds(row - 1, 8), :] + u[part, layer, pl.ds(row + 1, 8), :])
+                        total = total + (
+                            jnp.where(first_lane, 0.0, pltpu.roll(here, 1, 1))
+                            + jnp.where(last_lane, 0.0, pltpu.roll(here, 127, 1))
+                        )
+                        if tile in (1, 2):
+                            if j < STEPS - 1:
+                                v_ref[j, part, tile - 1, sp, zz] = total
+                            else:
+                                last[part, tile - 1, sp, zz] = total
+                        else:
+                            edge[part, tile // 3, sp, zz] = total
+            return 0
+
+        lax.fori_loop(0, NZ // 2, spread, 0)
+
+    def vector(j, part, side, sp, zz):
+        if j == 0:
+            return own_ref[side, sp, part, zz]
+        if j == STEPS:
+            return last[part, side, sp, zz]
+        return v_ref[j - 1, part, side, sp, zz]
+
+    for i in range(STEPS + 1):
+        names = [name for name in entry if name[1] == i]
+
+        def inner(sp, totals, names=names, i=i):
+            places = [(side, zz) for side in range(2) for zz in range(2)]
+            left = [[vector(i, part, side, sp, zz) for part in range(2)] for side, zz in places]
+            out = []
+            for j in range(i, STEPS + 1):
+                right = left if j == i else [[vector(j, part, side, sp, zz) for part in range(2)] for side, zz in places]
+                pairs = list(zip(left, right))
+                out.append(("re", i, j, tree_sum([a[0] * b[0] for a, b in pairs])))
+                out.append(("im", i, j, tree_sum([a[1] * b[1] for a, b in pairs])))
+                if j > i:
+                    out.append(("x", i, j, tree_sum([a[0] * b[1] - a[1] * b[0] for a, b in pairs])))
+            found = {o[:3]: o[3] for o in out}
+            return tuple(t + found[name] for t, name in zip(totals, names))
+
+        def outer(group, totals, names=names, inner=inner):
+            part_totals = tuple(blank for _ in names)
+            part_totals = lax.fori_loop(group * 4, group * 4 + 4, inner, part_totals)
+            return tuple(a + b for a, b in zip(totals, part_totals))
+
+        totals = lax.fori_loop(0, 4, outer, tuple(blank for _ in names))
+        for name, total in zip(names, totals):
+            sums[entry[name]] = total
+    for spare in range(len(entry), sums.shape[0]):
+        sums[spare] = blank
+
+    rows = jnp.sum(sums[...], axis=1)
+    column = jnp.sum(rows, axis=1, keepdims=True)
+    where = lax.broadcasted_iota(jnp.int32, rows.shape, 0) == lax.broadcasted_iota(jnp.int32, rows.shape, 1)
+    packed = jnp.sum(jnp.where(where, column, 0.0), axis=0, keepdims=True)
+    gram_ref[...] = jnp.broadcast_to(packed[None], gram_ref.shape)
+
+
+def multiplied(a, b):
+    return (a[0] * b[0] - a[1] * b[1], a[0] * b[1] + a[1] * b[0])
+
+
+def combine_kernel(at_ref, count_ref, part_ref, own_ref, v_ref, inv_ref, out_ref):
+    slot = at_ref[0]
+    ends = slot == 0
+    low = lax.broadcasted_iota(jnp.int32, (8, 128), 1) < 64
+    row = tree_sum([part_ref[i] for i in range(part_ref.shape[0])])
+
+    def spread(name):
+        return jnp.broadcast_to(row[:, entry[name] : entry[name] + 1], (8, 128))
+
+    gram = {}
+    for i, j in same:
+        re, im = spread(("re", i, j)), spread(("im", i, j))
+        real = jnp.where(ends, jnp.where(low, re, im), re + im)
+        imag = jnp.where(ends, 0.0, spread(("x", i, j))) if j > i else jnp.zeros_like(real)
+        gram[i, j] = (real, imag)
+
+    count_a = count_ref[slot]
+    count_b = count_ref[jnp.where(ends, PAIRS, L - slot)]
+    one, none = jnp.ones((8, 128), jnp.float32), jnp.zeros((8, 128), jnp.float32)
+    poly, answer = [(one, none)], [(none, none) for _ in range(STEPS)]
+    bound, doubt, scale = gram_rounding * gram[0, 0][0], none, None
+    for m in range(STEPS):
+        in_a, in_b = (jnp.where(m < count, one, none) for count in (count_a, count_b))
+        weight = jnp.where(ends, jnp.where(low, in_a, in_b), in_a + in_b)
+        g00, g01, g11 = gram[0, 0][0], gram[0, 1], gram[1, 1][0]
+        denominator = (g00 - 2.0 * g01[0] + g11) + norm_floor
+        inverse = 1.0 / denominator
+        coef = ((g00 - g01[0]) * inverse, g01[1] * inverse)
+        size = jnp.abs(coef[0]) + jnp.abs(coef[1])
+        length = jnp.sqrt(jnp.maximum(g00, 0.0))
+        if m == 0:
+            scale = size * length
+        step_doubt = bound * (2.0 + 4.0 * size) * jnp.abs(inverse) * length
+        doubt = doubt + jnp.where(weight > 0.0, step_doubt, none)
+        for j, p in enumerate(poly):
+            term = multiplied(coef, p)
+            answer[j] = (answer[j][0] + weight * term[0], answer[j][1] + weight * term[1])
+        if m == STEPS - 1:
+            break
+        rest = (1.0 - coef[0], -coef[1])
+        padded = [None] + poly + [None]
+        following = []
+        for j in range(len(poly) + 1):
+            kept = multiplied(rest, poly[j]) if j < len(poly) else (none, none)
+            moved = multiplied(coef, poly[j - 1]) if j > 0 else (none, none)
+            following.append((kept[0] + moved[0], kept[1] + moved[1]))
+        poly = following
+        rr = rest[0] * rest[0] + rest[1] * rest[1]
+        cc = coef[0] * coef[0] + coef[1] * coef[1]
+        rc = multiplied((rest[0], -rest[1]), coef)
+        cr = (rc[0], -rc[1])
+        size_rest = jnp.abs(rest[0]) + jnp.abs(rest[1])
+        bound = bound * (size + size_rest) * (size + size_rest)
+
+        def at(i, j):
+            return gram[i, j] if i <= j else (gram[j, i][0], -gram[j, i][1])
+
+        shrunk = {}
+        top = STEPS - m
+        for i in range(top):
+            for j in range(i, top):
+                a, b, d = at(i, j), at(i, j + 1), at(i + 1, j + 1)
+                if i == j:
+                    ab = multiplied(rc, b)
+                    shrunk[i, j] = (rr * a[0] + 2.0 * ab[0] + cc * d[0], none)
+                else:
+                    ab, ac = multiplied(rc, b), multiplied(cr, at(i + 1, j))
+                    shrunk[i, j] = tuple(rr * a[x] + (ab[x] + ac[x]) + cc * d[x] for x in range(2))
+        gram = shrunk
+
+    trusted = doubt <= error_allowed * scale
+    weights = []
+    for re, im in answer:
+        re = jnp.where(trusted, re, jnp.nan)
+        weights.append(
+            (
+                jnp.broadcast_to(re[:, 0:1], (8, 128)),
+                jnp.broadcast_to(re[:, 127:128], (8, 128)),
+                jnp.broadcast_to(im[:, 0:1], (8, 128)),
+            )
+        )
+
+    def finish(sp, _):
+        for side in range(2):
+            for zz in range(2):
+                res, ims = [], []
+                for j, (wa, wb, wi) in enumerate(weights):
+                    re, im = ((own_ref[side, sp, part, zz] if j == 0 else v_ref[j - 1, part, side, sp, zz]) for part in range(2))
+                    res.append(wa * re - wi * im)
+                    ims.append(wb * im + wi * re)
+                re, im = tree_sum(res), tree_sum(ims)
+                a, b, c = (inv_ref[i, side, sp, zz] for i in range(3))
+                out_ref[side, sp, 0, zz] = a * re - c * im
+                out_ref[side, sp, 1, zz] = b * im + c * re
+        return 0
+
+    lax.fori_loop(0, NZ // 2, finish, 0)
+
+
+def slot_shifts():
+    table = np.zeros((PAIRS, 4), np.float32)
+    for slot in range(PAIRS):
+        angle = 2 * math.pi * slot / L
+        table[slot, :2] = (1 - decay * math.cos(angle)) / step_size
+        table[slot, 2] = decay * math.sin(angle) / step_size
+    table[0, 1] = (1 + decay) / step_size
+    return table
+
+
+def exchanged(blocks, axes):
+    return lax.all_to_all(blocks, axes, split_axis=0, concat_axis=0, tiled=True)
+
+
+def f32(*shape):
+    return jax.ShapeDtypeStruct(shape, jnp.float32)
+
+
+VMEM = pl.BlockSpec(memory_space=pltpu.VMEM)
+SMEM = pl.BlockSpec(memory_space=pltpu.SMEM)
+
+
+def together(residual, absorption, counts):
+    z = lax.axis_index("z")
+    at = jnp.stack([lax.axis_index(SLOTS), z]).astype(jnp.int32)
+    chips = lax.axis_size("z")
+
+    tall = jnp.pad(absorption, ((0, 0), (8, 8), (0, 0)))
+    first = 16 * z + 16 * lax.axis_index("core")
+    near = lax.dynamic_slice_in_dim(tall, first, 16, axis=1).reshape(2, 2, 8, 128)
+    near = exchanged(jnp.broadcast_to(near, (32, 2, 2, 8, 128)), SLOTS).reshape(2, 16, 2, 2, 8, 128)
+
+    bands = residual.reshape(4, 2, 16, 8, 128).transpose(2, 0, 1, 3, 4)
+    series = exchanged(bands, TM).reshape(L, 2, 8, 128)
+    spectrum = pl.pallas_call(
+        forward_kernel, out_shape=f32(PAIRS, 2, 2, 8, 128), in_specs=[VMEM], out_specs=VMEM, name="forward"
+    )(series)
+    own = exchanged(spectrum, SLOTS).reshape(2, 16, 2, 2, 8, 128)
+    left = lax.ppermute(own[1], "z", [(i, i + 1) for i in range(chips - 1)])
+    right = lax.ppermute(own[0], "z", [(i + 1, i) for i in range(chips - 1)])
+    basis, inverses, partial = pl.pallas_call(
+        basis_kernel,
+        out_shape=(f32(STEPS - 1, 2, 2, 16, 2, 8, 128), f32(3, 2, 16, 2, 8, 128), f32(8, 8, 128)),
+        in_specs=[SMEM, SMEM, VMEM, VMEM, VMEM, VMEM],
+        out_specs=(VMEM, VMEM, VMEM),
+        scratch_shapes=[
+            pltpu.VMEM((2, NZ + 2, 48, 128), jnp.float32),
+            pltpu.VMEM((2, 2, 16, 2, 8, 128), jnp.float32),
+            pltpu.VMEM((3, 2, 16, 2, 8, 128), jnp.float32),
+            pltpu.VMEM((2, 2, 16, 2, 8, 128), jnp.float32),
+            pltpu.VMEM((80, 8, 128), jnp.float32),
+        ],
+        name="basis",
+    )(at, jnp.asarray(slot_shifts()), own, left, right, near)
+    partials = exchanged(partial, "z")
+    solved = pl.pallas_call(
+        combine_kernel,
+        out_shape=f32(2, 16, 2, 2, 8, 128),
+        in_specs=[SMEM, SMEM, VMEM, VMEM, VMEM, VMEM],
+        out_specs=VMEM,
+        name="combine",
+    )(at, counts, partials, own, basis, inverses)
+    gathered = exchanged(solved.reshape(32, 2, 2, 8, 128), SLOTS)
+    values = pl.pallas_call(
+        inverse_kernel, out_shape=f32(L, 2, 8, 128), in_specs=[VMEM], out_specs=VMEM, name="inverse"
+    )(gathered)
+    return exchanged(values.reshape(16, 4, 2, 8, 128), TM)
+
+
+def body(residual, absorption, counts):
+    bands = together(residual, absorption, counts)
+    failed = jnp.isnan(bands[0, 0, 0, 0, 0])
+    return lax.cond(
+        failed,
+        lambda r, a, c, b: stepwise(r, a, c),
+        lambda r, a, c, b: b.transpose(1, 2, 0, 3, 4).reshape(r.shape),
+        residual, absorption, counts, bands,
+    )
 
 
 def solution(mesh):
-    in_specs = (P("tm", "space", None, None), P("space", None, None), P())
-    out_specs = P("tm", "space", None, None)
-    return jax.shard_map(body, mesh=mesh, in_specs=in_specs, out_specs=out_specs, check_vma=False)
+    chips, cores = mesh.shape["tm"] // 2, 2
+    devices = mesh.devices.reshape(chips, cores, 4, 4)
+    inner = Mesh(devices, ("z", "core", "y", "x"))
+    in_specs = (P(TM, SPACE, None, None), P(SPACE, None, None), P())
+    out_specs = P(TM, SPACE, None, None)
+    return jax.shard_map(body, mesh=inner, in_specs=in_specs, out_specs=out_specs, check_vma=False)

time: 343 us -> 147 us (0.43)
  waiting for transfers between devices: 153 us -> 36.2 us
  starting transfers between devices: 89.2 us -> 19 us
  other arithmetic: 32 us -> 0.65 us
  Pallas kernels: 0 us -> 25.1 us
  blocking collectives: 47.4 us -> 59.2 us
  local copies, waits for them, and re-layouts: 11.6 us -> 4.42 us
  loops' own time: 5.21 us -> 0.01 us
    ppermute x12 -> x2, waiting for transfers between devices: 60.7 us -> 0.01 us  [the longest x1 0.01 us: together(): left = lax.ppermute(own[1], 'z', [(i, i + 1) for i in range(chips - 1)])]
    all_to_all x8 -> x3, waiting for transfers between devices: 92.4 us -> 36.2 us  [exchanged(): return lax.all_to_all(blocks, axes, split_axis=0, concat_axis=0, tiled=True)]
    all_to_all x8 -> x3, starting transfers between devices: 67.9 us -> 16.4 us  [exchanged(): return lax.all_to_all(blocks, axes, split_axis=0, concat_axis=0, tiled=True)]
    pallas_call x0 -> x4, Pallas kernels: none -> 25.1 us  [the longest x1 17.1 us: together(): pl.pallas_call(basis_kernel, out_shape=(f32(STEPS - 1, 2, 2, 16, 2, 8, 12...]
    ppermute x12 -> x2, starting transfers between devices: 21.3 us -> 2.6 us  [the longest x1 1.31 us: together(): left = lax.ppermute(own[1], 'z', [(i, i + 1) for i in range(chips - 1)])]
    sub x12 -> x0, other arithmetic: 18.3 us -> none  [the longest x6 16.6 us: advance(): res_im = res_im - (coef_re * img_im + coef_im * img_re)]
    all_to_all x2 -> x3, blocking collectives: 47.4 us -> 59.2 us  [exchanged(): return lax.all_to_all(blocks, axes, split_axis=0, concat_axis=0, tiled=True)]
    another operation x1, loops' own time: 5.21 us -> 0.01 us  [body(): lax.cond(failed, lambda r, a, c, b: stepwise(r, a, c), lambda r, a, c, b:...]
  transfers between devices with their start and end apart: 20 -> 5, of which waited for: 20 -> 3; matrix products, arithmetic and copies ran while one was open for 1% -> 0% of each run, Pallas kernels for 0% -> 0%
where the time goes in v1:
time: 147 us; the launch traced here: 146 us
  blocking collectives  59.2 us (40%)
  waiting for transfers between devices  36.2 us (25%)
  Pallas kernels  25.1 us (17%)
  starting transfers between devices  19 us (13%)
  local copies, waits for them, and re-layouts  4.42 us (3%)
    all_to_all x3, blocking collectives, exchanged(): return lax.all_to_all(blocks, axes, split_axis=0, concat_axis=0, tiled=True)  59.2 us
    all_to_all x3, waiting for transfers between devices, exchanged(): return lax.all_to_all(blocks, axes, split_axis=0, concat_axis=0, tiled=True)  36.2 us
    pallas_call x1, Pallas kernels, together(): pl.pallas_call(basis_kernel, out_shape=(f32(STEPS - 1, 2, 2, 16, 2, 8, 12...  17.1 us
    all_to_all x3, starting transfers between devices, exchanged(): return lax.all_to_all(blocks, axes, split_axis=0, concat_axis=0, tiled=True)  16.4 us
    pallas_call x1, Pallas kernels, together(): pl.pallas_call(combine_kernel, out_shape=f32(2, 16, 2, 2, 8, 128), in_spe...  3.84 us
  transfers between devices with their start and end apart: 5, of which 3 were waited for; matrix products, arithmetic and copies ran while one was open for 0% of the time, Pallas kernels for 0%

profile of v1, /device:TPU:1, one launch (start us, length us, event | category | flops | bytes accessed | tf_op | source)
XLA Modules:
  0.0 146.0 jit_solution(1895680588935874194)
XLA Ops:
  0.0 0.0 copy-start.1
  0.0 1.1 copy_bitcast_fusion.5
  1.1 27.1 %all_to_all.103 = f32[16,4,2,8,128]{4,3,2,1,0:T(8,128)} all-to-all(f32[16,4,2,8,128]{4,3,2,1,0:T(8,128)S(1)} %copy_bitcast_fusion.5), channel_id=1, replica_groups=mesh['z'=8,'core'=2,'y'=4,'x'=4] {'z','core'}, dimensions={0} | all-to-all | bytes 1048576 | tf_op jit(solution)/shard_map/all_to_all | solution.py:470
  28.2 2.1 %forward.1 = f32[32,2,2,8,128]{4,3,2,1,0:T(8,128)} custom-call(f32[64,2,8,128]{3,2,1,0:T(8,128)} %bitcast.112), custom_call_target="tpu_custom_call" | custom-call | tf_op jit(solution)/shard_map/forward/pallas_call | solution.py:493
  30.3 7.3 %all-to-all-start.6 = ((f32[32,2,2,8,128]{4,3,2,1,0:T(8,128)}), f32[32,2,2,8,128]{4,3,2,1,0:T(8,128)S(1)}, u32[]{:S(2)}, u32[]{:S(2)}) async-start(f32[32,2,2,8,128]{4,3,2,1,0:T(8,128)} %forward.1), calls=%async_computation.6 | async-start | bytes 1048576 | tf_op jit(solution)/shard_map/all_to_all | solution.py:470
  37.6 0.0 copy-done.1
  37.7 11.1 %all-to-all-done.6 = f32[32,2,2,8,128]{4,3,2,1,0:T(8,128)S(1)} async-done(((f32[32,2,2,8,128]{4,3,2,1,0:T(8,128)}), f32[32,2,2,8,128]{4,3,2,1,0:T(8,128)S(1)}, u32[]{:S(2)}, u32[]{:S(2)}) %all-to-all-start.6) | async-done | bytes 524320 | tf_op jit(solution)/shard_map/all_to_all | solution.py:470
  48.8 0.9 broadcast_in_dim.30
  49.7 4.7 %all-to-all-start.7 = ((f32[32,2,2,8,128]{4,3,2,1,0:T(8,128)}), f32[32,2,2,8,128]{4,3,2,1,0:T(8,128)S(1)}, u32[]{:S(2)}, u32[]{:S(2)}) async-start(f32[32,2,2,8,128]{4,3,2,1,0:T(8,128)} %broadcast_in_dim.30), calls=%async_computation.7 | async-start | bytes 1048576 | tf_op jit(solution)/shard_map/all_to_all | solution.py:470
  54.5 1.3 collective-permute-start.2
  55.8 1.3 collective-permute-start.3
  57.1 0.7 pad_add_fusion.at_ref
  57.7 7.8 %all-to-all-done.7 = f32[32,2,2,8,128]{4,3,2,1,0:T(8,128)S(1)} async-done(((f32[32,2,2,8,128]{4,3,2,1,0:T(8,128)}), f32[32,2,2,8,128]{4,3,2,1,0:T(8,128)S(1)}, u32[]{:S(2)}, u32[]{:S(2)}) %all-to-all-start.7) | async-done | bytes 524320 | tf_op jit(solution)/shard_map/all_to_all | solution.py:470
  65.5 0.0 collective-permute-done.2.left_ref
  65.5 0.0 collective-permute-done.3.right_ref
  65.5 0.0 copy-start.6
  65.6 0.0 copy-done.2
  65.6 0.8 copy-done.4
  66.3 0.1 copy-done.5
  66.4 0.1 copy-done.6
  66.5 17.1 %basis.1 = (f32[5,2,2,16,2,8,128]{6,5,4,3,2,1,0:T(8,128)}, f32[3,2,16,2,8,128]{5,4,3,2,1,0:T(8,128)}, f32[8,8,128]{2,1,0:T(8,128)}) custom-call(s32[2]{0:T(128)} %pad_add_fusion.at_ref, f32[32,4]{1,0:T(8,128)} %constant.105.clone.shift_ref, f32[2,16,2,2,8,128]{5,4,3,2,1,0:T(8,128)} %bitcast.100, f32[16,2,2,8,128]{4,3,2,1,0:T(8,128)} %copy-done.5, ...), custom_call_target="tpu_custom_call" | custom-call | tf_op jit(solution)/shard_map/basis/pallas_call | solution.py:499
  83.6 10.9 %all_to_all.104.part_ref = f32[8,8,128]{2,1,0:T(8,128)} all-to-all(f32[8,8,128]{2,1,0:T(8,128)} %get-tuple-element.162), channel_id=1, replica_groups=mesh['z'=8,'core'=2,'y'=4,'x'=4] {'z'}, dimensions={0} | all-to-all | bytes 65536 | tf_op jit(solution)/shard_map/all_to_all | solution.py:470
  94.5 0.0 copy-done
  94.5 3.8 %combine.1 = f32[2,16,2,2,8,128]{5,4,3,2,1,0:T(8,128)} custom-call(s32[2]{0:T(128)} %pad_add_fusion.at_ref, s32[64]{0:T(128)S(1)} %copy-done, f32[8,8,128]{2,1,0:T(8,128)} %all_to_all.104.part_ref, f32[2,16,2,2,8,128]{5,4,3,2,1,0:T(8,128)} %bitcast.101, f32[5,2,2,16,2,8,128]{6,5,4,3,2,1,0:T(8,128)} %get-tuple-element.163.v_ref, ...), custom_call_target="tpu_custom_call" | custom-call | tf_op jit(solution)/shard_map/combine/pallas_call | solution.py:514
  98.3 21.2 %all_to_all.105.s_ref = f32[32,2,2,8,128]{4,3,2,1,0:T(8,128)} all-to-all(f32[32,2,2,8,128]{4,3,2,1,0:T(8,128)} %bitcast.109), channel_id=1, replica_groups=mesh['z'=8,'core'=2,'y'=4,'x'=4] {'core','y','x'}, dimensions={0} | all-to-all | bytes 1048576 | tf_op jit(solution)/shard_map/all_to_all | solution.py:470
  119.6 2.1 %inverse.1 = f32[64,2,8,128]{3,2,1,0:T(8,128)} custom-call(f32[32,2,2,8,128]{4,3,2,1,0:T(8,128)} %all_to_all.105.s_ref), custom_call_target="tpu_custom_call" | custom-call | tf_op jit(solution)/shard_map/inverse/pallas_call | solution.py:522
  121.7 4.4 %all-to-all-start.10 = ((f32[16,4,2,8,128]{4,3,2,1,0:T(8,128)}), f32[16,4,2,8,128]{4,3,2,1,0:T(8,128)S(1)}, u32[]{:S(2)}, u32[]{:S(2)}) async-start(f32[16,4,2,8,128]{4,3,2,1,0:T(8,128)} %bitcast.111), calls=%async_computation.10 | async-start | bytes 1048576 | tf_op jit(solution)/shard_map/all_to_all | solution.py:470
  126.1 17.3 %all-to-all-done.10 = f32[16,4,2,8,128]{4,3,2,1,0:T(8,128)S(1)} async-done(((f32[16,4,2,8,128]{4,3,2,1,0:T(8,128)}), f32[16,4,2,8,128]{4,3,2,1,0:T(8,128)S(1)}, u32[]{:S(2)}, u32[]{:S(2)}) %all-to-all-start.10) | async-done | bytes 524320 | tf_op jit(solution)/shard_map/all_to_all | solution.py:470
  143.4 0.5 slice.146
  145.2 0.0 copy-done.3
  145.2 0.8 conditional.1
  145.2 0.8 copy_bitcast_fusion
  (7 shorter events, 0.1 us)
Async XLA Ops:
  0.0 37.6 %copy-start.1 = (f32[2,128,128]{2,1,0:T(8,128)S(1)}, f32[2,128,128]{2,1,0:T(8,128)}, u32[]{:S(2)}) copy-start(f32[2,128,128]{2,1,0:T(8,128)} %param.9) | copy-start | bytes 393220
  30.3 64.2 %copy-start = (s32[64]{0:T(128)S(1)}, s32[64]{0:T(128)}, u32[]{:S(2)}) copy-start(s32[64]{0:T(128)} %count_ref.1) | copy-start | bytes 772
  30.3 18.5 %all-to-all-start.6 = ((f32[32,2,2,8,128]{4,3,2,1,0:T(8,128)}), f32[32,2,2,8,128]{4,3,2,1,0:T(8,128)S(1)}, u32[]{:S(2)}, u32[]{:S(2)}) async-start(f32[32,2,2,8,128]{4,3,2,1,0:T(8,128)} %forward.1), calls=%async_computation.6 | async-start | bytes 1048576 | tf_op jit(solution)/shard_map/all_to_all | solution.py:470
  48.8 16.8 %copy-start.2 = (f32[32,2,2,8,128]{4,3,2,1,0:T(8,128)}, f32[32,2,2,8,128]{4,3,2,1,0:T(8,128)S(1)}, u32[]{:S(2)}) copy-start(f32[32,2,2,8,128]{4,3,2,1,0:T(8,128)S(1)} %all-to-all-done.6) | copy-start | bytes 1572868
  49.7 15.8 %all-to-all-start.7 = ((f32[32,2,2,8,128]{4,3,2,1,0:T(8,128)}), f32[32,2,2,8,128]{4,3,2,1,0:T(8,128)S(1)}, u32[]{:S(2)}, u32[]{:S(2)}) async-start(f32[32,2,2,8,128]{4,3,2,1,0:T(8,128)} %broadcast_in_dim.30), calls=%async_computation.7 | async-start | bytes 1048576 | tf_op jit(solution)/shard_map/all_to_all | solution.py:470
  54.5 11.1 %collective-permute-start.2 = (f32[16,2,2,8,128]{4,3,2,1,0:T(8,128)S(1)}, f32[16,2,2,8,128]{4,3,2,1,0:T(8,128)S(1)}, u32[]{:S(2)}, u32[]{:S(2)}) collective-permute-start(f32[16,2,2,8,128]{4,3,2,1,0:T(8,128)S(1)} %get-tuple-element.311), channel_id=1, source_target_pairs={{0,32},{32,64},{64,96},{96,128},{128,160},{160,192},{192,224},{1,3... | collective-permute-start | bytes 786440 | tf_op jit(solution)/shard_map/ppermute | solution.py:497
  55.8 9.8 %collective-permute-start.3 = (f32[16,2,2,8,128]{4,3,2,1,0:T(8,128)S(1)}, f32[16,2,2,8,128]{4,3,2,1,0:T(8,128)S(1)}, u32[]{:S(2)}, u32[]{:S(2)}) collective-permute-start(f32[16,2,2,8,128]{4,3,2,1,0:T(8,128)S(1)} %get-tuple-element.310), channel_id=1, source_target_pairs={{32,0},{64,32},{96,64},{128,96},{160,128},{192,160},{224,192},{33,... | collective-permute-start | bytes 786440 | tf_op jit(solution)/shard_map/ppermute | solution.py:498
  65.5 0.8 copy-start.4
  65.5 0.9 copy-start.5
  65.5 1.0 copy-start.6
  98.3 46.9 %copy-start.3 = (f32[4,2,128,128]{3,2,1,0:T(8,128)S(1)}, f32[4,2,128,128]{3,2,1,0:T(8,128)}, u32[]{:S(2)}) copy-start(f32[4,2,128,128]{3,2,1,0:T(8,128)} %param.8) | copy-start | bytes 1572868
  121.7 21.7 %all-to-all-start.10 = ((f32[16,4,2,8,128]{4,3,2,1,0:T(8,128)}), f32[16,4,2,8,128]{4,3,2,1,0:T(8,128)S(1)}, u32[]{:S(2)}, u32[]{:S(2)}) async-start(f32[16,4,2,8,128]{4,3,2,1,0:T(8,128)} %bitcast.111), calls=%async_computation.10 | async-start | bytes 1048576 | tf_op jit(solution)/shard_map/all_to_all | solution.py:470

commit v2 on v1

--- a/solution.py
+++ b/solution.py
@@ -200,7 +200,8 @@
     return [halves[i % 2][i // 2] for i in range(n)]
 
 
-def forward_kernel(x_ref, out_ref):
+def forward_kernel(x_ref, after_ref, out_ref):
+    del after_ref
     for zz in range(2):
         spectrum = real_transform([x_ref[n, zz] * decay**n for n in range(L)])
         out_ref[0, 0, zz] = spectrum[0][0]
@@ -210,7 +211,8 @@
             out_ref[k, 1, zz] = spectrum[k][1]
 
 
-def inverse_kernel(s_ref, out_ref):
+def inverse_kernel(s_ref, out_ref, failed_ref):
+    failed = jnp.zeros((8, 128), jnp.float32)
     for zz in range(2):
         ends = [s_ref[0, part, zz] for part in range(2)]
         spectrum = [(ends[0] + ends[0], None)]
@@ -219,6 +221,8 @@
         values = real_inverse(spectrum)
         for n in range(L):
             out_ref[n, zz] = values[n] * (decay ** (-n) / (2 * L))
+        failed = jnp.where(values[0] != values[0], 1.0, failed)
+    failed_ref[0] = jnp.where(jnp.max(failed) > 0.0, 1, 0)
 
 
 same = [(i, j) for i in range(STEPS + 1) for j in range(i, STEPS + 1)]
@@ -234,8 +238,8 @@
     return terms[0]
 
 
-def basis_kernel(at_ref, shift_ref, own_ref, left_ref, right_ref, abs_ref, v_ref, inv_ref, gram_ref, u, edge, edge_inv, last, sums):
-    slot, z = at_ref[0], at_ref[1]
+def basis_kernel(shift_ref, own_ref, left_ref, right_ref, abs_ref, v_ref, inv_ref, gram_ref, u, edge, edge_inv, last, sums):
+    slot, z = lax.axis_index(SLOTS), lax.axis_index("z")
     shift_a, shift_b, shift_im = (shift_ref[slot, i] for i in range(3))
     lanes = lax.broadcasted_iota(jnp.int32, (8, 128), 1)
     first_lane, last_lane = lanes == 0, lanes == 127
@@ -269,7 +273,7 @@
                         edge_inv[i, tile // 3, sp, zz] = jnp.where(inside, found[i], 0.0)
         return 0
 
-    lax.fori_loop(0, NZ // 2, prepare, 0)
+    lax.fori_loop(0, NZ // 2, prepare, 0, unroll=4)
 
     for j in range(STEPS):
         def scaled(sp, _, j=j):
@@ -286,7 +290,7 @@
                     u[1, 2 * sp + zz + 1, pl.ds(8 + 8 * tile, 8), :] = b * im + c * re
             return 0
 
-        lax.fori_loop(0, NZ // 2, scaled, 0)
+        lax.fori_loop(0, NZ // 2, scaled, 0, unroll=4)
 
         def spread(sp, _, j=j):
             for tile in range(4) if j < STEPS - 1 else (1, 2):
@@ -309,7 +313,7 @@
                             edge[part, tile // 3, sp, zz] = total
             return 0
 
-        lax.fori_loop(0, NZ // 2, spread, 0)
+        lax.fori_loop(0, NZ // 2, spread, 0, unroll=8)
 
     def vector(j, part, side, sp, zz):
         if j == 0:
@@ -357,8 +361,8 @@
     return (a[0] * b[0] - a[1] * b[1], a[0] * b[1] + a[1] * b[0])
 
 
-def combine_kernel(at_ref, count_ref, part_ref, own_ref, v_ref, inv_ref, out_ref):
-    slot = at_ref[0]
+def combine_kernel(count_ref, part_ref, own_ref, v_ref, inv_ref, out_ref):
+    slot = lax.axis_index(SLOTS)
     ends = slot == 0
     low = lax.broadcasted_iota(jnp.int32, (8, 128), 1) < 64
     row = tree_sum([part_ref[i] for i in range(part_ref.shape[0])])
@@ -453,7 +457,7 @@
                 out_ref[side, sp, 1, zz] = b * im + c * re
         return 0
 
-    lax.fori_loop(0, NZ // 2, finish, 0)
+    lax.fori_loop(0, NZ // 2, finish, 0, unroll=2)
 
 
 def slot_shifts():
@@ -470,36 +474,47 @@
     return lax.all_to_all(blocks, axes, split_axis=0, concat_axis=0, tiled=True)
 
 
-def f32(*shape):
-    return jax.ShapeDtypeStruct(shape, jnp.float32)
-
-
 VMEM = pl.BlockSpec(memory_space=pltpu.VMEM)
 SMEM = pl.BlockSpec(memory_space=pltpu.SMEM)
 
 
+def f32(*shape):
+    return pltpu.VMEM(shape, jnp.float32)
+
+
+def held(x):
+    return pltpu.with_memory_space_constraint(x, pltpu.MemorySpace.VMEM)
+
+
+def room(mebibytes):
+    return pltpu.CompilerParams(vmem_limit_bytes=mebibytes * 2**20)
+
+
 def together(residual, absorption, counts):
-    z = lax.axis_index("z")
-    at = jnp.stack([lax.axis_index(SLOTS), z]).astype(jnp.int32)
-    chips = lax.axis_size("z")
+    z, chips = lax.axis_index("z"), lax.axis_size("z")
 
     tall = jnp.pad(absorption, ((0, 0), (8, 8), (0, 0)))
     first = 16 * z + 16 * lax.axis_index("core")
     near = lax.dynamic_slice_in_dim(tall, first, 16, axis=1).reshape(2, 2, 8, 128)
-    near = exchanged(jnp.broadcast_to(near, (32, 2, 2, 8, 128)), SLOTS).reshape(2, 16, 2, 2, 8, 128)
+    near = exchanged(jnp.broadcast_to(near, (32, 2, 2, 8, 128)), SLOTS)
 
     bands = residual.reshape(4, 2, 16, 8, 128).transpose(2, 0, 1, 3, 4)
     series = exchanged(bands, TM).reshape(L, 2, 8, 128)
     spectrum = pl.pallas_call(
-        forward_kernel, out_shape=f32(PAIRS, 2, 2, 8, 128), in_specs=[VMEM], out_specs=VMEM, name="forward"
-    )(series)
+        forward_kernel,
+        out_shape=f32(PAIRS, 2, 2, 8, 128),
+        in_specs=[VMEM, VMEM],
+        out_specs=VMEM,
+        compiler_params=room(4),
+        name="forward",
+    )(held(series), held(near))
     own = exchanged(spectrum, SLOTS).reshape(2, 16, 2, 2, 8, 128)
     left = lax.ppermute(own[1], "z", [(i, i + 1) for i in range(chips - 1)])
     right = lax.ppermute(own[0], "z", [(i + 1, i) for i in range(chips - 1)])
     basis, inverses, partial = pl.pallas_call(
         basis_kernel,
         out_shape=(f32(STEPS - 1, 2, 2, 16, 2, 8, 128), f32(3, 2, 16, 2, 8, 128), f32(8, 8, 128)),
-        in_specs=[SMEM, SMEM, VMEM, VMEM, VMEM, VMEM],
+        in_specs=[SMEM, VMEM, VMEM, VMEM, VMEM],
         out_specs=(VMEM, VMEM, VMEM),
         scratch_shapes=[
             pltpu.VMEM((2, NZ + 2, 48, 128), jnp.float32),
@@ -508,28 +523,34 @@
             pltpu.VMEM((2, 2, 16, 2, 8, 128), jnp.float32),
             pltpu.VMEM((80, 8, 128), jnp.float32),
         ],
+        compiler_params=room(10),
         name="basis",
-    )(at, jnp.asarray(slot_shifts()), own, left, right, near)
+    )(jnp.asarray(slot_shifts()), held(own), held(left), held(right), held(near.reshape(2, 16, 2, 2, 8, 128)))
     partials = exchanged(partial, "z")
     solved = pl.pallas_call(
         combine_kernel,
         out_shape=f32(2, 16, 2, 2, 8, 128),
-        in_specs=[SMEM, SMEM, VMEM, VMEM, VMEM, VMEM],
+        in_specs=[SMEM, VMEM, VMEM, VMEM, VMEM],
         out_specs=VMEM,
+        compiler_params=room(6),
         name="combine",
-    )(at, counts, partials, own, basis, inverses)
+    )(counts, held(partials), held(own), held(basis), held(inverses))
     gathered = exchanged(solved.reshape(32, 2, 2, 8, 128), SLOTS)
-    values = pl.pallas_call(
-        inverse_kernel, out_shape=f32(L, 2, 8, 128), in_specs=[VMEM], out_specs=VMEM, name="inverse"
-    )(gathered)
-    return exchanged(values.reshape(16, 4, 2, 8, 128), TM)
+    values, failed = pl.pallas_call(
+        inverse_kernel,
+        out_shape=(f32(L, 2, 8, 128), jax.ShapeDtypeStruct((1,), jnp.int32)),
+        in_specs=[VMEM],
+        out_specs=(VMEM, SMEM),
+        compiler_params=room(4),
+        name="inverse",
+    )(held(gathered))
+    return exchanged(values.reshape(16, 4, 2, 8, 128), TM), failed
 
 
 def body(residual, absorption, counts):
-    bands = together(residual, absorption, counts)
-    failed = jnp.isnan(bands[0, 0, 0, 0, 0])
+    bands, failed = together(residual, absorption, counts)
     return lax.cond(
-        failed,
+        failed[0] > 0,
         lambda r, a, c, b: stepwise(r, a, c),
         lambda r, a, c, b: b.transpose(1, 2, 0, 3, 4).reshape(r.shape),
         residual, absorption, counts, bands,

time: 147 us -> 136 us (0.925)
  Pallas kernels: 25.1 us -> 11.4 us
  blocking collectives: 59.2 us -> 70.1 us
  starting transfers between devices: 19 us -> 15.6 us
  waiting for transfers between devices: 36.2 us -> 34.2 us
    all_to_all x3 -> x4, blocking collectives: 59.2 us -> 70.1 us  [exchanged(): return lax.all_to_all(blocks, axes, split_axis=0, concat_axis=0, tiled=True)]
    all_to_all x3 -> x2, waiting for transfers between devices: 36.2 us -> 26.8 us  [exchanged(): return lax.all_to_all(blocks, axes, split_axis=0, concat_axis=0, tiled=True)]
    pallas_call x1, Pallas kernels: 17.1 us -> 8.7 us  [together(): pl.pallas_call(basis_kernel, out_shape=(f32(STEPS - 1, 2, 2, 16, 2, 8, 12...]
    ppermute x1, waiting for transfers between devices: 0.01 us -> 3.85 us  [together(): right = lax.ppermute(own[0], 'z', [(i + 1, i) for i in range(chips - 1)])]
    ppermute x1, waiting for transfers between devices: 0.01 us -> 3.56 us  [together(): left = lax.ppermute(own[1], 'z', [(i, i + 1) for i in range(chips - 1)])]
    all_to_all x3 -> x2, starting transfers between devices: 16.4 us -> 13 us  [exchanged(): return lax.all_to_all(blocks, axes, split_axis=0, concat_axis=0, tiled=True)]
    pallas_call x1, Pallas kernels: 3.84 us -> 1.41 us  [together(): pl.pallas_call(combine_kernel, out_shape=f32(2, 16, 2, 2, 8, 128), in_spe...]
    pallas_call x1, Pallas kernels: 2.06 us -> 0.23 us  [together(): pl.pallas_call(forward_kernel, out_shape=f32(PAIRS, 2, 2, 8, 128), in_spe...]
  transfers between devices with their start and end apart: 5 -> 4, of which waited for: 3 -> 4; matrix products, arithmetic and copies ran while one was open for 0% -> 1% of each run, Pallas kernels for 0% -> 0%
where the time goes in v2:
time: 136 us; the launch traced here: 135 us
  blocking collectives  70.1 us (52%)
  waiting for transfers between devices  34.2 us (25%)
  starting transfers between devices  15.6 us (11%)
  Pallas kernels  11.4 us (8%)
  local copies, waits for them, and re-layouts  3.55 us (3%)
    all_to_all x4, blocking collectives, exchanged(): return lax.all_to_all(blocks, axes, split_axis=0, concat_axis=0, tiled=True)  70.1 us
    all_to_all x2, waiting for transfers between devices, exchanged(): return lax.all_to_all(blocks, axes, split_axis=0, concat_axis=0, tiled=True)  26.8 us
    all_to_all x2, starting transfers between devices, exchanged(): return lax.all_to_all(blocks, axes, split_axis=0, concat_axis=0, tiled=True)  13 us
    pallas_call x1, Pallas kernels, together(): pl.pallas_call(basis_kernel, out_shape=(f32(STEPS - 1, 2, 2, 16, 2, 8, 12...  8.7 us
    ppermute x1, waiting for transfers between devices, together(): right = lax.ppermute(own[0], 'z', [(i + 1, i) for i in range(chips - 1)])  3.85 us
    ppermute x1, waiting for transfers between devices, together(): left = lax.ppermute(own[1], 'z', [(i, i + 1) for i in range(chips - 1)])  3.56 us
  transfers between devices with their start and end apart: 4, of which 4 were waited for; matrix products, arithmetic and copies ran while one was open for 1% of the time, Pallas kernels for 0%

profile of v2, /device:TPU:1, one launch (start us, length us, event | category | flops | bytes accessed | tf_op | source)
XLA Modules:
  0.0 135.5 jit_solution(4630546034941222339)
XLA Ops:
  0.0 0.7 fusion.54
  0.7 0.9 broadcast_in_dim.30
  1.6 8.6 %all-to-all-start.6 = ((f32[32,2,2,8,128]{4,3,2,1,0:T(8,128)}), f32[32,2,2,8,128]{4,3,2,1,0:T(8,128)S(1)}, u32[]{:S(2)}, u32[]{:S(2)}) async-start(f32[32,2,2,8,128]{4,3,2,1,0:T(8,128)} %broadcast_in_dim.30), calls=%async_computation.6 | async-start | bytes 1048576 | tf_op jit(solution)/shard_map/all_to_all | solution.py:474
  10.2 1.1 copy_bitcast_fusion.5
  11.2 0.0 copy-start
  11.3 10.0 %all-to-all-done.6.after_ref = f32[32,2,2,8,128]{4,3,2,1,0:T(8,128)S(1)} async-done(((f32[32,2,2,8,128]{4,3,2,1,0:T(8,128)}), f32[32,2,2,8,128]{4,3,2,1,0:T(8,128)S(1)}, u32[]{:S(2)}, u32[]{:S(2)}) %all-to-all-start.6) | async-done | bytes 524320 | tf_op jit(solution)/shard_map/all_to_all | solution.py:474
  21.3 26.5 %all_to_all.103 = f32[16,4,2,8,128]{4,3,2,1,0:T(8,128)S(1)} all-to-all(f32[16,4,2,8,128]{4,3,2,1,0:T(8,128)S(1)} %copy_bitcast_fusion.5), channel_id=1, replica_groups=mesh['z'=8,'core'=2,'y'=4,'x'=4] {'z','core'}, dimensions={0} | all-to-all | bytes 1048576 | tf_op jit(solution)/shard_map/all_to_all | solution.py:474
  47.8 0.0 copy-start.1
  47.8 0.2 forward.1
  48.1 14.1 %all_to_all.104 = f32[32,2,2,8,128]{4,3,2,1,0:T(8,128)S(1)} all-to-all(f32[32,2,2,8,128]{4,3,2,1,0:T(8,128)S(1)} %forward.1), channel_id=1, replica_groups=mesh['z'=8,'core'=2,'y'=4,'x'=4] {'core','y','x'}, dimensions={0} | all-to-all | bytes 1048576 | tf_op jit(solution)/shard_map/all_to_all | solution.py:474
  62.2 1.3 collective-permute-start.2
  63.6 1.3 collective-permute-start.3
  64.9 3.6 %collective-permute-done.2.left_ref = f32[16,2,2,8,128]{4,3,2,1,0:T(8,128)S(1)} collective-permute-done((f32[16,2,2,8,128]{4,3,2,1,0:T(8,128)S(1)}, f32[16,2,2,8,128]{4,3,2,1,0:T(8,128)S(1)}, u32[]{:S(2)}, u32[]{:S(2)}) %collective-permute-start.2) | collective-permute-done | bytes 262176 | tf_op jit(solution)/shard_map/ppermute | solution.py:512
  68.4 3.8 %collective-permute-done.3.right_ref = f32[16,2,2,8,128]{4,3,2,1,0:T(8,128)S(1)} collective-permute-done((f32[16,2,2,8,128]{4,3,2,1,0:T(8,128)S(1)}, f32[16,2,2,8,128]{4,3,2,1,0:T(8,128)S(1)}, u32[]{:S(2)}, u32[]{:S(2)}) %collective-permute-start.3) | collective-permute-done | bytes 262176 | tf_op jit(solution)/shard_map/ppermute | solution.py:513
  72.3 0.0 copy-done
  72.3 8.7 %basis.1 = (f32[5,2,2,16,2,8,128]{6,5,4,3,2,1,0:T(8,128)S(1)}, f32[3,2,16,2,8,128]{5,4,3,2,1,0:T(8,128)S(1)}, f32[8,8,128]{2,1,0:T(8,128)S(1)}) custom-call(f32[32,4]{1,0:T(8,128)S(1)} %copy-done, f32[2,16,2,2,8,128]{5,4,3,2,1,0:T(8,128)S(1)} %bitcast.92, f32[16,2,2,8,128]{4,3,2,1,0:T(8,128)S(1)} %collective-permute-done.2.left_ref, ...), custom_call_target="tpu_custom_call" | custom-call | tf_op jit(solution)/shard_map/basis/pallas_call | solution.py:514
  81.0 11.1 %all_to_all.105.part_ref = f32[8,8,128]{2,1,0:T(8,128)S(1)} all-to-all(f32[8,8,128]{2,1,0:T(8,128)S(1)} %get-tuple-element.164), channel_id=1, replica_groups=mesh['z'=8,'core'=2,'y'=4,'x'=4] {'z'}, dimensions={0} | all-to-all | bytes 65536 | tf_op jit(solution)/shard_map/all_to_all | solution.py:474
  92.1 0.0 copy-done.1
  92.1 0.0 copy-start.2
  92.1 0.0 copy-start.3
  92.1 1.4 %combine.1 = f32[2,16,2,2,8,128]{5,4,3,2,1,0:T(8,128)S(1)} custom-call(s32[64]{0:T(128)S(1)} %copy-done.1, f32[8,8,128]{2,1,0:T(8,128)S(1)} %all_to_all.105.part_ref, f32[2,16,2,2,8,128]{5,4,3,2,1,0:T(8,128)S(1)} %bitcast.93, f32[5,2,2,16,2,8,128]{6,5,4,3,2,1,0:T(8,128)S(1)} %get-tuple-element.165.v_ref, f32[3,2,16,2,8,128]{5,4,3,2,1,0:T(8,128)S(1)} %get-tuple-element.166.inv_ref), custom_call_target="tpu_custom_call" | custom-call | tf_op jit(solution)/shard_map/combine/pallas_call | solution.py:530
  93.5 18.3 %all_to_all.106.s_ref = f32[32,2,2,8,128]{4,3,2,1,0:T(8,128)S(1)} all-to-all(f32[32,2,2,8,128]{4,3,2,1,0:T(8,128)S(1)} %bitcast.95), channel_id=1, replica_groups=mesh['z'=8,'core'=2,'y'=4,'x'=4] {'core','y','x'}, dimensions={0} | all-to-all | bytes 1048576 | tf_op jit(solution)/shard_map/all_to_all | solution.py:474
  111.9 1.0 inverse.1
  112.9 4.4 %all-to-all-start.10 = ((f32[16,4,2,8,128]{4,3,2,1,0:T(8,128)}), f32[16,4,2,8,128]{4,3,2,1,0:T(8,128)S(1)}, u32[]{:S(2)}, u32[]{:S(2)}) async-start(f32[16,4,2,8,128]{4,3,2,1,0:T(8,128)} %bitcast.39), calls=%async_computation.10 | async-start | bytes 1048576 | tf_op jit(solution)/shard_map/all_to_all | solution.py:474
  117.9 16.8 %all-to-all-done.10 = f32[16,4,2,8,128]{4,3,2,1,0:T(8,128)S(1)} async-done(((f32[16,4,2,8,128]{4,3,2,1,0:T(8,128)}), f32[16,4,2,8,128]{4,3,2,1,0:T(8,128)S(1)}, u32[]{:S(2)}, u32[]{:S(2)}) %all-to-all-start.10) | async-done | bytes 524320 | tf_op jit(solution)/shard_map/all_to_all | solution.py:474
  134.6 0.0 copy-done.2
  134.6 0.0 copy-done.3
  134.6 0.8 conditional.1
  134.6 0.8 copy_bitcast_fusion
  (1 shorter events, 0.0 us)
Async XLA Ops:
  1.6 19.7 %all-to-all-start.6 = ((f32[32,2,2,8,128]{4,3,2,1,0:T(8,128)}), f32[32,2,2,8,128]{4,3,2,1,0:T(8,128)S(1)}, u32[]{:S(2)}, u32[]{:S(2)}) async-start(f32[32,2,2,8,128]{4,3,2,1,0:T(8,128)} %broadcast_in_dim.30), calls=%async_computation.6 | async-start | bytes 1048576 | tf_op jit(solution)/shard_map/all_to_all | solution.py:474
  11.2 61.0 %copy-start = (f32[32,4]{1,0:T(8,128)S(1)}, f32[32,4]{1,0:T(8,128)}, u32[]{:S(2)}) copy-start(f32[32,4]{1,0:T(8,128)} %constant.98.clone.shift_ref) | copy-start | bytes 1540
  47.8 44.2 %copy-start.1 = (s32[64]{0:T(128)S(1)}, s32[64]{0:T(128)}, u32[]{:S(2)}) copy-start(s32[64]{0:T(128)} %count_ref.1) | copy-start | bytes 772
  62.2 6.2 %collective-permute-start.2 = (f32[16,2,2,8,128]{4,3,2,1,0:T(8,128)S(1)}, f32[16,2,2,8,128]{4,3,2,1,0:T(8,128)S(1)}, u32[]{:S(2)}, u32[]{:S(2)}) collective-permute-start(f32[16,2,2,8,128]{4,3,2,1,0:T(8,128)S(1)} %get-tuple-element.315), channel_id=1, source_target_pairs={{0,32},{32,64},{64,96},{96,128},{128,160},{160,192},{192,224},{1,3... | collective-permute-start | bytes 786440 | tf_op jit(solution)/shard_map/ppermute | solution.py:512
  63.6 8.7 %collective-permute-start.3 = (f32[16,2,2,8,128]{4,3,2,1,0:T(8,128)S(1)}, f32[16,2,2,8,128]{4,3,2,1,0:T(8,128)S(1)}, u32[]{:S(2)}, u32[]{:S(2)}) collective-permute-start(f32[16,2,2,8,128]{4,3,2,1,0:T(8,128)S(1)} %get-tuple-element.314), channel_id=1, source_target_pairs={{32,0},{64,32},{96,64},{128,96},{160,128},{192,160},{224,192},{33,... | collective-permute-start | bytes 786440 | tf_op jit(solution)/shard_map/ppermute | solution.py:513
  92.1 42.5 %copy-start.2 = (f32[2,128,128]{2,1,0:T(8,128)S(1)}, f32[2,128,128]{2,1,0:T(8,128)}, u32[]{:S(2)}) copy-start(f32[2,128,128]{2,1,0:T(8,128)} %param.9) | copy-start | bytes 393220
  92.1 42.5 %copy-start.3 = (f32[4,2,128,128]{3,2,1,0:T(8,128)S(1)}, f32[4,2,128,128]{3,2,1,0:T(8,128)}, u32[]{:S(2)}) copy-start(f32[4,2,128,128]{3,2,1,0:T(8,128)} %param.8) | copy-start | bytes 1572868
  112.9 21.7 %all-to-all-start.10 = ((f32[16,4,2,8,128]{4,3,2,1,0:T(8,128)}), f32[16,4,2,8,128]{4,3,2,1,0:T(8,128)S(1)}, u32[]{:S(2)}, u32[]{:S(2)}) async-start(f32[16,4,2,8,128]{4,3,2,1,0:T(8,128)} %bitcast.39), calls=%async_computation.10 | async-start | bytes 1048576 | tf_op jit(solution)/shard_map/all_to_all | solution.py:474

commit v3 on v2

--- a/solution.py
+++ b/solution.py
@@ -11,6 +11,8 @@
 
 L = 64
 STEPS = 6
+HALO = 6
+NX = 128
 NZ = 32
 PAIRS = L // 2
 TM = ("z", "core")
@@ -200,15 +202,24 @@
     return [halves[i % 2][i // 2] for i in range(n)]
 
 
-def forward_kernel(x_ref, after_ref, out_ref):
-    del after_ref
+def band_edges():
+    return 16 * lax.axis_index("z") + 16 * lax.axis_index("core") - 8
+
+
+def forward_kernel(x_ref, abs_ref, out_ref):
+    for core in range(2):
+        row = pl.multiple_of(jnp.clip(band_edges() + 8 * core, 0, NX - 8), 8)
+        for zz in range(2):
+            rows = abs_ref[zz, pl.ds(row, 8), :]
+            for slot in range(16 * core, 16 * core + 16):
+                out_ref[slot, 4 + zz] = rows
     for zz in range(2):
         spectrum = real_transform([x_ref[n, zz] * decay**n for n in range(L)])
-        out_ref[0, 0, zz] = spectrum[0][0]
-        out_ref[0, 1, zz] = spectrum[PAIRS][0]
+        out_ref[0, zz] = spectrum[0][0]
+        out_ref[0, 2 + zz] = spectrum[PAIRS][0]
         for k in range(1, PAIRS):
-            out_ref[k, 0, zz] = spectrum[k][0]
-            out_ref[k, 1, zz] = spectrum[k][1]
+            out_ref[k, zz] = spectrum[k][0]
+            out_ref[k, 2 + zz] = spectrum[k][1]
 
 
 def inverse_kernel(s_ref, out_ref, failed_ref):
@@ -238,113 +249,131 @@
     return terms[0]
 
 
-def basis_kernel(shift_ref, own_ref, left_ref, right_ref, abs_ref, v_ref, inv_ref, gram_ref, u, edge, edge_inv, last, sums):
-    slot, z = lax.axis_index(SLOTS), lax.axis_index("z")
-    shift_a, shift_b, shift_im = (shift_ref[slot, i] for i in range(3))
+def pick(slot, values):
+    found = jnp.float32(values[0])
+    for i in range(1, len(values)):
+        found = jnp.where(slot == i, jnp.float32(values[i]), found)
+    return found
+
+
+def edges_kernel(own_ref, up_ref, down_ref, abs_ref):
+    for sp in range(16):
+        for i in range(4):
+            up_ref[sp, pl.ds(HALO * i, HALO), :] = own_ref[1, sp, i, pl.ds(8 - HALO, HALO), :]
+            down_ref[sp, pl.ds(HALO * i, HALO), :] = own_ref[0, sp, i, pl.ds(0, HALO), :]
+        for side in range(2):
+            for zz in range(2):
+                abs_ref[side, sp, zz] = own_ref[side, sp, 4 + zz]
+
+
+def basis_kernel(own_ref, left_ref, right_ref, swap_ref, v_ref, inv_ref, gram_ref, u, edge_inv, sums):
+    slot, z, core = lax.axis_index(SLOTS), lax.axis_index("z"), lax.axis_index("core")
+    shifts_here = slot_shifts()
+    shift_a, shift_b, shift_im = (pick(slot, shifts_here[:, i]) for i in range(3))
     lanes = lax.broadcasted_iota(jnp.int32, (8, 128), 1)
     first_lane, last_lane = lanes == 0, lanes == 127
     blank = jnp.zeros((8, 128), jnp.float32)
 
-    for part in range(2):
-        for row in range(0, 48, 8):
-            u[part, 0, pl.ds(row, 8), :] = blank
-            u[part, NZ + 1, pl.ds(row, 8), :] = blank
+    for turn in range(2):
+        for part in range(2):
+            for row in range(8, 40, 8):
+                u[turn, part, 0, pl.ds(row, 8), :] = blank
+                u[turn, part, NZ + 1, pl.ds(row, 8), :] = blank
+
+    def put(turn, tile, layer, inverse, re, im):
+        a, b, c = inverse
+        u[turn, 0, layer, pl.ds(8 + 8 * tile, 8), :] = a * re - c * im
+        u[turn, 1, layer, pl.ds(8 + 8 * tile, 8), :] = b * im + c * re
 
     def prepare(sp, _):
-        for part in range(2):
+        for turn in range(2):
+            for part in range(2):
+                for zz in range(2):
+                    u[turn, part, 2 * sp + zz + 1, pl.ds(0, 8), :] = blank
+                    u[turn, part, 2 * sp + zz + 1, pl.ds(40, 8), :] = blank
+        for tile in range(4):
             for zz in range(2):
-                u[part, 2 * sp + zz + 1, pl.ds(0, 8), :] = blank
-                u[part, 2 * sp + zz + 1, pl.ds(40, 8), :] = blank
-        for tile in range(4):
-            inside = True
-            if tile == 0:
-                inside = z > 0
-            if tile == 3:
-                inside = z < lax.axis_size("z") - 1
-            for zz in range(2):
-                base = abs_ref[tile // 2, sp, zz, tile % 2]
+                mine, other = own_ref[tile // 2, sp, 4 + zz], swap_ref[tile // 2, sp, zz]
+                base = jnp.where(core == tile % 2, mine, other)
                 da, db = (shift_a + 6.0) + base, (shift_b + 6.0) + base
                 ra, rb = 1.0 / (da * da + shift_im * shift_im), 1.0 / (db * db + shift_im * shift_im)
-                found = (da * ra, db * rb, -shift_im * ra)
-                for i in range(3):
-                    if tile in (1, 2):
+                found = [da * ra, db * rb, -shift_im * ra]
+                if tile in (1, 2):
+                    for i in range(3):
                         inv_ref[i, tile - 1, sp, zz] = found[i]
-                    else:
-                        edge_inv[i, tile // 3, sp, zz] = jnp.where(inside, found[i], 0.0)
+                    re, im = (own_ref[tile - 1, sp, 2 * part + zz] for part in range(2))
+                else:
+                    inside = z > 0 if tile == 0 else z < lax.axis_size("z") - 1
+                    found = [jnp.where(inside, f, 0.0) for f in found]
+                    for i in range(3):
+                        edge_inv[i, tile // 3, sp, zz] = found[i]
+                    pair = []
+                    for part in range(2):
+                        at = HALO * (2 * part + zz)
+                        if tile == 0:
+                            start = max(at - (8 - HALO), 0)
+                            rows = left_ref[sp, pl.ds(start, 8), :]
+                            shift = start - (at - (8 - HALO))
+                        else:
+                            start = min(at, 4 * HALO - 8)
+                            rows = right_ref[sp, pl.ds(start, 8), :]
+                            shift = (start - at) % 8
+                        pair.append(pltpu.roll(rows, shift, 0) if shift else rows)
+                    re, im = pair
+                put(0, tile, 2 * sp + zz + 1, found, re, im)
         return 0
 
     lax.fori_loop(0, NZ // 2, prepare, 0, unroll=4)
 
+    def vector(j, side, sp, zz):
+        if j == 0:
+            return [own_ref[side, sp, 2 * part + zz] for part in range(2)]
+        return [v_ref[j - 1, part, side, sp, zz] for part in range(2)]
+
     for j in range(STEPS):
-        def scaled(sp, _, j=j):
-            for tile in range(4):
+        names = [name for name in entry if name[2] == j + 1 or (j == 0 and name[2] == 0)]
+
+        def step(group, totals, j=j, names=names):
+            by_layer = []
+            for sp in [4 * group + s for s in range(4)]:
+                found = {name: [] for name in names}
                 for zz in range(2):
-                    if tile in (1, 2):
-                        a, b, c = (inv_ref[i, tile - 1, sp, zz] for i in range(3))
-                        re, im = ((own_ref[tile - 1, sp, part, zz] if j == 0 else v_ref[j - 1, part, tile - 1, sp, zz]) for part in range(2))
-                    else:
-                        a, b, c = (edge_inv[i, tile // 3, sp, zz] for i in range(3))
-                        side = (left_ref, None, None, right_ref)[tile]
-                        re, im = ((side[sp, part, zz] if j == 0 else edge[part, tile // 3, sp, zz]) for part in range(2))
-                    u[0, 2 * sp + zz + 1, pl.ds(8 + 8 * tile, 8), :] = a * re - c * im
-                    u[1, 2 * sp + zz + 1, pl.ds(8 + 8 * tile, 8), :] = b * im + c * re
-            return 0
-
-        lax.fori_loop(0, NZ // 2, scaled, 0, unroll=4)
-
-        def spread(sp, _, j=j):
-            for tile in range(4) if j < STEPS - 1 else (1, 2):
-                for zz in range(2):
-                    for part in range(2):
+                    for tile in range(4) if j < STEPS - 1 else (1, 2):
                         layer, row = 2 * sp + zz + 1, 8 + 8 * tile
-                        here = u[part, layer, pl.ds(row, 8), :]
-                        total = u[part, layer - 1, pl.ds(row, 8), :] + u[part, layer + 1, pl.ds(row, 8), :]
-                        total = total + (u[part, layer, pl.ds(row - 1, 8), :] + u[part, layer, pl.ds(row + 1, 8), :])
-                        total = total + (
-                            jnp.where(first_lane, 0.0, pltpu.roll(here, 1, 1))
-                            + jnp.where(last_lane, 0.0, pltpu.roll(here, 127, 1))
-                        )
+                        pair = []
+                        for part in range(2):
+                            old = u.at[j % 2, part]
+                            here = old[layer, pl.ds(row, 8), :]
+                            total = old[layer - 1, pl.ds(row, 8), :] + old[layer + 1, pl.ds(row, 8), :]
+                            total = total + (old[layer, pl.ds(row - 1, 8), :] + old[layer, pl.ds(row + 1, 8), :])
+                            total = total + (
+                                jnp.where(first_lane, 0.0, pltpu.roll(here, 1, 1))
+                                + jnp.where(last_lane, 0.0, pltpu.roll(here, 127, 1))
+                            )
+                            pair.append(total)
                         if tile in (1, 2):
+                            side = tile - 1
                             if j < STEPS - 1:
-                                v_ref[j, part, tile - 1, sp, zz] = total
+                                for part in range(2):
+                                    v_ref[j, part, side, sp, zz] = pair[part]
+                            known = [vector(i, side, sp, zz) for i in range(j + 1)] + [pair]
+                            for kind, i, k in names:
+                                a, b = known[i], known[k]
+                                if kind == "x":
+                                    found[kind, i, k].append(a[0] * b[1] - a[1] * b[0])
+                                else:
+                                    part = ("re", "im").index(kind)
+                                    found[kind, i, k].append(a[part] * b[part])
+                        if j < STEPS - 1:
+                            if tile in (1, 2):
+                                inverse = [inv_ref[i, tile - 1, sp, zz] for i in range(3)]
                             else:
-                                last[part, tile - 1, sp, zz] = total
-                        else:
-                            edge[part, tile // 3, sp, zz] = total
-            return 0
-
-        lax.fori_loop(0, NZ // 2, spread, 0, unroll=8)
-
-    def vector(j, part, side, sp, zz):
-        if j == 0:
-            return own_ref[side, sp, part, zz]
-        if j == STEPS:
-            return last[part, side, sp, zz]
-        return v_ref[j - 1, part, side, sp, zz]
-
-    for i in range(STEPS + 1):
-        names = [name for name in entry if name[1] == i]
-
-        def inner(sp, totals, names=names, i=i):
-            places = [(side, zz) for side in range(2) for zz in range(2)]
-            left = [[vector(i, part, side, sp, zz) for part in range(2)] for side, zz in places]
-            out = []
-            for j in range(i, STEPS + 1):
-                right = left if j == i else [[vector(j, part, side, sp, zz) for part in range(2)] for side, zz in places]
-                pairs = list(zip(left, right))
-                out.append(("re", i, j, tree_sum([a[0] * b[0] for a, b in pairs])))
-                out.append(("im", i, j, tree_sum([a[1] * b[1] for a, b in pairs])))
-                if j > i:
-                    out.append(("x", i, j, tree_sum([a[0] * b[1] - a[1] * b[0] for a, b in pairs])))
-            found = {o[:3]: o[3] for o in out}
-            return tuple(t + found[name] for t, name in zip(totals, names))
-
-        def outer(group, totals, names=names, inner=inner):
-            part_totals = tuple(blank for _ in names)
-            part_totals = lax.fori_loop(group * 4, group * 4 + 4, inner, part_totals)
-            return tuple(a + b for a, b in zip(totals, part_totals))
-
-        totals = lax.fori_loop(0, 4, outer, tuple(blank for _ in names))
+                                inverse = [edge_inv[i, tile // 3, sp, zz] for i in range(3)]
+                            put((j + 1) % 2, tile, layer, inverse, *pair)
+                by_layer.append([tree_sum(found[name]) for name in names])
+            return tuple(t + tree_sum(list(parts)) for t, parts in zip(totals, zip(*by_layer)))
+
+        totals = lax.fori_loop(0, NZ // 8, step, tuple(blank for _ in names), unroll=2)
         for name, total in zip(names, totals):
             sums[entry[name]] = total
     for spare in range(len(entry), sums.shape[0]):
@@ -377,13 +406,16 @@
         imag = jnp.where(ends, 0.0, spread(("x", i, j))) if j > i else jnp.zeros_like(real)
         gram[i, j] = (real, imag)
 
-    count_a = count_ref[slot]
-    count_b = count_ref[jnp.where(ends, PAIRS, L - slot)]
+    count_lane = lax.broadcasted_iota(jnp.int32, (1, L), 1)
+    count_a, count_b = (
+        jnp.sum(jnp.where(count_lane == k, count_ref[...], 0).astype(jnp.float32), axis=1, keepdims=True)
+        for k in (slot, jnp.where(ends, PAIRS, L - slot))
+    )
     one, none = jnp.ones((8, 128), jnp.float32), jnp.zeros((8, 128), jnp.float32)
     poly, answer = [(one, none)], [(none, none) for _ in range(STEPS)]
     bound, doubt, scale = gram_rounding * gram[0, 0][0], none, None
     for m in range(STEPS):
-        in_a, in_b = (jnp.where(m < count, one, none) for count in (count_a, count_b))
+        in_a, in_b = (jnp.broadcast_to(jnp.where(m < count, 1.0, 0.0), (8, 128)) for count in (count_a, count_b))
         weight = jnp.where(ends, jnp.where(low, in_a, in_b), in_a + in_b)
         g00, g01, g11 = gram[0, 0][0], gram[0, 1], gram[1, 1][0]
         denominator = (g00 - 2.0 * g01[0] + g11) + norm_floor
@@ -448,7 +480,7 @@
             for zz in range(2):
                 res, ims = [], []
                 for j, (wa, wb, wi) in enumerate(weights):
-                    re, im = ((own_ref[side, sp, part, zz] if j == 0 else v_ref[j - 1, part, side, sp, zz]) for part in range(2))
+                    re, im = ((own_ref[side, sp, 2 * part + zz] if j == 0 else v_ref[j - 1, part, side, sp, zz]) for part in range(2))
                     res.append(wa * re - wi * im)
                     ims.append(wb * im + wi * re)
                 re, im = tree_sum(res), tree_sum(ims)
@@ -491,50 +523,51 @@
 
 
 def together(residual, absorption, counts):
-    z, chips = lax.axis_index("z"), lax.axis_size("z")
-
-    tall = jnp.pad(absorption, ((0, 0), (8, 8), (0, 0)))
-    first = 16 * z + 16 * lax.axis_index("core")
-    near = lax.dynamic_slice_in_dim(tall, first, 16, axis=1).reshape(2, 2, 8, 128)
-    near = exchanged(jnp.broadcast_to(near, (32, 2, 2, 8, 128)), SLOTS)
-
+    chips = lax.axis_size("z")
     bands = residual.reshape(4, 2, 16, 8, 128).transpose(2, 0, 1, 3, 4)
     series = exchanged(bands, TM).reshape(L, 2, 8, 128)
     spectrum = pl.pallas_call(
         forward_kernel,
-        out_shape=f32(PAIRS, 2, 2, 8, 128),
+        out_shape=f32(PAIRS, 6, 8, 128),
         in_specs=[VMEM, VMEM],
         out_specs=VMEM,
         compiler_params=room(4),
         name="forward",
-    )(held(series), held(near))
-    own = exchanged(spectrum, SLOTS).reshape(2, 16, 2, 2, 8, 128)
-    left = lax.ppermute(own[1], "z", [(i, i + 1) for i in range(chips - 1)])
-    right = lax.ppermute(own[0], "z", [(i + 1, i) for i in range(chips - 1)])
+    )(held(series), held(absorption))
+    own = held(exchanged(spectrum, SLOTS).reshape(2, 16, 6, 8, 128))
+    up, down, swap = pl.pallas_call(
+        edges_kernel,
+        out_shape=(f32(16, 4 * HALO, 128), f32(16, 4 * HALO, 128), f32(2, 16, 2, 8, 128)),
+        in_specs=[VMEM],
+        out_specs=(VMEM, VMEM, VMEM),
+        compiler_params=room(2),
+        name="edges",
+    )(own)
+    left = lax.ppermute(up, "z", [(i, i + 1) for i in range(chips - 1)])
+    right = lax.ppermute(down, "z", [(i + 1, i) for i in range(chips - 1)])
+    swap = lax.ppermute(swap, "core", [(0, 1), (1, 0)])
     basis, inverses, partial = pl.pallas_call(
         basis_kernel,
         out_shape=(f32(STEPS - 1, 2, 2, 16, 2, 8, 128), f32(3, 2, 16, 2, 8, 128), f32(8, 8, 128)),
-        in_specs=[SMEM, VMEM, VMEM, VMEM, VMEM],
+        in_specs=[VMEM, VMEM, VMEM, VMEM],
         out_specs=(VMEM, VMEM, VMEM),
         scratch_shapes=[
-            pltpu.VMEM((2, NZ + 2, 48, 128), jnp.float32),
-            pltpu.VMEM((2, 2, 16, 2, 8, 128), jnp.float32),
+            pltpu.VMEM((2, 2, NZ + 2, 48, 128), jnp.float32),
             pltpu.VMEM((3, 2, 16, 2, 8, 128), jnp.float32),
-            pltpu.VMEM((2, 2, 16, 2, 8, 128), jnp.float32),
             pltpu.VMEM((80, 8, 128), jnp.float32),
         ],
         compiler_params=room(10),
         name="basis",
-    )(jnp.asarray(slot_shifts()), held(own), held(left), held(right), held(near.reshape(2, 16, 2, 2, 8, 128)))
+    )(own, held(left), held(right), held(swap))
     partials = exchanged(partial, "z")
     solved = pl.pallas_call(
         combine_kernel,
         out_shape=f32(2, 16, 2, 2, 8, 128),
-        in_specs=[SMEM, VMEM, VMEM, VMEM, VMEM],
+        in_specs=[VMEM, VMEM, VMEM, VMEM, VMEM],
         out_specs=VMEM,
         compiler_params=room(6),
         name="combine",
-    )(counts, held(partials), held(own), held(basis), held(inverses))
+    )(held(counts.reshape(1, L)), held(partials), own, held(basis), held(inverses))
     gathered = exchanged(solved.reshape(32, 2, 2, 8, 128), SLOTS)
     values, failed = pl.pallas_call(
         inverse_kernel,
@@ -544,16 +577,21 @@
         compiler_params=room(4),
         name="inverse",
     )(held(gathered))
-    return exchanged(values.reshape(16, 4, 2, 8, 128), TM), failed
+    return values, failed
+
+
+def to_steps(values, shape):
+    bands = exchanged(values.reshape(16, 4, 2, 8, 128), TM)
+    return bands.transpose(1, 2, 0, 3, 4).reshape(shape)
 
 
 def body(residual, absorption, counts):
-    bands, failed = together(residual, absorption, counts)
+    values, failed = together(residual, absorption, counts)
     return lax.cond(
         failed[0] > 0,
-        lambda r, a, c, b: stepwise(r, a, c),
-        lambda r, a, c, b: b.transpose(1, 2, 0, 3, 4).reshape(r.shape),
-        residual, absorption, counts, bands,
+        lambda r, a, c, v: stepwise(r, a, c),
+        lambda r, a, c, v: to_steps(v, r.shape),
+        residual, absorption, counts, values,
     )
 
 

time: 136 us -> 120 us (0.88)
  waiting for transfers between devices: 34.2 us -> 18.1 us
  blocking collectives: 70.1 us -> 79.5 us
  starting transfers between devices: 15.6 us -> 10.2 us
  Pallas kernels: 11.4 us -> 8.26 us
    all_to_all x2 -> x1, waiting for transfers between devices: 26.8 us -> 11.1 us  [exchanged(): return lax.all_to_all(blocks, axes, split_axis=0, concat_axis=0, tiled=True)]
    all_to_all x4, blocking collectives: 70.1 us -> 79.5 us  [exchanged(): return lax.all_to_all(blocks, axes, split_axis=0, concat_axis=0, tiled=True)]
    all_to_all x2 -> x1, starting transfers between devices: 13 us -> 6.24 us  [exchanged(): return lax.all_to_all(blocks, axes, split_axis=0, concat_axis=0, tiled=True)]
    pallas_call x1, Pallas kernels: 8.7 us -> 5.41 us  [together(): pl.pallas_call(basis_kernel, out_shape=(f32(STEPS - 1, 2, 2, 16, 2, 8, 12...]
    unnamed x8 -> x10, local copies, waits for them, and re-layouts: 0.02 us -> 1.7 us
    reshape x2 -> x0, local copies, waits for them, and re-layouts: 1.55 us -> none  [the longest x1 0.83 us: body(): b.transpose(1, 2, 0, 3, 4).reshape(r.shape)]
    ppermute x2 -> x3, starting transfers between devices: 2.6 us -> 3.93 us  [the longest x1 1.35 us: together(): swap = lax.ppermute(swap, 'core', [(0, 1), (1, 0)])]
    ppermute x2 -> x3, waiting for transfers between devices: 7.41 us -> 7.03 us  [the longest x1 3.84 us: together(): right = lax.ppermute(down, 'z', [(i + 1, i) for i in range(chips - 1)])]
  transfers between devices with their start and end apart: 4 -> 4, of which waited for: 4 -> 3; matrix products, arithmetic and copies ran while one was open for 1% -> 0% of each run, Pallas kernels for 0% -> 0%
where the time goes in v3:
time: 120 us
  blocking collectives  79.5 us (66%)
  waiting for transfers between devices  18.1 us (15%)
  starting transfers between devices  10.2 us (8%)
  Pallas kernels  8.26 us (7%)
  local copies, waits for them, and re-layouts  2.82 us (2%)
    all_to_all x4, blocking collectives, exchanged(): return lax.all_to_all(blocks, axes, split_axis=0, concat_axis=0, tiled=True)  79.5 us
    all_to_all x1, waiting for transfers between devices, exchanged(): return lax.all_to_all(blocks, axes, split_axis=0, concat_axis=0, tiled=True)  11.1 us
    all_to_all x1, starting transfers between devices, exchanged(): return lax.all_to_all(blocks, axes, split_axis=0, concat_axis=0, tiled=True)  6.24 us
    pallas_call x1, Pallas kernels, together(): pl.pallas_call(basis_kernel, out_shape=(f32(STEPS - 1, 2, 2, 16, 2, 8, 12...  5.41 us
    ppermute x1, waiting for transfers between devices, together(): right = lax.ppermute(down, 'z', [(i + 1, i) for i in range(chips - 1)])  3.84 us
    ppermute x1, waiting for transfers between devices, together(): left = lax.ppermute(up, 'z', [(i, i + 1) for i in range(chips - 1)])  3.18 us
  transfers between devices with their start and end apart: 4, of which 3 were waited for; matrix products, arithmetic and copies ran while one was open for 0% of the time, Pallas kernels for 0%

profile of v3, /device:TPU:1, one launch (start us, length us, event | category | flops | bytes accessed | tf_op | source)
XLA Modules:
  0.0 119.9 jit_solution(1574553756125326357)
XLA Ops:
  0.0 1.1 copy_bitcast_fusion.5
  1.1 27.0 %all_to_all.95 = f32[16,4,2,8,128]{4,3,2,1,0:T(8,128)S(1)} all-to-all(f32[16,4,2,8,128]{4,3,2,1,0:T(8,128)S(1)} %copy_bitcast_fusion.5), channel_id=1, replica_groups=mesh['z'=8,'core'=2,'y'=4,'x'=4] {'z','core'}, dimensions={0} | all-to-all | bytes 1048576 | tf_op jit(solution)/shard_map/all_to_all | solution.py:506
  28.1 0.0 copy-start.1
  28.1 0.9 copy-done.1
  29.0 0.0 copy-start
  29.0 0.2 forward.1
  29.2 20.7 %all_to_all.96 = f32[32,6,8,128]{3,2,1,0:T(8,128)S(1)} all-to-all(f32[32,6,8,128]{3,2,1,0:T(8,128)S(1)} %forward.1), channel_id=1, replica_groups=mesh['z'=8,'core'=2,'y'=4,'x'=4] {'core','y','x'}, dimensions={0} | all-to-all | bytes 1572864 | tf_op jit(solution)/shard_map/all_to_all | solution.py:506
  49.9 0.1 edges.1
  49.9 1.3 %collective-permute-start.4 = (f32[2,16,2,8,128]{4,3,2,1,0:T(8,128)S(1)}, f32[2,16,2,8,128]{4,3,2,1,0:T(8,128)S(1)}, u32[]{:S(2)}, u32[]{:S(2)}) collective-permute-start(f32[2,16,2,8,128]{4,3,2,1,0:T(8,128)S(1)} %get-tuple-element.169), channel_id=1, source_target_pairs={{0,16},{16,0},{1,17},{17,1},{2,18},{18,2},{3,19},{19,3},{4,20},{20... | collective-permute-start | bytes 786440 | tf_op jit(solution)/shard_map/ppermute | solution.py:548
  51.3 1.3 %collective-permute-start.2 = (f32[16,24,128]{2,1,0:T(8,128)S(1)}, f32[16,24,128]{2,1,0:T(8,128)S(1)}, u32[]{:S(2)}, u32[]{:S(2)}) collective-permute-start(f32[16,24,128]{2,1,0:T(8,128)S(1)} %get-tuple-element.167), channel_id=1, source_target_pairs={{0,32},{32,64},{64,96},{96,128},{128,160},{160,192},{192,224},{1,3... | collective-permute-start | bytes 589832 | tf_op jit(solution)/shard_map/ppermute | solution.py:546
  52.6 1.3 %collective-permute-start.3 = (f32[16,24,128]{2,1,0:T(8,128)S(1)}, f32[16,24,128]{2,1,0:T(8,128)S(1)}, u32[]{:S(2)}, u32[]{:S(2)}) collective-permute-start(f32[16,24,128]{2,1,0:T(8,128)S(1)} %get-tuple-element.168), channel_id=1, source_target_pairs={{32,0},{64,32},{96,64},{128,96},{160,128},{192,160},{224,192},{33,... | collective-permute-start | bytes 589832 | tf_op jit(solution)/shard_map/ppermute | solution.py:547
  53.9 3.2 %collective-permute-done.2.left_ref = f32[16,24,128]{2,1,0:T(8,128)S(1)} collective-permute-done((f32[16,24,128]{2,1,0:T(8,128)S(1)}, f32[16,24,128]{2,1,0:T(8,128)S(1)}, u32[]{:S(2)}, u32[]{:S(2)}) %collective-permute-start.2) | collective-permute-done | bytes 196640 | tf_op jit(solution)/shard_map/ppermute | solution.py:546
  57.1 3.8 %collective-permute-done.3.right_ref = f32[16,24,128]{2,1,0:T(8,128)S(1)} collective-permute-done((f32[16,24,128]{2,1,0:T(8,128)S(1)}, f32[16,24,128]{2,1,0:T(8,128)S(1)}, u32[]{:S(2)}, u32[]{:S(2)}) %collective-permute-start.3) | collective-permute-done | bytes 196640 | tf_op jit(solution)/shard_map/ppermute | solution.py:547
  60.9 0.0 collective-permute-done.4.swap_ref
  60.9 5.4 %basis.1 = (f32[5,2,2,16,2,8,128]{6,5,4,3,2,1,0:T(8,128)S(1)}, f32[3,2,16,2,8,128]{5,4,3,2,1,0:T(8,128)S(1)}, f32[8,8,128]{2,1,0:T(8,128)S(1)}) custom-call(f32[2,16,6,8,128]{4,3,2,1,0:T(8,128)S(1)} %bitcast.92, f32[16,24,128]{2,1,0:T(8,128)S(1)} %collective-permute-done.2.left_ref, f32[16,24,128]{2,1,0:T(8,128)S(1)} %collective-permute-done.3.right_ref, ...), custom_call_target="tpu_custom_call" | custom-call | tf_op jit(solution)/shard_map/basis/pallas_call | solution.py:549
  66.3 11.1 %all_to_all.97.part_ref = f32[8,8,128]{2,1,0:T(8,128)S(1)} all-to-all(f32[8,8,128]{2,1,0:T(8,128)S(1)} %get-tuple-element.170), channel_id=1, replica_groups=mesh['z'=8,'core'=2,'y'=4,'x'=4] {'z'}, dimensions={0} | all-to-all | bytes 65536 | tf_op jit(solution)/shard_map/all_to_all | solution.py:506
  77.4 0.0 copy-done
  77.4 0.0 copy-start.2
  77.4 0.0 copy-start.3
  77.4 1.7 %combine.1 = f32[2,16,2,2,8,128]{5,4,3,2,1,0:T(8,128)} custom-call(s32[1,64]{1,0:T(1,128)S(1)} %bitcast.90, f32[8,8,128]{2,1,0:T(8,128)S(1)} %all_to_all.97.part_ref, f32[2,16,6,8,128]{4,3,2,1,0:T(8,128)S(1)} %bitcast.93, f32[5,2,2,16,2,8,128]{6,5,4,3,2,1,0:T(8,128)S(1)} %get-tuple-element.171.v_ref, f32[3,2,16,2,8,128]{5,4,3,2,1,0:T(8,128)S(1)} %get-tuple-element.172.inv_ref), custom_call_target="tpu_custom_call" | custom-call | tf_op jit(solution)/shard_map/combine/pallas_call | solution.py:563
  79.1 6.2 %all-to-all-start.9 = ((f32[32,2,2,8,128]{4,3,2,1,0:T(8,128)}), f32[32,2,2,8,128]{4,3,2,1,0:T(8,128)S(1)}, u32[]{:S(2)}, u32[]{:S(2)}) async-start(f32[32,2,2,8,128]{4,3,2,1,0:T(8,128)} %bitcast.37), calls=%async_computation.9 | async-start | bytes 1048576 | tf_op jit(solution)/shard_map/all_to_all | solution.py:506
  85.3 11.1 %all-to-all-done.9.s_ref = f32[32,2,2,8,128]{4,3,2,1,0:T(8,128)S(1)} async-done(((f32[32,2,2,8,128]{4,3,2,1,0:T(8,128)}), f32[32,2,2,8,128]{4,3,2,1,0:T(8,128)S(1)}, u32[]{:S(2)}, u32[]{:S(2)}) %all-to-all-start.9) | async-done | bytes 524320 | tf_op jit(solution)/shard_map/all_to_all | solution.py:506
  96.5 0.9 inverse.1
  98.0 0.0 copy-done.2
  98.0 0.0 copy-done.3
  98.0 21.1 %conditional.1 = (f32[4,2,128,128]{3,2,1,0:T(8,128)S(1)}) conditional(s32[]{:T(128)} %bitcast.38, f32[64,2,8,128]{3,2,1,0:T(8,128)S(1)} %get-tuple-element.174, (f32[4,2,128,128]{3,2,1,0:T(8,128)S(1)}, s32[64]{0:T(128)S(1)}, f32[2,128,128]{2,1,0:T(8,128)S(1)}) %tuple.78), branch_computations={%region_0.0_spmd, %region_1.9_spmd} | conditional | flops 413107744 | bytes 58483476 | solution.py:590
  98.0 20.8 %all_to_all.92 = f32[16,4,2,8,128]{4,3,2,1,0:T(8,128)S(1)} all-to-all(f32[16,4,2,8,128]{4,3,2,1,0:T(8,128)S(1)} %bitcast.95), channel_id=1, replica_groups=mesh['z'=8,'core'=2,'y'=4,'x'=4] {'z','core'}, dimensions={0} | all-to-all | bytes 1048576 | tf_op jit(solution)/shard_map/cond/branch_0_fun/all_to_all | solution.py:506
  119.1 0.0 copy-start.4
  119.1 0.8 copy-done.4
  (1 shorter events, 0.0 us)
Async XLA Ops:
  28.1 0.9 copy-start.1
  29.0 48.4 %copy-start = (s32[64]{0:T(128)S(1)}, s32[64]{0:T(128)}, u32[]{:S(2)}) copy-start(s32[64]{0:T(128)} %param.9) | copy-start | bytes 772
  49.9 11.0 %collective-permute-start.4 = (f32[2,16,2,8,128]{4,3,2,1,0:T(8,128)S(1)}, f32[2,16,2,8,128]{4,3,2,1,0:T(8,128)S(1)}, u32[]{:S(2)}, u32[]{:S(2)}) collective-permute-start(f32[2,16,2,8,128]{4,3,2,1,0:T(8,128)S(1)} %get-tuple-element.169), channel_id=1, source_target_pairs={{0,16},{16,0},{1,17},{17,1},{2,18},{18,2},{3,19},{19,3},{4,20},{20... | collective-permute-start | bytes 786440 | tf_op jit(solution)/shard_map/ppermute | solution.py:548
  51.3 5.8 %collective-permute-start.2 = (f32[16,24,128]{2,1,0:T(8,128)S(1)}, f32[16,24,128]{2,1,0:T(8,128)S(1)}, u32[]{:S(2)}, u32[]{:S(2)}) collective-permute-start(f32[16,24,128]{2,1,0:T(8,128)S(1)} %get-tuple-element.167), channel_id=1, source_target_pairs={{0,32},{32,64},{64,96},{96,128},{128,160},{160,192},{192,224},{1,3... | collective-permute-start | bytes 589832 | tf_op jit(solution)/shard_map/ppermute | solution.py:546
  52.6 8.3 %collective-permute-start.3 = (f32[16,24,128]{2,1,0:T(8,128)S(1)}, f32[16,24,128]{2,1,0:T(8,128)S(1)}, u32[]{:S(2)}, u32[]{:S(2)}) collective-permute-start(f32[16,24,128]{2,1,0:T(8,128)S(1)} %get-tuple-element.168), channel_id=1, source_target_pairs={{32,0},{64,32},{96,64},{128,96},{160,128},{192,160},{224,192},{33,... | collective-permute-start | bytes 589832 | tf_op jit(solution)/shard_map/ppermute | solution.py:547
  77.4 20.6 %copy-start.2 = (f32[2,128,128]{2,1,0:T(8,128)S(1)}, f32[2,128,128]{2,1,0:T(8,128)}, u32[]{:S(2)}) copy-start(f32[2,128,128]{2,1,0:T(8,128)} %abs_ref.1) | copy-start | bytes 393220
  77.4 20.6 %copy-start.3 = (f32[4,2,128,128]{3,2,1,0:T(8,128)S(1)}, f32[4,2,128,128]{3,2,1,0:T(8,128)}, u32[]{:S(2)}) copy-start(f32[4,2,128,128]{3,2,1,0:T(8,128)} %param.7) | copy-start | bytes 1572868
  79.1 17.4 %all-to-all-start.9 = ((f32[32,2,2,8,128]{4,3,2,1,0:T(8,128)}), f32[32,2,2,8,128]{4,3,2,1,0:T(8,128)S(1)}, u32[]{:S(2)}, u32[]{:S(2)}) async-start(f32[32,2,2,8,128]{4,3,2,1,0:T(8,128)} %bitcast.37), calls=%async_computation.9 | async-start | bytes 1048576 | tf_op jit(solution)/shard_map/all_to_all | solution.py:506
  119.1 0.8 copy-start.4

commit v4 on v3

--- a/solution.py
+++ b/solution.py
@@ -202,15 +202,24 @@
     return [halves[i % 2][i // 2] for i in range(n)]
 
 
-def band_edges():
-    return 16 * lax.axis_index("z") + 16 * lax.axis_index("core") - 8
-
-
-def forward_kernel(x_ref, abs_ref, out_ref):
+def bands_kernel(x_ref, a_ref, out_ref, rows_ref, sems):
+    copies = [
+        pltpu.make_async_copy(x_ref.at[:, :, pl.ds(8 * band, 8), :], out_ref.at[band], sems.at[band]) for band in range(16)
+    ]
+    first = 16 * lax.axis_index("z") + 16 * lax.axis_index("core") - 8
     for core in range(2):
-        row = pl.multiple_of(jnp.clip(band_edges() + 8 * core, 0, NX - 8), 8)
+        row = pl.multiple_of(jnp.clip(first + 8 * core, 0, NX - 8), 8)
+        copies.append(pltpu.make_async_copy(a_ref.at[:, pl.ds(row, 8), :], rows_ref.at[core], sems.at[16 + core]))
+    for copy in copies:
+        copy.start()
+    for copy in copies:
+        copy.wait()
+
+
+def forward_kernel(x_ref, rows_ref, out_ref):
+    for core in range(2):
         for zz in range(2):
-            rows = abs_ref[zz, pl.ds(row, 8), :]
+            rows = rows_ref[core, zz]
             for slot in range(16 * core, 16 * core + 16):
                 out_ref[slot, 4 + zz] = rows
     for zz in range(2):
@@ -256,17 +265,19 @@
     return found
 
 
-def edges_kernel(own_ref, up_ref, down_ref, abs_ref):
+def edges_kernel(own_ref, first_ref, second_ref, abs_ref):
+    low = lax.axis_index("core") == 0
     for sp in range(16):
         for i in range(4):
-            up_ref[sp, pl.ds(HALO * i, HALO), :] = own_ref[1, sp, i, pl.ds(8 - HALO, HALO), :]
-            down_ref[sp, pl.ds(HALO * i, HALO), :] = own_ref[0, sp, i, pl.ds(0, HALO), :]
+            up, down = own_ref[1, sp, i, pl.ds(8 - HALO, HALO), :], own_ref[0, sp, i, pl.ds(0, HALO), :]
+            first_ref[sp, pl.ds(HALO * i, HALO), :] = jnp.where(low, up, down)
+            second_ref[sp, pl.ds(HALO * i, HALO), :] = jnp.where(low, down, up)
         for side in range(2):
             for zz in range(2):
                 abs_ref[side, sp, zz] = own_ref[side, sp, 4 + zz]
 
 
-def basis_kernel(own_ref, left_ref, right_ref, swap_ref, v_ref, inv_ref, gram_ref, u, edge_inv, sums):
+def basis_kernel(own_ref, first_ref, second_ref, swap_ref, v_ref, inv_ref, gram_ref, u, edge_inv, sums):
     slot, z, core = lax.axis_index(SLOTS), lax.axis_index("z"), lax.axis_index("core")
     shifts_here = slot_shifts()
     shift_a, shift_b, shift_im = (pick(slot, shifts_here[:, i]) for i in range(3))
@@ -310,14 +321,11 @@
                     pair = []
                     for part in range(2):
                         at = HALO * (2 * part + zz)
-                        if tile == 0:
-                            start = max(at - (8 - HALO), 0)
-                            rows = left_ref[sp, pl.ds(start, 8), :]
-                            shift = start - (at - (8 - HALO))
-                        else:
-                            start = min(at, 4 * HALO - 8)
-                            rows = right_ref[sp, pl.ds(start, 8), :]
-                            shift = (start - at) % 8
+                        wanted = at - (8 - HALO) if tile == 0 else at
+                        start = min(max(wanted, 0), 4 * HALO - 8)
+                        first, second = (ref[sp, pl.ds(start, 8), :] for ref in (first_ref, second_ref))
+                        rows = jnp.where((core == 0) == (tile == 0), first, second)
+                        shift = (start - wanted) % 8
                         pair.append(pltpu.roll(rows, shift, 0) if shift else rows)
                     re, im = pair
                 put(0, tile, 2 * sp + zz + 1, found, re, im)
@@ -508,6 +516,7 @@
 
 VMEM = pl.BlockSpec(memory_space=pltpu.VMEM)
 SMEM = pl.BlockSpec(memory_space=pltpu.SMEM)
+ANY = pl.BlockSpec(memory_space=pl.ANY)
 
 
 def f32(*shape):
@@ -518,13 +527,25 @@
     return pltpu.with_memory_space_constraint(x, pltpu.MemorySpace.VMEM)
 
 
+def in_hbm(x):
+    return pltpu.with_memory_space_constraint(x, pltpu.MemorySpace.HBM)
+
+
 def room(mebibytes):
     return pltpu.CompilerParams(vmem_limit_bytes=mebibytes * 2**20)
 
 
 def together(residual, absorption, counts):
     chips = lax.axis_size("z")
-    bands = residual.reshape(4, 2, 16, 8, 128).transpose(2, 0, 1, 3, 4)
+    bands, rows = pl.pallas_call(
+        bands_kernel,
+        out_shape=(f32(16, 4, 2, 8, 128), f32(2, 2, 8, 128)),
+        in_specs=[ANY, ANY],
+        out_specs=(VMEM, VMEM),
+        scratch_shapes=[pltpu.SemaphoreType.DMA((18,))],
+        compiler_params=room(2),
+        name="bands",
+    )(in_hbm(residual), in_hbm(absorption))
     series = exchanged(bands, TM).reshape(L, 2, 8, 128)
     spectrum = pl.pallas_call(
         forward_kernel,
@@ -533,9 +554,9 @@
         out_specs=VMEM,
         compiler_params=room(4),
         name="forward",
-    )(held(series), held(absorption))
+    )(held(series), held(rows))
     own = held(exchanged(spectrum, SLOTS).reshape(2, 16, 6, 8, 128))
-    up, down, swap = pl.pallas_call(
+    first, second, swap = pl.pallas_call(
         edges_kernel,
         out_shape=(f32(16, 4 * HALO, 128), f32(16, 4 * HALO, 128), f32(2, 16, 2, 8, 128)),
         in_specs=[VMEM],
@@ -543,9 +564,11 @@
         compiler_params=room(2),
         name="edges",
     )(own)
-    left = lax.ppermute(up, "z", [(i, i + 1) for i in range(chips - 1)])
-    right = lax.ppermute(down, "z", [(i + 1, i) for i in range(chips - 1)])
+    ups = [[(2 * i + core, 2 * i + 2 + core) for i in range(chips - 1)] for core in range(2)]
+    downs = [[(b, a) for a, b in pairs] for pairs in ups]
     swap = lax.ppermute(swap, "core", [(0, 1), (1, 0)])
+    first = lax.ppermute(first, TM, ups[0] + downs[1])
+    second = lax.ppermute(second, TM, downs[0] + ups[1])
     basis, inverses, partial = pl.pallas_call(
         basis_kernel,
         out_shape=(f32(STEPS - 1, 2, 2, 16, 2, 8, 128), f32(3, 2, 16, 2, 8, 128), f32(8, 8, 128)),
@@ -558,7 +581,7 @@
         ],
         compiler_params=room(10),
         name="basis",
-    )(own, held(left), held(right), held(swap))
+    )(own, held(first), held(second), held(swap))
     partials = exchanged(partial, "z")
     solved = pl.pallas_call(
         combine_kernel,
@@ -571,7 +594,7 @@
     gathered = exchanged(solved.reshape(32, 2, 2, 8, 128), SLOTS)
     values, failed = pl.pallas_call(
         inverse_kernel,
-        out_shape=(f32(L, 2, 8, 128), jax.ShapeDtypeStruct((1,), jnp.int32)),
+        out_shape=(f32(L, 2, 8, 128), pltpu.SMEM((1,), jnp.int32)),
         in_specs=[VMEM],
         out_specs=(VMEM, SMEM),
         compiler_params=room(4),

time: 120 us -> 117 us (0.975)
  waiting for transfers between devices: 18.1 us -> 13.7 us
  blocking collectives: 79.5 us -> 81.8 us
  local copies, waits for them, and re-layouts: 2.82 us -> 0.84 us
    ppermute x2, waiting for transfers between devices: 7.03 us -> 2.58 us  [the longest x1 1.71 us: together(): first = lax.ppermute(first, TM, ups[0] + downs[1])]
    ppermute x2, starting transfers between devices: 2.58 us -> 5.28 us  [the longest x1 4 us: together(): second = lax.ppermute(second, TM, downs[0] + ups[1])]
    all_to_all x4, blocking collectives: 79.5 us -> 81.8 us  [exchanged(): return lax.all_to_all(blocks, axes, split_axis=0, concat_axis=0, tiled=True)]
    all_to_all x1, starting transfers between devices: 6.24 us -> 4.51 us  [exchanged(): return lax.all_to_all(blocks, axes, split_axis=0, concat_axis=0, tiled=True)]
    unnamed x10 -> x6, local copies, waits for them, and re-layouts: 1.7 us -> 0.01 us
where the time goes in v4:
time: 117 us
  blocking collectives  81.8 us (70%)
  waiting for transfers between devices  13.7 us (12%)
  starting transfers between devices  11.1 us (9%)
  Pallas kernels  9.04 us (8%)
    all_to_all x4, blocking collectives, exchanged(): return lax.all_to_all(blocks, axes, split_axis=0, concat_axis=0, tiled=True)  81.8 us
    all_to_all x1, waiting for transfers between devices, exchanged(): return lax.all_to_all(blocks, axes, split_axis=0, concat_axis=0, tiled=True)  11.1 us
    pallas_call x1, Pallas kernels, together(): pl.pallas_call(basis_kernel, out_shape=(f32(STEPS - 1, 2, 2, 16, 2, 8, 12...  5.53 us
    all_to_all x1, starting transfers between devices, exchanged(): return lax.all_to_all(blocks, axes, split_axis=0, concat_axis=0, tiled=True)  4.51 us
    ppermute x1, starting transfers between devices, together(): second = lax.ppermute(second, TM, downs[0] + ups[1])  4 us
  transfers between devices with their start and end apart: 4, of which 3 were waited for; matrix products, arithmetic and copies ran while one was open for 0% of the time, Pallas kernels for 0%

profile of v4, /device:TPU:1, one launch (start us, length us, event | category | flops | bytes accessed | tf_op | source)
XLA Modules:
  0.0 116.6 jit_solution(11395615588394721287)
XLA Ops:
  0.0 1.2 bands.1
  1.2 27.0 %all_to_all.95 = f32[16,4,2,8,128]{4,3,2,1,0:T(8,128)S(1)} all-to-all(f32[16,4,2,8,128]{4,3,2,1,0:T(8,128)S(1)} %get-tuple-element.169), channel_id=1, replica_groups=mesh['z'=8,'core'=2,'y'=4,'x'=4] {'z','core'}, dimensions={0} | all-to-all | bytes 1048576 | tf_op jit(solution)/shard_map/all_to_all | solution.py:514
  28.1 0.0 copy-start
  28.1 0.2 forward.1
  28.4 20.7 %all_to_all.96 = f32[32,6,8,128]{3,2,1,0:T(8,128)S(1)} all-to-all(f32[32,6,8,128]{3,2,1,0:T(8,128)S(1)} %forward.1), channel_id=1, replica_groups=mesh['z'=8,'core'=2,'y'=4,'x'=4] {'core','y','x'}, dimensions={0} | all-to-all | bytes 1572864 | tf_op jit(solution)/shard_map/all_to_all | solution.py:514
  49.0 0.1 edges.1
  49.1 1.3 %collective-permute-start.4 = (f32[2,16,2,8,128]{4,3,2,1,0:T(8,128)S(1)}, f32[2,16,2,8,128]{4,3,2,1,0:T(8,128)S(1)}, u32[]{:S(2)}, u32[]{:S(2)}) collective-permute-start(f32[2,16,2,8,128]{4,3,2,1,0:T(8,128)S(1)} %get-tuple-element.173), channel_id=1, source_target_pairs={{0,16},{16,0},{1,17},{17,1},{2,18},{18,2},{3,19},{19,3},{4,20},{20... | collective-permute-start | bytes 786440 | tf_op jit(solution)/shard_map/ppermute | solution.py:569
  50.5 1.3 %collective-permute-start.2 = (f32[16,24,128]{2,1,0:T(8,128)S(1)}, f32[16,24,128]{2,1,0:T(8,128)S(1)}, u32[]{:S(2)}, u32[]{:S(2)}) collective-permute-start(f32[16,24,128]{2,1,0:T(8,128)S(1)} %get-tuple-element.171), channel_id=1, source_target_pairs={{0,32},{32,64},{64,96},{96,128},{128,160},{160,192},{192,224},{48,... | collective-permute-start | bytes 589832 | tf_op jit(solution)/shard_map/ppermute | solution.py:570
  51.7 4.0 %collective-permute-start.3 = (f32[16,24,128]{2,1,0:T(8,128)S(1)}, f32[16,24,128]{2,1,0:T(8,128)S(1)}, u32[]{:S(2)}, u32[]{:S(2)}) collective-permute-start(f32[16,24,128]{2,1,0:T(8,128)S(1)} %get-tuple-element.172), channel_id=1, source_target_pairs={{32,0},{64,32},{96,64},{128,96},{160,128},{192,160},{224,192},{16,... | collective-permute-start | bytes 589832 | tf_op jit(solution)/shard_map/ppermute | solution.py:571
  55.7 1.7 %collective-permute-done.2.first_ref = f32[16,24,128]{2,1,0:T(8,128)S(1)} collective-permute-done((f32[16,24,128]{2,1,0:T(8,128)S(1)}, f32[16,24,128]{2,1,0:T(8,128)S(1)}, u32[]{:S(2)}, u32[]{:S(2)}) %collective-permute-start.2) | collective-permute-done | bytes 196640 | tf_op jit(solution)/shard_map/ppermute | solution.py:570
  57.5 0.9 collective-permute-done.3.second_ref
  58.3 0.0 collective-permute-done.4.swap_ref
  58.3 5.5 %basis.1 = (f32[5,2,2,16,2,8,128]{6,5,4,3,2,1,0:T(8,128)S(1)}, f32[3,2,16,2,8,128]{5,4,3,2,1,0:T(8,128)S(1)}, f32[8,8,128]{2,1,0:T(8,128)S(1)}) custom-call(f32[2,16,6,8,128]{4,3,2,1,0:T(8,128)S(1)} %bitcast.87, f32[16,24,128]{2,1,0:T(8,128)S(1)} %collective-permute-done.2.first_ref, f32[16,24,128]{2,1,0:T(8,128)S(1)} %collective-permute-done.3.second_ref, ...), custom_call_target="tpu_custom_call" | custom-call | tf_op jit(solution)/shard_map/basis/pallas_call | solution.py:572
  63.9 13.4 %all_to_all.97.part_ref = f32[8,8,128]{2,1,0:T(8,128)S(1)} all-to-all(f32[8,8,128]{2,1,0:T(8,128)S(1)} %get-tuple-element.174), channel_id=1, replica_groups=mesh['z'=8,'core'=2,'y'=4,'x'=4] {'z'}, dimensions={0} | all-to-all | bytes 65536 | tf_op jit(solution)/shard_map/all_to_all | solution.py:514
  77.2 0.0 copy-done
  77.2 0.0 copy-start.1
  77.2 0.0 copy-start.2
  77.2 1.7 %combine.1 = f32[2,16,2,2,8,128]{5,4,3,2,1,0:T(8,128)} custom-call(s32[1,64]{1,0:T(1,128)S(1)} %bitcast.85, f32[8,8,128]{2,1,0:T(8,128)S(1)} %all_to_all.97.part_ref, f32[2,16,6,8,128]{4,3,2,1,0:T(8,128)S(1)} %bitcast.88, f32[5,2,2,16,2,8,128]{6,5,4,3,2,1,0:T(8,128)S(1)} %get-tuple-element.175.v_ref, f32[3,2,16,2,8,128]{5,4,3,2,1,0:T(8,128)S(1)} %get-tuple-element.176.inv_ref), custom_call_target="tpu_custom_call" | custom-call | tf_op jit(solution)/shard_map/combine/pallas_call | solution.py:586
  79.0 4.5 %all-to-all-start.9 = ((f32[32,2,2,8,128]{4,3,2,1,0:T(8,128)}), f32[32,2,2,8,128]{4,3,2,1,0:T(8,128)S(1)}, u32[]{:S(2)}, u32[]{:S(2)}) async-start(f32[32,2,2,8,128]{4,3,2,1,0:T(8,128)} %bitcast.35), calls=%async_computation.9 | async-start | bytes 1048576 | tf_op jit(solution)/shard_map/all_to_all | solution.py:514
  83.5 11.1 %all-to-all-done.9.s_ref = f32[32,2,2,8,128]{4,3,2,1,0:T(8,128)S(1)} async-done(((f32[32,2,2,8,128]{4,3,2,1,0:T(8,128)}), f32[32,2,2,8,128]{4,3,2,1,0:T(8,128)S(1)}, u32[]{:S(2)}, u32[]{:S(2)}) %all-to-all-start.9) | async-done | bytes 524320 | tf_op jit(solution)/shard_map/all_to_all | solution.py:514
  94.6 0.3 inverse.1
  94.9 0.0 copy-done.1
  95.0 0.0 copy-done.2
  95.0 21.7 %conditional.1 = (f32[4,2,128,128]{3,2,1,0:T(8,128)}) conditional(s32[]{:T(128)} %bitcast.36, f32[64,2,8,128]{3,2,1,0:T(8,128)S(1)} %get-tuple-element.178, (f32[4,2,128,128]{3,2,1,0:T(8,128)S(1)}, s32[64]{0:T(128)S(1)}, f32[2,128,128]{2,1,0:T(8,128)S(1)}) %tuple.78), branch_computations={%region_0.0_spmd, %region_1.9_spmd} | conditional | flops 413107744 | bytes 58483476 | solution.py:613
  95.0 20.8 %all_to_all.92 = f32[16,4,2,8,128]{4,3,2,1,0:T(8,128)S(1)} all-to-all(f32[16,4,2,8,128]{4,3,2,1,0:T(8,128)S(1)} %bitcast.90), channel_id=1, replica_groups=mesh['z'=8,'core'=2,'y'=4,'x'=4] {'z','core'}, dimensions={0} | all-to-all | bytes 1048576 | tf_op jit(solution)/shard_map/cond/branch_0_fun/all_to_all | solution.py:514
  115.8 0.8 copy.89
Async XLA Ops:
  28.1 49.1 %copy-start = (s32[64]{0:T(128)S(1)}, s32[64]{0:T(128)}, u32[]{:S(2)}) copy-start(s32[64]{0:T(128)} %param.9) | copy-start | bytes 772
  49.1 9.2 %collective-permute-start.4 = (f32[2,16,2,8,128]{4,3,2,1,0:T(8,128)S(1)}, f32[2,16,2,8,128]{4,3,2,1,0:T(8,128)S(1)}, u32[]{:S(2)}, u32[]{:S(2)}) collective-permute-start(f32[2,16,2,8,128]{4,3,2,1,0:T(8,128)S(1)} %get-tuple-element.173), channel_id=1, source_target_pairs={{0,16},{16,0},{1,17},{17,1},{2,18},{18,2},{3,19},{19,3},{4,20},{20... | collective-permute-start | bytes 786440 | tf_op jit(solution)/shard_map/ppermute | solution.py:569
  50.5 7.0 %collective-permute-start.2 = (f32[16,24,128]{2,1,0:T(8,128)S(1)}, f32[16,24,128]{2,1,0:T(8,128)S(1)}, u32[]{:S(2)}, u32[]{:S(2)}) collective-permute-start(f32[16,24,128]{2,1,0:T(8,128)S(1)} %get-tuple-element.171), channel_id=1, source_target_pairs={{0,32},{32,64},{64,96},{96,128},{128,160},{160,192},{192,224},{48,... | collective-permute-start | bytes 589832 | tf_op jit(solution)/shard_map/ppermute | solution.py:570
  51.7 6.6 %collective-permute-start.3 = (f32[16,24,128]{2,1,0:T(8,128)S(1)}, f32[16,24,128]{2,1,0:T(8,128)S(1)}, u32[]{:S(2)}, u32[]{:S(2)}) collective-permute-start(f32[16,24,128]{2,1,0:T(8,128)S(1)} %get-tuple-element.172), channel_id=1, source_target_pairs={{32,0},{64,32},{96,64},{128,96},{160,128},{192,160},{224,192},{16,... | collective-permute-start | bytes 589832 | tf_op jit(solution)/shard_map/ppermute | solution.py:571
  77.2 17.7 %copy-start.1 = (f32[2,128,128]{2,1,0:T(8,128)S(1)}, f32[2,128,128]{2,1,0:T(8,128)}, u32[]{:S(2)}) copy-start(f32[2,128,128]{2,1,0:T(8,128)} %a_ref.1) | copy-start | bytes 393220
  77.2 17.7 %copy-start.2 = (f32[4,2,128,128]{3,2,1,0:T(8,128)S(1)}, f32[4,2,128,128]{3,2,1,0:T(8,128)}, u32[]{:S(2)}) copy-start(f32[4,2,128,128]{3,2,1,0:T(8,128)} %x_ref.1) | copy-start | bytes 1572868
  79.0 15.6 %all-to-all-start.9 = ((f32[32,2,2,8,128]{4,3,2,1,0:T(8,128)}), f32[32,2,2,8,128]{4,3,2,1,0:T(8,128)S(1)}, u32[]{:S(2)}, u32[]{:S(2)}) async-start(f32[32,2,2,8,128]{4,3,2,1,0:T(8,128)} %bitcast.35), calls=%async_computation.9 | async-start | bytes 1048576 | tf_op jit(solution)/shard_map/all_to_all | solution.py:514

commit v5 on v4

--- a/solution.py
+++ b/solution.py
@@ -25,8 +25,8 @@
 highest = lax.Precision.HIGHEST
 decay = wrap_factor ** (1.0 / L)
 
-gram_rounding = 2.5e-7
-error_allowed = 5e-4
+gram_rounding = 1e-6
+error_allowed = 1.5e-4
 
 
 def with_halo(cells, sides, width):
@@ -421,7 +421,8 @@
     )
     one, none = jnp.ones((8, 128), jnp.float32), jnp.zeros((8, 128), jnp.float32)
     poly, answer = [(one, none)], [(none, none) for _ in range(STEPS)]
-    bound, doubt, scale = gram_rounding * gram[0, 0][0], none, None
+    sizes = [jnp.sqrt(jnp.maximum(gram[i, i][0], 0.0)) for i in range(STEPS + 1)]
+    doubt, scale = none, None
     for m in range(STEPS):
         in_a, in_b = (jnp.broadcast_to(jnp.where(m < count, 1.0, 0.0), (8, 128)) for count in (count_a, count_b))
         weight = jnp.where(ends, jnp.where(low, in_a, in_b), in_a + in_b)
@@ -433,7 +434,8 @@
         length = jnp.sqrt(jnp.maximum(g00, 0.0))
         if m == 0:
             scale = size * length
-        step_doubt = bound * (2.0 + 4.0 * size) * jnp.abs(inverse) * length
+        pair = sizes[0] + sizes[1]
+        step_doubt = (gram_rounding * (1 + m / 2)) * pair * (sizes[0] + size * pair) * jnp.abs(inverse) * length
         doubt = doubt + jnp.where(weight > 0.0, step_doubt, none)
         for j, p in enumerate(poly):
             term = multiplied(coef, p)
@@ -453,7 +455,7 @@
         rc = multiplied((rest[0], -rest[1]), coef)
         cr = (rc[0], -rc[1])
         size_rest = jnp.abs(rest[0]) + jnp.abs(rest[1])
-        bound = bound * (size + size_rest) * (size + size_rest)
+        sizes = [size_rest * a + size * b for a, b in zip(sizes[:-1], sizes[1:])]
 
         def at(i, j):
             return gram[i, j] if i <= j else (gram[j, i][0], -gram[j, i][1])
@@ -493,8 +495,8 @@
                     ims.append(wb * im + wi * re)
                 re, im = tree_sum(res), tree_sum(ims)
                 a, b, c = (inv_ref[i, side, sp, zz] for i in range(3))
-                out_ref[side, sp, 0, zz] = a * re - c * im
-                out_ref[side, sp, 1, zz] = b * im + c * re
+                out_ref[16 * side + sp, 0, zz] = a * re - c * im
+                out_ref[16 * side + sp, 1, zz] = b * im + c * re
         return 0
 
     lax.fori_loop(0, NZ // 2, finish, 0, unroll=2)
@@ -585,13 +587,13 @@
     partials = exchanged(partial, "z")
     solved = pl.pallas_call(
         combine_kernel,
-        out_shape=f32(2, 16, 2, 2, 8, 128),
+        out_shape=f32(PAIRS, 2, 2, 8, 128),
         in_specs=[VMEM, VMEM, VMEM, VMEM, VMEM],
         out_specs=VMEM,
         compiler_params=room(6),
         name="combine",
     )(held(counts.reshape(1, L)), held(partials), own, held(basis), held(inverses))
-    gathered = exchanged(solved.reshape(32, 2, 2, 8, 128), SLOTS)
+    gathered = exchanged(solved, SLOTS)
     values, failed = pl.pallas_call(
         inverse_kernel,
         out_shape=(f32(L, 2, 8, 128), pltpu.SMEM((1,), jnp.int32)),
@@ -603,6 +605,27 @@
     return values, failed
 
 
+def taken_kernel(*refs):
+    count = len(refs) // 2
+    copies = [pltpu.make_async_copy(refs[i], refs[count + i], refs[-1].at[i]) for i in range(count)]
+    for copy in copies:
+        copy.start()
+    for copy in copies:
+        copy.wait()
+
+
+def taken(*arrays):
+    return pl.pallas_call(
+        taken_kernel,
+        out_shape=tuple(f32(*a.shape) for a in arrays),
+        in_specs=[ANY] * len(arrays),
+        out_specs=(VMEM,) * len(arrays),
+        scratch_shapes=[pltpu.SemaphoreType.DMA((len(arrays),))],
+        compiler_params=room(2),
+        name="taken",
+    )(*(in_hbm(a) for a in arrays))
+
+
 def to_steps(values, shape):
     bands = exchanged(values.reshape(16, 4, 2, 8, 128), TM)
     return bands.transpose(1, 2, 0, 3, 4).reshape(shape)
@@ -612,7 +635,7 @@
     values, failed = together(residual, absorption, counts)
     return lax.cond(
         failed[0] > 0,
-        lambda r, a, c, v: stepwise(r, a, c),
+        lambda r, a, c, v: stepwise(*taken(r, a), c),
         lambda r, a, c, v: to_steps(v, r.shape),
         residual, absorption, counts, values,
     )

time: 117 us -> 117 us (level)
  no operation moved by 1% of the time
where the time goes in v5:
time: 117 us
  blocking collectives  81.8 us (70%)
  waiting for transfers between devices  13.7 us (12%)
  starting transfers between devices  11.1 us (9%)
  Pallas kernels  8.92 us (8%)
    all_to_all x4, blocking collectives, exchanged(): return lax.all_to_all(blocks, axes, split_axis=0, concat_axis=0, tiled=True)  81.8 us
    all_to_all x1, waiting for transfers between devices, exchanged(): return lax.all_to_all(blocks, axes, split_axis=0, concat_axis=0, tiled=True)  11.1 us
    pallas_call x1, Pallas kernels, together(): pl.pallas_call(basis_kernel, out_shape=(f32(STEPS - 1, 2, 2, 16, 2, 8, 12...  5.43 us
    all_to_all x1, starting transfers between devices, exchanged(): return lax.all_to_all(blocks, axes, split_axis=0, concat_axis=0, tiled=True)  4.5 us
    ppermute x1, starting transfers between devices, together(): second = lax.ppermute(second, TM, downs[0] + ups[1])  4 us
  transfers between devices with their start and end apart: 4, of which 3 were waited for; matrix products, arithmetic and copies ran while one was open for 0% of the time, Pallas kernels for 0%

profile of v5, /device:TPU:1, one launch (start us, length us, event | category | flops | bytes accessed | tf_op | source)
XLA Modules:
  0.0 116.7 jit_solution(11974776053453784889)
XLA Ops:
  0.0 1.2 bands.1
  1.2 27.0 %all_to_all.95 = f32[16,4,2,8,128]{4,3,2,1,0:T(8,128)S(1)} all-to-all(f32[16,4,2,8,128]{4,3,2,1,0:T(8,128)S(1)} %get-tuple-element.171), channel_id=1, replica_groups=mesh['z'=8,'core'=2,'y'=4,'x'=4] {'z','core'}, dimensions={0} | all-to-all | bytes 1048576 | tf_op jit(solution)/shard_map/all_to_all | solution.py:516
  28.1 0.0 copy-start
  28.1 0.2 forward.1
  28.4 20.7 %all_to_all.96 = f32[32,6,8,128]{3,2,1,0:T(8,128)S(1)} all-to-all(f32[32,6,8,128]{3,2,1,0:T(8,128)S(1)} %forward.1), channel_id=1, replica_groups=mesh['z'=8,'core'=2,'y'=4,'x'=4] {'core','y','x'}, dimensions={0} | all-to-all | bytes 1572864 | tf_op jit(solution)/shard_map/all_to_all | solution.py:516
  49.0 0.1 edges.1
  49.1 1.3 %collective-permute-start.4 = (f32[2,16,2,8,128]{4,3,2,1,0:T(8,128)S(1)}, f32[2,16,2,8,128]{4,3,2,1,0:T(8,128)S(1)}, u32[]{:S(2)}, u32[]{:S(2)}) collective-permute-start(f32[2,16,2,8,128]{4,3,2,1,0:T(8,128)S(1)} %get-tuple-element.175), channel_id=1, source_target_pairs={{0,16},{16,0},{1,17},{17,1},{2,18},{18,2},{3,19},{19,3},{4,20},{20... | collective-permute-start | bytes 786440 | tf_op jit(solution)/shard_map/ppermute | solution.py:571
  50.5 1.3 %collective-permute-start.2 = (f32[16,24,128]{2,1,0:T(8,128)S(1)}, f32[16,24,128]{2,1,0:T(8,128)S(1)}, u32[]{:S(2)}, u32[]{:S(2)}) collective-permute-start(f32[16,24,128]{2,1,0:T(8,128)S(1)} %get-tuple-element.173), channel_id=1, source_target_pairs={{0,32},{32,64},{64,96},{96,128},{128,160},{160,192},{192,224},{48,... | collective-permute-start | bytes 589832 | tf_op jit(solution)/shard_map/ppermute | solution.py:572
  51.7 4.0 %collective-permute-start.3 = (f32[16,24,128]{2,1,0:T(8,128)S(1)}, f32[16,24,128]{2,1,0:T(8,128)S(1)}, u32[]{:S(2)}, u32[]{:S(2)}) collective-permute-start(f32[16,24,128]{2,1,0:T(8,128)S(1)} %get-tuple-element.174), channel_id=1, source_target_pairs={{32,0},{64,32},{96,64},{128,96},{160,128},{192,160},{224,192},{16,... | collective-permute-start | bytes 589832 | tf_op jit(solution)/shard_map/ppermute | solution.py:573
  55.7 1.7 %collective-permute-done.2.first_ref = f32[16,24,128]{2,1,0:T(8,128)S(1)} collective-permute-done((f32[16,24,128]{2,1,0:T(8,128)S(1)}, f32[16,24,128]{2,1,0:T(8,128)S(1)}, u32[]{:S(2)}, u32[]{:S(2)}) %collective-permute-start.2) | collective-permute-done | bytes 196640 | tf_op jit(solution)/shard_map/ppermute | solution.py:572
  57.5 0.9 collective-permute-done.3.second_ref
  58.3 0.0 collective-permute-done.4.swap_ref
  58.3 5.4 %basis.1 = (f32[5,2,2,16,2,8,128]{6,5,4,3,2,1,0:T(8,128)S(1)}, f32[3,2,16,2,8,128]{5,4,3,2,1,0:T(8,128)S(1)}, f32[8,8,128]{2,1,0:T(8,128)S(1)}) custom-call(f32[2,16,6,8,128]{4,3,2,1,0:T(8,128)S(1)} %bitcast.86, f32[16,24,128]{2,1,0:T(8,128)S(1)} %collective-permute-done.2.first_ref, f32[16,24,128]{2,1,0:T(8,128)S(1)} %collective-permute-done.3.second_ref, ...), custom_call_target="tpu_custom_call" | custom-call | tf_op jit(solution)/shard_map/basis/pallas_call | solution.py:574
  63.8 13.4 %all_to_all.97.part_ref = f32[8,8,128]{2,1,0:T(8,128)S(1)} all-to-all(f32[8,8,128]{2,1,0:T(8,128)S(1)} %get-tuple-element.176), channel_id=1, replica_groups=mesh['z'=8,'core'=2,'y'=4,'x'=4] {'z'}, dimensions={0} | all-to-all | bytes 65536 | tf_op jit(solution)/shard_map/all_to_all | solution.py:516
  77.1 0.0 copy-done
  77.1 1.7 %combine.1 = f32[32,2,2,8,128]{4,3,2,1,0:T(8,128)} custom-call(s32[1,64]{1,0:T(1,128)S(1)} %bitcast.84, f32[8,8,128]{2,1,0:T(8,128)S(1)} %all_to_all.97.part_ref, f32[2,16,6,8,128]{4,3,2,1,0:T(8,128)S(1)} %bitcast.87, f32[5,2,2,16,2,8,128]{6,5,4,3,2,1,0:T(8,128)S(1)} %get-tuple-element.177.v_ref, f32[3,2,16,2,8,128]{5,4,3,2,1,0:T(8,128)S(1)} %get-tuple-element.178.inv_ref), custom_call_target="tpu_custom_call" | custom-call | tf_op jit(solution)/shard_map/combine/pallas_call | solution.py:588
  78.8 4.5 %all-to-all-start.9 = ((f32[32,2,2,8,128]{4,3,2,1,0:T(8,128)}), f32[32,2,2,8,128]{4,3,2,1,0:T(8,128)S(1)}, u32[]{:S(2)}, u32[]{:S(2)}) async-start(f32[32,2,2,8,128]{4,3,2,1,0:T(8,128)} %combine.1), calls=%async_computation.9 | async-start | bytes 1048576 | tf_op jit(solution)/shard_map/all_to_all | solution.py:516
  83.3 11.1 %all-to-all-done.9.s_ref = f32[32,2,2,8,128]{4,3,2,1,0:T(8,128)S(1)} async-done(((f32[32,2,2,8,128]{4,3,2,1,0:T(8,128)}), f32[32,2,2,8,128]{4,3,2,1,0:T(8,128)S(1)}, u32[]{:S(2)}, u32[]{:S(2)}) %all-to-all-start.9) | async-done | bytes 524320 | tf_op jit(solution)/shard_map/all_to_all | solution.py:516
  94.5 0.3 inverse.1
  94.8 21.1 %conditional.1 = (f32[4,2,128,128]{3,2,1,0:T(8,128)S(1)}) conditional(s32[]{:T(128)} %bitcast.35, f32[64,2,8,128]{3,2,1,0:T(8,128)S(1)} %get-tuple-element.180, (f32[4,2,128,128]{3,2,1,0:T(8,128)}, f32[2,128,128]{2,1,0:T(8,128)}, s32[64]{0:T(128)S(1)}) %tuple.70), branch_computations={%region_0.0_spmd, %region_1.9_spmd} | conditional | flops 413107744 | bytes 59532052 | solution.py:636
  94.8 20.8 %all_to_all.92 = f32[16,4,2,8,128]{4,3,2,1,0:T(8,128)S(1)} all-to-all(f32[16,4,2,8,128]{4,3,2,1,0:T(8,128)S(1)} %bitcast.89), channel_id=1, replica_groups=mesh['z'=8,'core'=2,'y'=4,'x'=4] {'z','core'}, dimensions={0} | all-to-all | bytes 1048576 | tf_op jit(solution)/shard_map/cond/branch_0_fun/all_to_all | solution.py:516
  115.9 0.0 copy-start.1
  116.0 0.8 copy-done.1
  (1 shorter events, 0.0 us)
Async XLA Ops:
  28.1 49.0 %copy-start = (s32[64]{0:T(128)S(1)}, s32[64]{0:T(128)}, u32[]{:S(2)}) copy-start(s32[64]{0:T(128)} %param.9) | copy-start | bytes 772
  49.1 9.2 %collective-permute-start.4 = (f32[2,16,2,8,128]{4,3,2,1,0:T(8,128)S(1)}, f32[2,16,2,8,128]{4,3,2,1,0:T(8,128)S(1)}, u32[]{:S(2)}, u32[]{:S(2)}) collective-permute-start(f32[2,16,2,8,128]{4,3,2,1,0:T(8,128)S(1)} %get-tuple-element.175), channel_id=1, source_target_pairs={{0,16},{16,0},{1,17},{17,1},{2,18},{18,2},{3,19},{19,3},{4,20},{20... | collective-permute-start | bytes 786440 | tf_op jit(solution)/shard_map/ppermute | solution.py:571
  50.5 7.0 %collective-permute-start.2 = (f32[16,24,128]{2,1,0:T(8,128)S(1)}, f32[16,24,128]{2,1,0:T(8,128)S(1)}, u32[]{:S(2)}, u32[]{:S(2)}) collective-permute-start(f32[16,24,128]{2,1,0:T(8,128)S(1)} %get-tuple-element.173), channel_id=1, source_target_pairs={{0,32},{32,64},{64,96},{96,128},{128,160},{160,192},{192,224},{48,... | collective-permute-start | bytes 589832 | tf_op jit(solution)/shard_map/ppermute | solution.py:572
  51.7 6.6 %collective-permute-start.3 = (f32[16,24,128]{2,1,0:T(8,128)S(1)}, f32[16,24,128]{2,1,0:T(8,128)S(1)}, u32[]{:S(2)}, u32[]{:S(2)}) collective-permute-start(f32[16,24,128]{2,1,0:T(8,128)S(1)} %get-tuple-element.174), channel_id=1, source_target_pairs={{32,0},{64,32},{96,64},{128,96},{160,128},{192,160},{224,192},{16,... | collective-permute-start | bytes 589832 | tf_op jit(solution)/shard_map/ppermute | solution.py:573
  78.8 15.6 %all-to-all-start.9 = ((f32[32,2,2,8,128]{4,3,2,1,0:T(8,128)}), f32[32,2,2,8,128]{4,3,2,1,0:T(8,128)S(1)}, u32[]{:S(2)}, u32[]{:S(2)}) async-start(f32[32,2,2,8,128]{4,3,2,1,0:T(8,128)} %combine.1), calls=%async_computation.9 | async-start | bytes 1048576 | tf_op jit(solution)/shard_map/all_to_all | solution.py:516
  115.9 0.8 copy-start.1

commit v6 on v5

--- a/solution.py
+++ b/solution.py
@@ -216,12 +216,7 @@
         copy.wait()
 
 
-def forward_kernel(x_ref, rows_ref, out_ref):
-    for core in range(2):
-        for zz in range(2):
-            rows = rows_ref[core, zz]
-            for slot in range(16 * core, 16 * core + 16):
-                out_ref[slot, 4 + zz] = rows
+def forward_kernel(x_ref, out_ref):
     for zz in range(2):
         spectrum = real_transform([x_ref[n, zz] * decay**n for n in range(L)])
         out_ref[0, zz] = spectrum[0][0]
@@ -265,20 +260,18 @@
     return found
 
 
-def edges_kernel(own_ref, first_ref, second_ref, abs_ref):
+def edges_kernel(own_ref, first_ref, second_ref):
     low = lax.axis_index("core") == 0
     for sp in range(16):
         for i in range(4):
             up, down = own_ref[1, sp, i, pl.ds(8 - HALO, HALO), :], own_ref[0, sp, i, pl.ds(0, HALO), :]
             first_ref[sp, pl.ds(HALO * i, HALO), :] = jnp.where(low, up, down)
             second_ref[sp, pl.ds(HALO * i, HALO), :] = jnp.where(low, down, up)
-        for side in range(2):
-            for zz in range(2):
-                abs_ref[side, sp, zz] = own_ref[side, sp, 4 + zz]
-
-
-def basis_kernel(own_ref, first_ref, second_ref, swap_ref, v_ref, inv_ref, gram_ref, u, edge_inv, sums):
+
+
+def basis_kernel(own_ref, first_ref, second_ref, abs_ref, swap_ref, v_ref, inv_ref, gram_ref, u, edge_inv, sums):
     slot, z, core = lax.axis_index(SLOTS), lax.axis_index("z"), lax.axis_index("core")
+    home = lax.axis_index(SPACE)
     shifts_here = slot_shifts()
     shift_a, shift_b, shift_im = (pick(slot, shifts_here[:, i]) for i in range(3))
     lanes = lax.broadcasted_iota(jnp.int32, (8, 128), 1)
@@ -304,8 +297,8 @@
                     u[turn, part, 2 * sp + zz + 1, pl.ds(40, 8), :] = blank
         for tile in range(4):
             for zz in range(2):
-                mine, other = own_ref[tile // 2, sp, 4 + zz], swap_ref[tile // 2, sp, zz]
-                base = jnp.where(core == tile % 2, mine, other)
+                mine, other = (ref[sp ^ home, tile % 2, zz] for ref in (abs_ref, swap_ref))
+                base = jnp.where(core == tile // 2, mine, other)
                 da, db = (shift_a + 6.0) + base, (shift_b + 6.0) + base
                 ra, rb = 1.0 / (da * da + shift_im * shift_im), 1.0 / (db * db + shift_im * shift_im)
                 found = [da * ra, db * rb, -shift_im * ra]
@@ -549,32 +542,37 @@
         name="bands",
     )(in_hbm(residual), in_hbm(absorption))
     series = exchanged(bands, TM).reshape(L, 2, 8, 128)
+    rows = rows[None]
+    for axis in ("x", "y"):
+        for bit in (1, 2):
+            near = lax.ppermute(rows, axis, [(i, i ^ bit) for i in range(lax.axis_size(axis))])
+            rows = jnp.concatenate([rows, near])
+    swap = lax.ppermute(rows, "core", [(0, 1), (1, 0)])
     spectrum = pl.pallas_call(
         forward_kernel,
-        out_shape=f32(PAIRS, 6, 8, 128),
-        in_specs=[VMEM, VMEM],
+        out_shape=f32(PAIRS, 4, 8, 128),
+        in_specs=[VMEM],
         out_specs=VMEM,
         compiler_params=room(4),
         name="forward",
-    )(held(series), held(rows))
-    own = held(exchanged(spectrum, SLOTS).reshape(2, 16, 6, 8, 128))
-    first, second, swap = pl.pallas_call(
+    )(held(series))
+    own = held(exchanged(spectrum, SLOTS).reshape(2, 16, 4, 8, 128))
+    first, second = pl.pallas_call(
         edges_kernel,
-        out_shape=(f32(16, 4 * HALO, 128), f32(16, 4 * HALO, 128), f32(2, 16, 2, 8, 128)),
+        out_shape=(f32(16, 4 * HALO, 128), f32(16, 4 * HALO, 128)),
         in_specs=[VMEM],
-        out_specs=(VMEM, VMEM, VMEM),
+        out_specs=(VMEM, VMEM),
         compiler_params=room(2),
         name="edges",
     )(own)
     ups = [[(2 * i + core, 2 * i + 2 + core) for i in range(chips - 1)] for core in range(2)]
     downs = [[(b, a) for a, b in pairs] for pairs in ups]
-    swap = lax.ppermute(swap, "core", [(0, 1), (1, 0)])
     first = lax.ppermute(first, TM, ups[0] + downs[1])
     second = lax.ppermute(second, TM, downs[0] + ups[1])
     basis, inverses, partial = pl.pallas_call(
         basis_kernel,
         out_shape=(f32(STEPS - 1, 2, 2, 16, 2, 8, 128), f32(3, 2, 16, 2, 8, 128), f32(8, 8, 128)),
-        in_specs=[VMEM, VMEM, VMEM, VMEM],
+        in_specs=[VMEM, VMEM, VMEM, VMEM, VMEM],
         out_specs=(VMEM, VMEM, VMEM),
         scratch_shapes=[
             pltpu.VMEM((2, 2, NZ + 2, 48, 128), jnp.float32),
@@ -583,7 +581,7 @@
         ],
         compiler_params=room(10),
         name="basis",
-    )(own, held(first), held(second), held(swap))
+    )(own, held(first), held(second), held(rows), held(swap))
     partials = exchanged(partial, "z")
     solved = pl.pallas_call(
         combine_kernel,

time: 117 us -> 119 us (1.017)
  blocking collectives: 81.8 us -> 34.2 us
  starting transfers between devices: 11.1 us -> 37.7 us
  waiting for transfers between devices: 13.7 us -> 34.7 us
  Pallas kernels: 8.92 us -> 10.9 us
    all_to_all x4 -> x2, blocking collectives: 81.8 us -> 34.2 us  [exchanged(): return lax.all_to_all(blocks, axes, split_axis=0, concat_axis=0, tiled=True)]
    all_to_all x1 -> x3, starting transfers between devices: 4.5 us -> 23 us  [exchanged(): return lax.all_to_all(blocks, axes, split_axis=0, concat_axis=0, tiled=True)]
    ppermute x1 -> x5, waiting for transfers between devices: 0.01 us -> 12.1 us  [the longest x4 12.1 us: together(): lax.ppermute(rows, axis, [(i, i ^ bit) for i in range(lax.axis_size(axis))])]
    all_to_all x1 -> x3, waiting for transfers between devices: 11.1 us -> 20 us  [exchanged(): return lax.all_to_all(blocks, axes, split_axis=0, concat_axis=0, tiled=True)]
    ppermute x1 -> x5, starting transfers between devices: 1.35 us -> 9.34 us  [the longest x4 8.32 us: together(): lax.ppermute(rows, axis, [(i, i ^ bit) for i in range(lax.axis_size(axis))])]
  transfers between devices with their start and end apart: 4 -> 10, of which waited for: 3 -> 7; matrix products, arithmetic and copies ran while one was open for 0% -> 0% of each run, Pallas kernels for 0% -> 1%
where the time goes in v6:
time: 119 us
  starting transfers between devices  37.7 us (32%)
  waiting for transfers between devices  34.7 us (29%)
  blocking collectives  34.2 us (29%)
  Pallas kernels  10.9 us (9%)
    all_to_all x2, blocking collectives, exchanged(): return lax.all_to_all(blocks, axes, split_axis=0, concat_axis=0, tiled=True)  34.2 us
    all_to_all x3, starting transfers between devices, exchanged(): return lax.all_to_all(blocks, axes, split_axis=0, concat_axis=0, tiled=True)  23 us
    all_to_all x3, waiting for transfers between devices, exchanged(): return lax.all_to_all(blocks, axes, split_axis=0, concat_axis=0, tiled=True)  20 us
    ppermute x4, waiting for transfers between devices, together(): lax.ppermute(rows, axis, [(i, i ^ bit) for i in range(lax.axis_size(axis))])  12.1 us
    ppermute x4, starting transfers between devices, together(): lax.ppermute(rows, axis, [(i, i ^ bit) for i in range(lax.axis_size(axis))])  8.32 us
    pallas_call x1, Pallas kernels, together(): pl.pallas_call(basis_kernel, out_shape=(f32(STEPS - 1, 2, 2, 16, 2, 8, 12...  5.81 us
    ppermute x1, starting transfers between devices, together(): second = lax.ppermute(second, TM, downs[0] + ups[1])  4 us
  transfers between devices with their start and end apart: 10, of which 7 were waited for; matrix products, arithmetic and copies ran while one was open for 0% of the time, Pallas kernels for 1%

profile of v6, /device:TPU:1, one launch (start us, length us, event | category | flops | bytes accessed | tf_op | source)
XLA Modules:
  0.0 118.6 jit_solution(17380952243695186572)
XLA Ops:
  0.0 2.0 %bands.1 = (f32[16,4,2,8,128]{4,3,2,1,0:T(8,128)}, f32[2,2,8,128]{3,2,1,0:T(8,128)S(1)}) custom-call(f32[4,2,128,128]{3,2,1,0:T(8,128)} %x_ref.1, f32[2,128,128]{2,1,0:T(8,128)} %a_ref.1), custom_call_target="tpu_custom_call" | custom-call | tf_op jit(solution)/shard_map/bands/pallas_call | solution.py:535
  2.0 10.0 %all-to-all-start.6 = ((f32[16,4,2,8,128]{4,3,2,1,0:T(8,128)}), f32[16,4,2,8,128]{4,3,2,1,0:T(8,128)S(1)}, u32[]{:S(2)}, u32[]{:S(2)}) async-start(f32[16,4,2,8,128]{4,3,2,1,0:T(8,128)} %get-tuple-element.170), calls=%async_computation.6 | async-start | bytes 1048576 | tf_op jit(solution)/shard_map/all_to_all | solution.py:509
  11.9 0.0 copy-start
  11.9 1.3 %collective-permute-start.4 = (f32[1,2,2,8,128]{4,3,2,1,0:T(8,128)S(1)}, f32[1,2,2,8,128]{4,3,2,1,0:T(8,128)S(1)}, u32[]{:S(2)}, u32[]{:S(2)}) collective-permute-start(f32[1,2,2,8,128]{4,3,2,1,0:T(8,128)S(1)} %bitcast.92), channel_id=1, source_target_pairs={{0,1},{1,0},{2,3},{3,2},{4,5},{5,4},{6,7},{7,6},{8,9},{9,8},{10,11... | collective-permute-start | bytes 49160 | tf_op jit(solution)/shard_map/ppermute | solution.py:548
  13.2 1.4 %collective-permute-done.4 = f32[1,2,2,8,128]{4,3,2,1,0:T(8,128)S(1)} collective-permute-done((f32[1,2,2,8,128]{4,3,2,1,0:T(8,128)S(1)}, f32[1,2,2,8,128]{4,3,2,1,0:T(8,128)S(1)}, u32[]{:S(2)}, u32[]{:S(2)}) %collective-permute-start.4) | collective-permute-done | bytes 16416 | tf_op jit(solution)/shard_map/ppermute | solution.py:548
  14.6 2.7 %collective-permute-start.5 = (f32[2,2,2,8,128]{4,3,2,1,0:T(8,128)S(1)}, f32[2,2,2,8,128]{4,3,2,1,0:T(8,128)S(1)}, u32[]{:S(2)}, u32[]{:S(2)}) collective-permute-start(f32[2,2,2,8,128]{4,3,2,1,0:T(8,128)S(1)} %pad_maximum_fusion.10), channel_id=1, source_target_pairs={{0,2},{1,3},{2,0},{3,1},{4,6},{5,7},{6,4},{7,5},{8,10},{9,11},{10,... | collective-permute-start | bytes 98312 | tf_op jit(solution)/shard_map/ppermute | solution.py:548
  17.4 1.7 %collective-permute-done.5 = f32[2,2,2,8,128]{4,3,2,1,0:T(8,128)S(1)} collective-permute-done((f32[2,2,2,8,128]{4,3,2,1,0:T(8,128)S(1)}, f32[2,2,2,8,128]{4,3,2,1,0:T(8,128)S(1)}, u32[]{:S(2)}, u32[]{:S(2)}) %collective-permute-start.5) | collective-permute-done | bytes 32800 | tf_op jit(solution)/shard_map/ppermute | solution.py:548
  19.0 1.3 %collective-permute-start.6 = (f32[4,2,2,8,128]{4,3,2,1,0:T(8,128)S(1)}, f32[4,2,2,8,128]{4,3,2,1,0:T(8,128)S(1)}, u32[]{:S(2)}, u32[]{:S(2)}) collective-permute-start(f32[4,2,2,8,128]{4,3,2,1,0:T(8,128)S(1)} %pad_maximum_fusion.9), channel_id=1, source_target_pairs={{0,4},{4,0},{8,12},{12,8},{1,5},{5,1},{9,13},{13,9},{2,6},{6,2},{1... | collective-permute-start | bytes 196616 | tf_op jit(solution)/shard_map/ppermute | solution.py:548
  20.3 8.8 %all-to-all-done.6 = f32[16,4,2,8,128]{4,3,2,1,0:T(8,128)S(1)} async-done(((f32[16,4,2,8,128]{4,3,2,1,0:T(8,128)}), f32[16,4,2,8,128]{4,3,2,1,0:T(8,128)S(1)}, u32[]{:S(2)}, u32[]{:S(2)}) %all-to-all-start.6) | async-done | bytes 524320 | tf_op jit(solution)/shard_map/all_to_all | solution.py:509
  29.1 1.0 forward.1
  30.2 7.2 %all-to-all-start.7 = ((f32[32,4,8,128]{3,2,1,0:T(8,128)}), f32[32,4,8,128]{3,2,1,0:T(8,128)S(1)}, u32[]{:S(2)}, u32[]{:S(2)}) async-start(f32[32,4,8,128]{3,2,1,0:T(8,128)} %forward.1), calls=%async_computation.7 | async-start | bytes 1048576 | tf_op jit(solution)/shard_map/all_to_all | solution.py:509
  37.4 0.0 collective-permute-done.6
  37.4 3.0 %collective-permute-start.7 = (f32[8,2,2,8,128]{4,3,2,1,0:T(8,128)S(1)}, f32[8,2,2,8,128]{4,3,2,1,0:T(8,128)S(1)}, u32[]{:S(2)}, u32[]{:S(2)}) collective-permute-start(f32[8,2,2,8,128]{4,3,2,1,0:T(8,128)S(1)} %pad_maximum_fusion.8), channel_id=1, source_target_pairs={{0,8},{4,12},{8,0},{12,4},{1,9},{5,13},{9,1},{13,5},{2,10},{6,14},... | collective-permute-start | bytes 393224 | tf_op jit(solution)/shard_map/ppermute | solution.py:548
  40.4 9.1 %collective-permute-done.7 = f32[8,2,2,8,128]{4,3,2,1,0:T(8,128)S(1)} collective-permute-done((f32[8,2,2,8,128]{4,3,2,1,0:T(8,128)S(1)}, f32[8,2,2,8,128]{4,3,2,1,0:T(8,128)S(1)}, u32[]{:S(2)}, u32[]{:S(2)}) %collective-permute-start.7) | collective-permute-done | bytes 131104 | tf_op jit(solution)/shard_map/ppermute | solution.py:548
  49.5 1.0 collective-permute-start.8
  50.5 0.0 all-to-all-done.7
  50.6 1.3 %collective-permute-start.2 = (f32[16,24,128]{2,1,0:T(8,128)S(1)}, f32[16,24,128]{2,1,0:T(8,128)S(1)}, u32[]{:S(2)}, u32[]{:S(2)}) collective-permute-start(f32[16,24,128]{2,1,0:T(8,128)S(1)} %get-tuple-element.171), channel_id=1, source_target_pairs={{0,32},{32,64},{64,96},{96,128},{128,160},{160,192},{192,224},{48,... | collective-permute-start | bytes 589832 | tf_op jit(solution)/shard_map/ppermute | solution.py:570
  51.9 4.0 %collective-permute-start.3 = (f32[16,24,128]{2,1,0:T(8,128)S(1)}, f32[16,24,128]{2,1,0:T(8,128)S(1)}, u32[]{:S(2)}, u32[]{:S(2)}) collective-permute-start(f32[16,24,128]{2,1,0:T(8,128)S(1)} %get-tuple-element.172), channel_id=1, source_target_pairs={{32,0},{64,32},{96,64},{128,96},{160,128},{192,160},{224,192},{16,... | collective-permute-start | bytes 589832 | tf_op jit(solution)/shard_map/ppermute | solution.py:571
  55.9 0.0 collective-permute-done.8.swap_ref
  55.9 1.7 %collective-permute-done.2.first_ref = f32[16,24,128]{2,1,0:T(8,128)S(1)} collective-permute-done((f32[16,24,128]{2,1,0:T(8,128)S(1)}, f32[16,24,128]{2,1,0:T(8,128)S(1)}, u32[]{:S(2)}, u32[]{:S(2)}) %collective-permute-start.2) | collective-permute-done | bytes 196640 | tf_op jit(solution)/shard_map/ppermute | solution.py:570
  57.6 0.9 collective-permute-done.3.second_ref
  58.5 5.8 %basis.1 = (f32[5,2,2,16,2,8,128]{6,5,4,3,2,1,0:T(8,128)S(1)}, f32[3,2,16,2,8,128]{5,4,3,2,1,0:T(8,128)S(1)}, f32[8,8,128]{2,1,0:T(8,128)S(1)}) custom-call(f32[2,16,4,8,128]{4,3,2,1,0:T(8,128)S(1)} %bitcast.88, f32[16,24,128]{2,1,0:T(8,128)S(1)} %collective-permute-done.2.first_ref, f32[16,24,128]{2,1,0:T(8,128)S(1)} %collective-permute-done.3.second_ref, ...), custom_call_target="tpu_custom_call" | custom-call | tf_op jit(solution)/shard_map/basis/pallas_call | solution.py:572
  64.3 13.4 %all_to_all.95.part_ref = f32[8,8,128]{2,1,0:T(8,128)S(1)} all-to-all(f32[8,8,128]{2,1,0:T(8,128)S(1)} %get-tuple-element.174), channel_id=1, replica_groups=mesh['z'=8,'core'=2,'y'=4,'x'=4] {'z'}, dimensions={0} | all-to-all | bytes 65536 | tf_op jit(solution)/shard_map/all_to_all | solution.py:509
  77.7 0.0 copy-done
  77.7 1.7 %combine.1 = f32[32,2,2,8,128]{4,3,2,1,0:T(8,128)} custom-call(s32[1,64]{1,0:T(1,128)S(1)} %bitcast.86, f32[8,8,128]{2,1,0:T(8,128)S(1)} %all_to_all.95.part_ref, f32[2,16,4,8,128]{4,3,2,1,0:T(8,128)S(1)} %bitcast.89, f32[5,2,2,16,2,8,128]{6,5,4,3,2,1,0:T(8,128)S(1)} %get-tuple-element.175.v_ref, f32[3,2,16,2,8,128]{5,4,3,2,1,0:T(8,128)S(1)} %get-tuple-element.176.inv_ref), custom_call_target="tpu_custom_call" | custom-call | tf_op jit(solution)/shard_map/combine/pallas_call | solution.py:586
  79.4 5.8 %all-to-all-start.9 = ((f32[32,2,2,8,128]{4,3,2,1,0:T(8,128)}), f32[32,2,2,8,128]{4,3,2,1,0:T(8,128)S(1)}, u32[]{:S(2)}, u32[]{:S(2)}) async-start(f32[32,2,2,8,128]{4,3,2,1,0:T(8,128)} %combine.1), calls=%async_computation.9 | async-start | bytes 1048576 | tf_op jit(solution)/shard_map/all_to_all | solution.py:509
  85.2 11.2 %all-to-all-done.9.s_ref = f32[32,2,2,8,128]{4,3,2,1,0:T(8,128)S(1)} async-done(((f32[32,2,2,8,128]{4,3,2,1,0:T(8,128)}), f32[32,2,2,8,128]{4,3,2,1,0:T(8,128)S(1)}, u32[]{:S(2)}, u32[]{:S(2)}) %all-to-all-start.9) | async-done | bytes 524320 | tf_op jit(solution)/shard_map/all_to_all | solution.py:509
  96.4 0.3 inverse.1
  96.7 21.1 %conditional.1 = (f32[4,2,128,128]{3,2,1,0:T(8,128)S(1)}) conditional(s32[]{:T(128)} %bitcast.36, f32[64,2,8,128]{3,2,1,0:T(8,128)S(1)} %get-tuple-element.178, (f32[4,2,128,128]{3,2,1,0:T(8,128)}, f32[2,128,128]{2,1,0:T(8,128)}, s32[64]{0:T(128)S(1)}) %tuple.70), branch_computations={%region_0.0_spmd, %region_1.9_spmd} | conditional | flops 413107744 | bytes 59532052 | solution.py:634
  96.7 20.8 %all_to_all.92 = f32[16,4,2,8,128]{4,3,2,1,0:T(8,128)S(1)} all-to-all(f32[16,4,2,8,128]{4,3,2,1,0:T(8,128)S(1)} %bitcast.91), channel_id=1, replica_groups=mesh['z'=8,'core'=2,'y'=4,'x'=4] {'z','core'}, dimensions={0} | all-to-all | bytes 1048576 | tf_op jit(solution)/shard_map/cond/branch_0_fun/all_to_all | solution.py:509
  117.8 0.0 copy-start.1
  117.8 0.8 copy-done.1
  (10 shorter events, 0.1 us)
Async XLA Ops:
  2.0 27.2 %all-to-all-start.6 = ((f32[16,4,2,8,128]{4,3,2,1,0:T(8,128)}), f32[16,4,2,8,128]{4,3,2,1,0:T(8,128)S(1)}, u32[]{:S(2)}, u32[]{:S(2)}) async-start(f32[16,4,2,8,128]{4,3,2,1,0:T(8,128)} %get-tuple-element.170), calls=%async_computation.6 | async-start | bytes 1048576 | tf_op jit(solution)/shard_map/all_to_all | solution.py:509
  11.9 65.7 %copy-start = (s32[64]{0:T(128)S(1)}, s32[64]{0:T(128)}, u32[]{:S(2)}) copy-start(s32[64]{0:T(128)} %param.9) | copy-start | bytes 772
  11.9 2.7 %collective-permute-start.4 = (f32[1,2,2,8,128]{4,3,2,1,0:T(8,128)S(1)}, f32[1,2,2,8,128]{4,3,2,1,0:T(8,128)S(1)}, u32[]{:S(2)}, u32[]{:S(2)}) collective-permute-start(f32[1,2,2,8,128]{4,3,2,1,0:T(8,128)S(1)} %bitcast.92), channel_id=1, source_target_pairs={{0,1},{1,0},{2,3},{3,2},{4,5},{5,4},{6,7},{7,6},{8,9},{9,8},{10,11... | collective-permute-start | bytes 49160 | tf_op jit(solution)/shard_map/ppermute | solution.py:548
  14.6 4.4 %collective-permute-start.5 = (f32[2,2,2,8,128]{4,3,2,1,0:T(8,128)S(1)}, f32[2,2,2,8,128]{4,3,2,1,0:T(8,128)S(1)}, u32[]{:S(2)}, u32[]{:S(2)}) collective-permute-start(f32[2,2,2,8,128]{4,3,2,1,0:T(8,128)S(1)} %pad_maximum_fusion.10), channel_id=1, source_target_pairs={{0,2},{1,3},{2,0},{3,1},{4,6},{5,7},{6,4},{7,5},{8,10},{9,11},{10,... | collective-permute-start | bytes 98312 | tf_op jit(solution)/shard_map/ppermute | solution.py:548
  19.0 18.3 %collective-permute-start.6 = (f32[4,2,2,8,128]{4,3,2,1,0:T(8,128)S(1)}, f32[4,2,2,8,128]{4,3,2,1,0:T(8,128)S(1)}, u32[]{:S(2)}, u32[]{:S(2)}) collective-permute-start(f32[4,2,2,8,128]{4,3,2,1,0:T(8,128)S(1)} %pad_maximum_fusion.9), channel_id=1, source_target_pairs={{0,4},{4,0},{8,12},{12,8},{1,5},{5,1},{9,13},{13,9},{2,6},{6,2},{1... | collective-permute-start | bytes 196616 | tf_op jit(solution)/shard_map/ppermute | solution.py:548
  30.2 20.4 %all-to-all-start.7 = ((f32[32,4,8,128]{3,2,1,0:T(8,128)}), f32[32,4,8,128]{3,2,1,0:T(8,128)S(1)}, u32[]{:S(2)}, u32[]{:S(2)}) async-start(f32[32,4,8,128]{3,2,1,0:T(8,128)} %forward.1), calls=%async_computation.7 | async-start | bytes 1048576 | tf_op jit(solution)/shard_map/all_to_all | solution.py:509
  37.4 12.1 %collective-permute-start.7 = (f32[8,2,2,8,128]{4,3,2,1,0:T(8,128)S(1)}, f32[8,2,2,8,128]{4,3,2,1,0:T(8,128)S(1)}, u32[]{:S(2)}, u32[]{:S(2)}) collective-permute-start(f32[8,2,2,8,128]{4,3,2,1,0:T(8,128)S(1)} %pad_maximum_fusion.8), channel_id=1, source_target_pairs={{0,8},{4,12},{8,0},{12,4},{1,9},{5,13},{9,1},{13,5},{2,10},{6,14},... | collective-permute-start | bytes 393224 | tf_op jit(solution)/shard_map/ppermute | solution.py:548
  49.5 6.4 %collective-permute-start.8 = (f32[16,2,2,8,128]{4,3,2,1,0:T(8,128)S(1)}, f32[16,2,2,8,128]{4,3,2,1,0:T(8,128)S(1)}, u32[]{:S(2)}, u32[]{:S(2)}) collective-permute-start(f32[16,2,2,8,128]{4,3,2,1,0:T(8,128)S(1)} %constant_dynamic-update-slice_fusion.abs_ref), channel_id=1, source_target_pairs={{0,16},{16,0},{1,17},{17,1},{2,18},{18,2},{3,19},{19,3},{4,20},{20... | collective-permute-start | bytes 786440 | tf_op jit(solution)/shard_map/ppermute | solution.py:550
  50.6 7.0 %collective-permute-start.2 = (f32[16,24,128]{2,1,0:T(8,128)S(1)}, f32[16,24,128]{2,1,0:T(8,128)S(1)}, u32[]{:S(2)}, u32[]{:S(2)}) collective-permute-start(f32[16,24,128]{2,1,0:T(8,128)S(1)} %get-tuple-element.171), channel_id=1, source_target_pairs={{0,32},{32,64},{64,96},{96,128},{128,160},{160,192},{192,224},{48,... | collective-permute-start | bytes 589832 | tf_op jit(solution)/shard_map/ppermute | solution.py:570
  51.9 6.6 %collective-permute-start.3 = (f32[16,24,128]{2,1,0:T(8,128)S(1)}, f32[16,24,128]{2,1,0:T(8,128)S(1)}, u32[]{:S(2)}, u32[]{:S(2)}) collective-permute-start(f32[16,24,128]{2,1,0:T(8,128)S(1)} %get-tuple-element.172), channel_id=1, source_target_pairs={{32,0},{64,32},{96,64},{128,96},{160,128},{192,160},{224,192},{16,... | collective-permute-start | bytes 589832 | tf_op jit(solution)/shard_map/ppermute | solution.py:571
  79.4 17.0 %all-to-all-start.9 = ((f32[32,2,2,8,128]{4,3,2,1,0:T(8,128)}), f32[32,2,2,8,128]{4,3,2,1,0:T(8,128)S(1)}, u32[]{:S(2)}, u32[]{:S(2)}) async-start(f32[32,2,2,8,128]{4,3,2,1,0:T(8,128)} %combine.1), calls=%async_computation.9 | async-start | bytes 1048576 | tf_op jit(solution)/shard_map/all_to_all | solution.py:509
  117.8 0.8 copy-start.1

commit v7 on v6

--- a/solution.py
+++ b/solution.py
@@ -216,7 +216,8 @@
         copy.wait()
 
 
-def forward_kernel(x_ref, out_ref):
+def forward_kernel(x_ref, rows_ref, swap_ref, out_ref):
+    del rows_ref, swap_ref
     for zz in range(2):
         spectrum = real_transform([x_ref[n, zz] * decay**n for n in range(L)])
         out_ref[0, zz] = spectrum[0][0]
@@ -271,7 +272,7 @@
 
 def basis_kernel(own_ref, first_ref, second_ref, abs_ref, swap_ref, v_ref, inv_ref, gram_ref, u, edge_inv, sums):
     slot, z, core = lax.axis_index(SLOTS), lax.axis_index("z"), lax.axis_index("core")
-    home = lax.axis_index(SPACE)
+    home_y, home_x = lax.axis_index("y"), lax.axis_index("x")
     shifts_here = slot_shifts()
     shift_a, shift_b, shift_im = (pick(slot, shifts_here[:, i]) for i in range(3))
     lanes = lax.broadcasted_iota(jnp.int32, (8, 128), 1)
@@ -297,7 +298,7 @@
                     u[turn, part, 2 * sp + zz + 1, pl.ds(40, 8), :] = blank
         for tile in range(4):
             for zz in range(2):
-                mine, other = (ref[sp ^ home, tile % 2, zz] for ref in (abs_ref, swap_ref))
+                mine, other = (ref[4 * ((home_y + 4 - sp // 4) % 4) + (home_x + 16 - sp) % 4, tile % 2, zz] for ref in (abs_ref, swap_ref))
                 base = jnp.where(core == tile // 2, mine, other)
                 da, db = (shift_a + 6.0) + base, (shift_b + 6.0) + base
                 ra, rb = 1.0 / (da * da + shift_im * shift_im), 1.0 / (db * db + shift_im * shift_im)
@@ -544,18 +545,18 @@
     series = exchanged(bands, TM).reshape(L, 2, 8, 128)
     rows = rows[None]
     for axis in ("x", "y"):
-        for bit in (1, 2):
-            near = lax.ppermute(rows, axis, [(i, i ^ bit) for i in range(lax.axis_size(axis))])
-            rows = jnp.concatenate([rows, near])
+        size = lax.axis_size(axis)
+        near = [lax.ppermute(rows, axis, [(i, (i + d) % size) for i in range(size)]) for d in range(1, size)]
+        rows = jnp.concatenate([rows, *near])
     swap = lax.ppermute(rows, "core", [(0, 1), (1, 0)])
     spectrum = pl.pallas_call(
         forward_kernel,
         out_shape=f32(PAIRS, 4, 8, 128),
-        in_specs=[VMEM],
+        in_specs=[VMEM, ANY, ANY],
         out_specs=VMEM,
         compiler_params=room(4),
         name="forward",
-    )(held(series))
+    )(held(series), rows, swap)
     own = held(exchanged(spectrum, SLOTS).reshape(2, 16, 4, 8, 128))
     first, second = pl.pallas_call(
         edges_kernel,

time: 119 us -> 121 us (1.017)
  blocking collectives: 34.2 us -> 47 us
  waiting for transfers between devices: 34.7 us -> 29 us
  starting transfers between devices: 37.7 us -> 33 us
    all_to_all x2 -> x3, blocking collectives: 34.2 us -> 47 us  [exchanged(): return lax.all_to_all(blocks, axes, split_axis=0, concat_axis=0, tiled=True)]
    ppermute x4 -> x6, waiting for transfers between devices: 12.1 us -> 2.4 us  [together(): lax.ppermute(rows, axis, [(i, (i + d) % size) for i in range(size)])]
    all_to_all x3 -> x2, starting transfers between devices: 23 us -> 18.2 us  [exchanged(): return lax.all_to_all(blocks, axes, split_axis=0, concat_axis=0, tiled=True)]
    ppermute x1, waiting for transfers between devices: 1.7 us -> 6.03 us  [together(): first = lax.ppermute(first, TM, ups[0] + downs[1])]
    ppermute x1, starting transfers between devices: 4 us -> 1.3 us  [together(): second = lax.ppermute(second, TM, downs[0] + ups[1])]
    ppermute x4 -> x6, starting transfers between devices: 8.32 us -> 10.8 us  [together(): lax.ppermute(rows, axis, [(i, (i + d) % size) for i in range(size)])]
    all_to_all x3 -> x2, waiting for transfers between devices: 20 us -> 18.2 us  [exchanged(): return lax.all_to_all(blocks, axes, split_axis=0, concat_axis=0, tiled=True)]
  transfers between devices with their start and end apart: 10 -> 11, of which waited for: 7 -> 6; matrix products, arithmetic and copies ran while one was open for 0% -> 0% of each run, Pallas kernels for 1% -> 0%
where the time goes in v7:
time: 121 us; the launch traced here: 120 us
  blocking collectives  47 us (39%)
  starting transfers between devices  33 us (27%)
  waiting for transfers between devices  29 us (24%)
  Pallas kernels  9.74 us (8%)
    all_to_all x3, blocking collectives, exchanged(): return lax.all_to_all(blocks, axes, split_axis=0, concat_axis=0, tiled=True)  47 us
    all_to_all x2, starting transfers between devices, exchanged(): return lax.all_to_all(blocks, axes, split_axis=0, concat_axis=0, tiled=True)  18.2 us
    all_to_all x2, waiting for transfers between devices, exchanged(): return lax.all_to_all(blocks, axes, split_axis=0, concat_axis=0, tiled=True)  18.2 us
    ppermute x6, starting transfers between devices, together(): lax.ppermute(rows, axis, [(i, (i + d) % size) for i in range(size)])  10.8 us
    ppermute x1, waiting for transfers between devices, together(): first = lax.ppermute(first, TM, ups[0] + downs[1])  6.03 us
    pallas_call x1, Pallas kernels, together(): pl.pallas_call(basis_kernel, out_shape=(f32(STEPS - 1, 2, 2, 16, 2, 8, 12...  5.47 us
  transfers between devices with their start and end apart: 11, of which 6 were waited for; matrix products, arithmetic and copies ran while one was open for 0% of the time, Pallas kernels for 0%

profile of v7, /device:TPU:1, one launch (start us, length us, event | category | flops | bytes accessed | tf_op | source)
XLA Modules:
  0.0 120.1 jit_solution(8227886845777782857)
XLA Ops:
  0.0 2.0 %bands.1 = (f32[16,4,2,8,128]{4,3,2,1,0:T(8,128)}, f32[2,2,8,128]{3,2,1,0:T(8,128)S(1)}) custom-call(f32[4,2,128,128]{3,2,1,0:T(8,128)} %x_ref.1, f32[2,128,128]{2,1,0:T(8,128)} %a_ref.1), custom_call_target="tpu_custom_call" | custom-call | tf_op jit(solution)/shard_map/bands/pallas_call | solution.py:536
  2.0 2.1 %collective-permute-start.2 = (f32[1,2,2,8,128]{4,3,2,1,0:T(8,128)S(1)}, f32[1,2,2,8,128]{4,3,2,1,0:T(8,128)S(1)}, u32[]{:S(2)}, u32[]{:S(2)}) collective-permute-start(f32[1,2,2,8,128]{4,3,2,1,0:T(8,128)S(1)} %bitcast.92), channel_id=1, source_target_pairs={{0,1},{1,2},{2,3},{3,0},{4,5},{5,6},{6,7},{7,4},{8,9},{9,10},{10,1... | collective-permute-start | bytes 49160 | tf_op jit(solution)/shard_map/ppermute | solution.py:549
  4.1 2.5 %collective-permute-start.3 = (f32[1,2,2,8,128]{4,3,2,1,0:T(8,128)S(1)}, f32[1,2,2,8,128]{4,3,2,1,0:T(8,128)S(1)}, u32[]{:S(2)}, u32[]{:S(2)}) collective-permute-start(f32[1,2,2,8,128]{4,3,2,1,0:T(8,128)S(1)} %bitcast.93), channel_id=1, source_target_pairs={{0,2},{1,3},{2,0},{3,1},{4,6},{5,7},{6,4},{7,5},{8,10},{9,11},{10,... | collective-permute-start | bytes 49160 | tf_op jit(solution)/shard_map/ppermute | solution.py:549
  6.5 1.2 collective-permute-start.4
  7.7 10.0 %all-to-all-start.6 = ((f32[16,4,2,8,128]{4,3,2,1,0:T(8,128)}), f32[16,4,2,8,128]{4,3,2,1,0:T(8,128)S(1)}, u32[]{:S(2)}, u32[]{:S(2)}) async-start(f32[16,4,2,8,128]{4,3,2,1,0:T(8,128)} %get-tuple-element.170), calls=%async_computation.6 | async-start | bytes 1048576 | tf_op jit(solution)/shard_map/all_to_all | solution.py:510
  17.7 0.0 copy-start
  17.7 0.0 collective-permute-done.2
  17.7 0.0 collective-permute-done.4
  17.7 1.4 %collective-permute-start.5 = (f32[4,2,2,8,128]{4,3,2,1,0:T(8,128)S(1)}, f32[4,2,2,8,128]{4,3,2,1,0:T(8,128)S(1)}, u32[]{:S(2)}, u32[]{:S(2)}) collective-permute-start(f32[4,2,2,8,128]{4,3,2,1,0:T(8,128)S(1)} %pad_maximum_fusion.8), channel_id=1, source_target_pairs={{0,4},{4,8},{8,12},{12,0},{1,5},{5,9},{9,13},{13,1},{2,6},{6,10},{... | collective-permute-start | bytes 196616 | tf_op jit(solution)/shard_map/ppermute | solution.py:549
  19.1 2.6 %collective-permute-start.6 = (f32[4,2,2,8,128]{4,3,2,1,0:T(8,128)S(1)}, f32[4,2,2,8,128]{4,3,2,1,0:T(8,128)S(1)}, u32[]{:S(2)}, u32[]{:S(2)}) collective-permute-start(f32[4,2,2,8,128]{4,3,2,1,0:T(8,128)S(1)} %pad_maximum_fusion.8), channel_id=1, source_target_pairs={{0,8},{4,12},{8,0},{12,4},{1,9},{5,13},{9,1},{13,5},{2,10},{6,14},... | collective-permute-start | bytes 196616 | tf_op jit(solution)/shard_map/ppermute | solution.py:549
  21.7 1.1 collective-permute-start.7
  22.8 0.0 collective-permute-done.5
  22.8 2.4 %collective-permute-done.6 = f32[4,2,2,8,128]{4,3,2,1,0:T(8,128)S(1)} collective-permute-done((f32[4,2,2,8,128]{4,3,2,1,0:T(8,128)S(1)}, f32[4,2,2,8,128]{4,3,2,1,0:T(8,128)S(1)}, u32[]{:S(2)}, u32[]{:S(2)}) %collective-permute-start.6) | collective-permute-done | bytes 65568 | tf_op jit(solution)/shard_map/ppermute | solution.py:549
  25.2 1.4 %collective-permute-start.8 = (f32[16,2,2,8,128]{4,3,2,1,0:T(8,128)S(1)}, f32[16,2,2,8,128]{4,3,2,1,0:T(8,128)S(1)}, u32[]{:S(2)}, u32[]{:S(2)}) collective-permute-start(f32[16,2,2,8,128]{4,3,2,1,0:T(8,128)S(1)} %constant_dynamic-update-slice_fusion.rows_ref.abs_ref), channel_id=1, source_target_pairs={{0,16},{16,0},{1,17},{17,1},{2,18},{18,2},{3,19},{19,3},{4,20},{20... | collective-permute-start | bytes 786440 | tf_op jit(solution)/shard_map/ppermute | solution.py:551
  26.7 1.2 collective-permute-done.8.swap_ref
  27.8 7.0 %all-to-all-done.6 = f32[16,4,2,8,128]{4,3,2,1,0:T(8,128)S(1)} async-done(((f32[16,4,2,8,128]{4,3,2,1,0:T(8,128)}), f32[16,4,2,8,128]{4,3,2,1,0:T(8,128)S(1)}, u32[]{:S(2)}, u32[]{:S(2)}) %all-to-all-start.6) | async-done | bytes 524320 | tf_op jit(solution)/shard_map/all_to_all | solution.py:510
  34.9 0.2 forward.1
  35.1 15.7 %all_to_all.95 = f32[32,4,8,128]{3,2,1,0:T(8,128)S(1)} all-to-all(f32[32,4,8,128]{3,2,1,0:T(8,128)S(1)} %forward.1), channel_id=1, replica_groups=mesh['z'=8,'core'=2,'y'=4,'x'=4] {'core','y','x'}, dimensions={0} | all-to-all | bytes 1048576 | tf_op jit(solution)/shard_map/all_to_all | solution.py:510
  50.9 1.3 %collective-permute-start.10 = (f32[16,24,128]{2,1,0:T(8,128)S(1)}, f32[16,24,128]{2,1,0:T(8,128)S(1)}, u32[]{:S(2)}, u32[]{:S(2)}) collective-permute-start(f32[16,24,128]{2,1,0:T(8,128)S(1)} %get-tuple-element.173), channel_id=1, source_target_pairs={{32,0},{64,32},{96,64},{128,96},{160,128},{192,160},{224,192},{16,... | collective-permute-start | bytes 589832 | tf_op jit(solution)/shard_map/ppermute | solution.py:572
  52.2 1.3 %collective-permute-start.9 = (f32[16,24,128]{2,1,0:T(8,128)S(1)}, f32[16,24,128]{2,1,0:T(8,128)S(1)}, u32[]{:S(2)}, u32[]{:S(2)}) collective-permute-start(f32[16,24,128]{2,1,0:T(8,128)S(1)} %get-tuple-element.172), channel_id=1, source_target_pairs={{0,32},{32,64},{64,96},{96,128},{128,160},{160,192},{192,224},{48,... | collective-permute-start | bytes 589832 | tf_op jit(solution)/shard_map/ppermute | solution.py:571
  53.5 1.3 %collective-permute-done.10.second_ref = f32[16,24,128]{2,1,0:T(8,128)S(1)} collective-permute-done((f32[16,24,128]{2,1,0:T(8,128)S(1)}, f32[16,24,128]{2,1,0:T(8,128)S(1)}, u32[]{:S(2)}, u32[]{:S(2)}) %collective-permute-start.10) | collective-permute-done | bytes 196640 | tf_op jit(solution)/shard_map/ppermute | solution.py:572
  54.8 6.0 %collective-permute-done.9.first_ref = f32[16,24,128]{2,1,0:T(8,128)S(1)} collective-permute-done((f32[16,24,128]{2,1,0:T(8,128)S(1)}, f32[16,24,128]{2,1,0:T(8,128)S(1)}, u32[]{:S(2)}, u32[]{:S(2)}) %collective-permute-start.9) | collective-permute-done | bytes 196640 | tf_op jit(solution)/shard_map/ppermute | solution.py:571
  60.8 5.5 %basis.1 = (f32[5,2,2,16,2,8,128]{6,5,4,3,2,1,0:T(8,128)S(1)}, f32[3,2,16,2,8,128]{5,4,3,2,1,0:T(8,128)S(1)}, f32[8,8,128]{2,1,0:T(8,128)S(1)}) custom-call(f32[2,16,4,8,128]{4,3,2,1,0:T(8,128)S(1)} %bitcast.88, f32[16,24,128]{2,1,0:T(8,128)S(1)} %collective-permute-done.9.first_ref, f32[16,24,128]{2,1,0:T(8,128)S(1)} %collective-permute-done.10.second_ref, ...), custom_call_target="tpu_custom_call" | custom-call | tf_op jit(solution)/shard_map/basis/pallas_call | solution.py:573
  66.3 10.5 %all_to_all.96.part_ref = f32[8,8,128]{2,1,0:T(8,128)S(1)} all-to-all(f32[8,8,128]{2,1,0:T(8,128)S(1)} %get-tuple-element.174), channel_id=1, replica_groups=mesh['z'=8,'core'=2,'y'=4,'x'=4] {'z'}, dimensions={0} | all-to-all | bytes 65536 | tf_op jit(solution)/shard_map/all_to_all | solution.py:510
  76.7 1.7 %combine.1 = f32[32,2,2,8,128]{4,3,2,1,0:T(8,128)} custom-call(s32[1,64]{1,0:T(1,128)S(1)} %bitcast.86, f32[8,8,128]{2,1,0:T(8,128)S(1)} %all_to_all.96.part_ref, f32[2,16,4,8,128]{4,3,2,1,0:T(8,128)S(1)} %bitcast.89, f32[5,2,2,16,2,8,128]{6,5,4,3,2,1,0:T(8,128)S(1)} %get-tuple-element.175.v_ref, f32[3,2,16,2,8,128]{5,4,3,2,1,0:T(8,128)S(1)} %get-tuple-element.176.inv_ref), custom_call_target="tpu_custom_call" | custom-call | tf_op jit(solution)/shard_map/combine/pallas_call | solution.py:587
  78.4 8.2 %all-to-all-start.9 = ((f32[32,2,2,8,128]{4,3,2,1,0:T(8,128)}), f32[32,2,2,8,128]{4,3,2,1,0:T(8,128)S(1)}, u32[]{:S(2)}, u32[]{:S(2)}) async-start(f32[32,2,2,8,128]{4,3,2,1,0:T(8,128)} %combine.1), calls=%async_computation.9 | async-start | bytes 1048576 | tf_op jit(solution)/shard_map/all_to_all | solution.py:510
  86.7 11.1 %all-to-all-done.9.s_ref = f32[32,2,2,8,128]{4,3,2,1,0:T(8,128)S(1)} async-done(((f32[32,2,2,8,128]{4,3,2,1,0:T(8,128)}), f32[32,2,2,8,128]{4,3,2,1,0:T(8,128)S(1)}, u32[]{:S(2)}, u32[]{:S(2)}) %all-to-all-start.9) | async-done | bytes 524320 | tf_op jit(solution)/shard_map/all_to_all | solution.py:510
  97.8 0.3 inverse.1
  98.2 21.1 %conditional.1 = (f32[4,2,128,128]{3,2,1,0:T(8,128)S(1)}) conditional(s32[]{:T(128)} %bitcast.36, f32[64,2,8,128]{3,2,1,0:T(8,128)S(1)} %get-tuple-element.178, (f32[4,2,128,128]{3,2,1,0:T(8,128)}, f32[2,128,128]{2,1,0:T(8,128)}, s32[64]{0:T(128)S(1)}) %tuple.70), branch_computations={%region_0.0_spmd, %region_1.9_spmd} | conditional | flops 413107744 | bytes 59532052 | solution.py:635
  98.2 20.8 %all_to_all.92 = f32[16,4,2,8,128]{4,3,2,1,0:T(8,128)S(1)} all-to-all(f32[16,4,2,8,128]{4,3,2,1,0:T(8,128)S(1)} %bitcast.91), channel_id=1, replica_groups=mesh['z'=8,'core'=2,'y'=4,'x'=4] {'z','core'}, dimensions={0} | all-to-all | bytes 1048576 | tf_op jit(solution)/shard_map/cond/branch_0_fun/all_to_all | solution.py:510
  119.3 0.0 copy-start.1
  119.3 0.8 copy-done.1
  (13 shorter events, 0.1 us)
Async XLA Ops:
  2.0 15.7 %collective-permute-start.2 = (f32[1,2,2,8,128]{4,3,2,1,0:T(8,128)S(1)}, f32[1,2,2,8,128]{4,3,2,1,0:T(8,128)S(1)}, u32[]{:S(2)}, u32[]{:S(2)}) collective-permute-start(f32[1,2,2,8,128]{4,3,2,1,0:T(8,128)S(1)} %bitcast.92), channel_id=1, source_target_pairs={{0,1},{1,2},{2,3},{3,0},{4,5},{5,6},{6,7},{7,4},{8,9},{9,10},{10,1... | collective-permute-start | bytes 49160 | tf_op jit(solution)/shard_map/ppermute | solution.py:549
  4.1 13.6 %collective-permute-start.3 = (f32[1,2,2,8,128]{4,3,2,1,0:T(8,128)S(1)}, f32[1,2,2,8,128]{4,3,2,1,0:T(8,128)S(1)}, u32[]{:S(2)}, u32[]{:S(2)}) collective-permute-start(f32[1,2,2,8,128]{4,3,2,1,0:T(8,128)S(1)} %bitcast.93), channel_id=1, source_target_pairs={{0,2},{1,3},{2,0},{3,1},{4,6},{5,7},{6,4},{7,5},{8,10},{9,11},{10,... | collective-permute-start | bytes 49160 | tf_op jit(solution)/shard_map/ppermute | solution.py:549
  6.5 11.2 %collective-permute-start.4 = (f32[1,2,2,8,128]{4,3,2,1,0:T(8,128)S(1)}, f32[1,2,2,8,128]{4,3,2,1,0:T(8,128)S(1)}, u32[]{:S(2)}, u32[]{:S(2)}) collective-permute-start(f32[1,2,2,8,128]{4,3,2,1,0:T(8,128)S(1)} %bitcast.94), channel_id=1, source_target_pairs={{0,3},{1,0},{2,1},{3,2},{4,7},{5,4},{6,5},{7,6},{8,11},{9,8},{10,9... | collective-permute-start | bytes 49160 | tf_op jit(solution)/shard_map/ppermute | solution.py:549
  7.7 27.2 %all-to-all-start.6 = ((f32[16,4,2,8,128]{4,3,2,1,0:T(8,128)}), f32[16,4,2,8,128]{4,3,2,1,0:T(8,128)S(1)}, u32[]{:S(2)}, u32[]{:S(2)}) async-start(f32[16,4,2,8,128]{4,3,2,1,0:T(8,128)} %get-tuple-element.170), calls=%async_computation.6 | async-start | bytes 1048576 | tf_op jit(solution)/shard_map/all_to_all | solution.py:510
  17.7 59.1 %copy-start = (s32[64]{0:T(128)S(1)}, s32[64]{0:T(128)}, u32[]{:S(2)}) copy-start(s32[64]{0:T(128)} %param.9) | copy-start | bytes 772
  17.7 5.1 %collective-permute-start.5 = (f32[4,2,2,8,128]{4,3,2,1,0:T(8,128)S(1)}, f32[4,2,2,8,128]{4,3,2,1,0:T(8,128)S(1)}, u32[]{:S(2)}, u32[]{:S(2)}) collective-permute-start(f32[4,2,2,8,128]{4,3,2,1,0:T(8,128)S(1)} %pad_maximum_fusion.8), channel_id=1, source_target_pairs={{0,4},{4,8},{8,12},{12,0},{1,5},{5,9},{9,13},{13,1},{2,6},{6,10},{... | collective-permute-start | bytes 196616 | tf_op jit(solution)/shard_map/ppermute | solution.py:549
  19.1 6.1 %collective-permute-start.6 = (f32[4,2,2,8,128]{4,3,2,1,0:T(8,128)S(1)}, f32[4,2,2,8,128]{4,3,2,1,0:T(8,128)S(1)}, u32[]{:S(2)}, u32[]{:S(2)}) collective-permute-start(f32[4,2,2,8,128]{4,3,2,1,0:T(8,128)S(1)} %pad_maximum_fusion.8), channel_id=1, source_target_pairs={{0,8},{4,12},{8,0},{12,4},{1,9},{5,13},{9,1},{13,5},{2,10},{6,14},... | collective-permute-start | bytes 196616 | tf_op jit(solution)/shard_map/ppermute | solution.py:549
  21.7 3.5 %collective-permute-start.7 = (f32[4,2,2,8,128]{4,3,2,1,0:T(8,128)S(1)}, f32[4,2,2,8,128]{4,3,2,1,0:T(8,128)S(1)}, u32[]{:S(2)}, u32[]{:S(2)}) collective-permute-start(f32[4,2,2,8,128]{4,3,2,1,0:T(8,128)S(1)} %pad_maximum_fusion.8), channel_id=1, source_target_pairs={{0,12},{4,0},{8,4},{12,8},{1,13},{5,1},{9,5},{13,9},{2,14},{6,2},{... | collective-permute-start | bytes 196616 | tf_op jit(solution)/shard_map/ppermute | solution.py:549
  25.2 2.6 %collective-permute-start.8 = (f32[16,2,2,8,128]{4,3,2,1,0:T(8,128)S(1)}, f32[16,2,2,8,128]{4,3,2,1,0:T(8,128)S(1)}, u32[]{:S(2)}, u32[]{:S(2)}) collective-permute-start(f32[16,2,2,8,128]{4,3,2,1,0:T(8,128)S(1)} %constant_dynamic-update-slice_fusion.rows_ref.abs_ref), channel_id=1, source_target_pairs={{0,16},{16,0},{1,17},{17,1},{2,18},{18,2},{3,19},{19,3},{4,20},{20... | collective-permute-start | bytes 786440 | tf_op jit(solution)/shard_map/ppermute | solution.py:551
  50.9 3.9 %collective-permute-start.10 = (f32[16,24,128]{2,1,0:T(8,128)S(1)}, f32[16,24,128]{2,1,0:T(8,128)S(1)}, u32[]{:S(2)}, u32[]{:S(2)}) collective-permute-start(f32[16,24,128]{2,1,0:T(8,128)S(1)} %get-tuple-element.173), channel_id=1, source_target_pairs={{32,0},{64,32},{96,64},{128,96},{160,128},{192,160},{224,192},{16,... | collective-permute-start | bytes 589832 | tf_op jit(solution)/shard_map/ppermute | solution.py:572
  52.2 8.6 %collective-permute-start.9 = (f32[16,24,128]{2,1,0:T(8,128)S(1)}, f32[16,24,128]{2,1,0:T(8,128)S(1)}, u32[]{:S(2)}, u32[]{:S(2)}) collective-permute-start(f32[16,24,128]{2,1,0:T(8,128)S(1)} %get-tuple-element.172), channel_id=1, source_target_pairs={{0,32},{32,64},{64,96},{96,128},{128,160},{160,192},{192,224},{48,... | collective-permute-start | bytes 589832 | tf_op jit(solution)/shard_map/ppermute | solution.py:571
  78.4 19.4 %all-to-all-start.9 = ((f32[32,2,2,8,128]{4,3,2,1,0:T(8,128)}), f32[32,2,2,8,128]{4,3,2,1,0:T(8,128)S(1)}, u32[]{:S(2)}, u32[]{:S(2)}) async-start(f32[32,2,2,8,128]{4,3,2,1,0:T(8,128)} %combine.1), calls=%async_computation.9 | async-start | bytes 1048576 | tf_op jit(solution)/shard_map/all_to_all | solution.py:510
  119.3 0.8 copy-start.1

commit v8 on v5

--- a/solution.py
+++ b/solution.py
@@ -277,31 +277,12 @@
                 abs_ref[side, sp, zz] = own_ref[side, sp, 4 + zz]
 
 
-def basis_kernel(own_ref, first_ref, second_ref, swap_ref, v_ref, inv_ref, gram_ref, u, edge_inv, sums):
+def inverses_kernel(own_ref, swap_ref, inv_ref, edge_inv_ref):
     slot, z, core = lax.axis_index(SLOTS), lax.axis_index("z"), lax.axis_index("core")
     shifts_here = slot_shifts()
     shift_a, shift_b, shift_im = (pick(slot, shifts_here[:, i]) for i in range(3))
-    lanes = lax.broadcasted_iota(jnp.int32, (8, 128), 1)
-    first_lane, last_lane = lanes == 0, lanes == 127
-    blank = jnp.zeros((8, 128), jnp.float32)
-
-    for turn in range(2):
-        for part in range(2):
-            for row in range(8, 40, 8):
-                u[turn, part, 0, pl.ds(row, 8), :] = blank
-                u[turn, part, NZ + 1, pl.ds(row, 8), :] = blank
-
-    def put(turn, tile, layer, inverse, re, im):
-        a, b, c = inverse
-        u[turn, 0, layer, pl.ds(8 + 8 * tile, 8), :] = a * re - c * im
-        u[turn, 1, layer, pl.ds(8 + 8 * tile, 8), :] = b * im + c * re
 
     def prepare(sp, _):
-        for turn in range(2):
-            for part in range(2):
-                for zz in range(2):
-                    u[turn, part, 2 * sp + zz + 1, pl.ds(0, 8), :] = blank
-                    u[turn, part, 2 * sp + zz + 1, pl.ds(40, 8), :] = blank
         for tile in range(4):
             for zz in range(2):
                 mine, other = own_ref[tile // 2, sp, 4 + zz], swap_ref[tile // 2, sp, zz]
@@ -312,12 +293,45 @@
                 if tile in (1, 2):
                     for i in range(3):
                         inv_ref[i, tile - 1, sp, zz] = found[i]
+                else:
+                    inside = z > 0 if tile == 0 else z < lax.axis_size("z") - 1
+                    for i in range(3):
+                        edge_inv_ref[i, tile // 3, sp, zz] = jnp.where(inside, found[i], 0.0)
+        return 0
+
+    lax.fori_loop(0, NZ // 2, prepare, 0, unroll=4)
+
+
+def basis_kernel(own_ref, first_ref, second_ref, inv_ref, edge_inv, v_ref, gram_ref, u, sums):
+    core = lax.axis_index("core")
+    lanes = lax.broadcasted_iota(jnp.int32, (8, 128), 1)
+    first_lane, last_lane = lanes == 0, lanes == 127
+    blank = jnp.zeros((8, 128), jnp.float32)
+
+    for turn in range(2):
+        for part in range(2):
+            for row in range(8, 40, 8):
+                u[turn, part, 0, pl.ds(row, 8), :] = blank
+                u[turn, part, NZ + 1, pl.ds(row, 8), :] = blank
+
+    def put(turn, tile, layer, inverse, re, im):
+        a, b, c = inverse
+        u[turn, 0, layer, pl.ds(8 + 8 * tile, 8), :] = a * re - c * im
+        u[turn, 1, layer, pl.ds(8 + 8 * tile, 8), :] = b * im + c * re
+
+    def prepare(sp, _):
+        for turn in range(2):
+            for part in range(2):
+                for zz in range(2):
+                    u[turn, part, 2 * sp + zz + 1, pl.ds(0, 8), :] = blank
+                    u[turn, part, 2 * sp + zz + 1, pl.ds(40, 8), :] = blank
+        for tile in range(4):
+            for zz in range(2):
+                if tile in (1, 2):
+                    found = [inv_ref[i, tile - 1, sp, zz] for i in range(3)]
                     re, im = (own_ref[tile - 1, sp, 2 * part + zz] for part in range(2))
                 else:
-                    inside = z > 0 if tile == 0 else z < lax.axis_size("z") - 1
-                    found = [jnp.where(inside, f, 0.0) for f in found]
-                    for i in range(3):
-                        edge_inv[i, tile // 3, sp, zz] = found[i]
+                    found = [edge_inv[i, tile // 3, sp, zz] for i in range(3)]
                     pair = []
                     for part in range(2):
                         at = HALO * (2 * part + zz)
@@ -571,19 +585,27 @@
     swap = lax.ppermute(swap, "core", [(0, 1), (1, 0)])
     first = lax.ppermute(first, TM, ups[0] + downs[1])
     second = lax.ppermute(second, TM, downs[0] + ups[1])
-    basis, inverses, partial = pl.pallas_call(
+    inverses, edge_inverses = pl.pallas_call(
+        inverses_kernel,
+        out_shape=(f32(3, 2, 16, 2, 8, 128), f32(3, 2, 16, 2, 8, 128)),
+        in_specs=[VMEM, VMEM],
+        out_specs=(VMEM, VMEM),
+        compiler_params=room(2),
+        cost_estimate=pl.CostEstimate(flops=2 * 10**6, bytes_accessed=2 * 10**6, transcendentals=0),
+        name="inverses",
+    )(own, held(swap))
+    basis, partial = pl.pallas_call(
         basis_kernel,
-        out_shape=(f32(STEPS - 1, 2, 2, 16, 2, 8, 128), f32(3, 2, 16, 2, 8, 128), f32(8, 8, 128)),
-        in_specs=[VMEM, VMEM, VMEM, VMEM],
-        out_specs=(VMEM, VMEM, VMEM),
+        out_shape=(f32(STEPS - 1, 2, 2, 16, 2, 8, 128), f32(8, 8, 128)),
+        in_specs=[VMEM] * 5,
+        out_specs=(VMEM, VMEM),
         scratch_shapes=[
             pltpu.VMEM((2, 2, NZ + 2, 48, 128), jnp.float32),
-            pltpu.VMEM((3, 2, 16, 2, 8, 128), jnp.float32),
             pltpu.VMEM((80, 8, 128), jnp.float32),
         ],
         compiler_params=room(10),
         name="basis",
-    )(own, held(first), held(second), held(swap))
+    )(own, held(first), held(second), held(inverses), held(edge_inverses))
     partials = exchanged(partial, "z")
     solved = pl.pallas_call(
         combine_kernel,
@@ -593,7 +615,7 @@
         compiler_params=room(6),
         name="combine",
     )(held(counts.reshape(1, L)), held(partials), own, held(basis), held(inverses))
-    gathered = exchanged(solved, SLOTS)
+    gathered, *arguments = lax.optimization_barrier((exchanged(solved, SLOTS), residual, absorption, counts))
     values, failed = pl.pallas_call(
         inverse_kernel,
         out_shape=(f32(L, 2, 8, 128), pltpu.SMEM((1,), jnp.int32)),
@@ -602,7 +624,7 @@
         compiler_params=room(4),
         name="inverse",
     )(held(gathered))
-    return values, failed
+    return values, failed, arguments
 
 
 def taken_kernel(*refs):
@@ -632,12 +654,12 @@
 
 
 def body(residual, absorption, counts):
-    values, failed = together(residual, absorption, counts)
+    values, failed, arguments = together(residual, absorption, counts)
     return lax.cond(
         failed[0] > 0,
         lambda r, a, c, v: stepwise(*taken(r, a), c),
         lambda r, a, c, v: to_steps(v, r.shape),
-        residual, absorption, counts, values,
+        *arguments, values,
     )
 
 

time: 117 us -> 115 us (0.983)
  blocking collectives: 81.8 us -> 96.8 us
  waiting for transfers between devices: 13.7 us -> 2.23 us
  starting transfers between devices: 11.1 us -> 6.63 us
    all_to_all x4 -> x5, blocking collectives: 81.8 us -> 96.8 us  [exchanged(): return lax.all_to_all(blocks, axes, split_axis=0, concat_axis=0, tiled=True)]
    all_to_all x1 -> x0, waiting for transfers between devices: 11.1 us -> none  [exchanged(): return lax.all_to_all(blocks, axes, split_axis=0, concat_axis=0, tiled=True)]
    all_to_all x1 -> x0, starting transfers between devices: 4.5 us -> none  [exchanged(): return lax.all_to_all(blocks, axes, split_axis=0, concat_axis=0, tiled=True)]
  transfers between devices with their start and end apart: 4 -> 3, of which waited for: 3 -> 2; matrix products, arithmetic and copies ran while one was open for 0% -> 0% of each run, Pallas kernels for 0% -> 0%
where the time goes in v8:
time: 115 us
  blocking collectives  96.8 us (84%)
  Pallas kernels  8.18 us (7%)
  starting transfers between devices  6.63 us (6%)
  waiting for transfers between devices  2.23 us (2%)
    all_to_all x5, blocking collectives, exchanged(): return lax.all_to_all(blocks, axes, split_axis=0, concat_axis=0, tiled=True)  96.8 us
    pallas_call x1, Pallas kernels, together(): pl.pallas_call(basis_kernel, out_shape=(f32(STEPS - 1, 2, 2, 16, 2, 8, 12...  5.14 us
    ppermute x1, starting transfers between devices, together(): second = lax.ppermute(second, TM, downs[0] + ups[1])  4 us
  transfers between devices with their start and end apart: 3, of which 2 were waited for; matrix products, arithmetic and copies ran while one was open for 0% of the time, Pallas kernels for 0%

profile of v8, /device:TPU:1, one launch (start us, length us, event | category | flops | bytes accessed | tf_op | source)
XLA Modules:
  0.0 115.0 jit_solution(3840598851084685445)
XLA Ops:
  0.0 1.2 %bands.1 = (f32[16,4,2,8,128]{4,3,2,1,0:T(8,128)S(1)}, f32[2,2,8,128]{3,2,1,0:T(8,128)S(1)}) custom-call(f32[4,2,128,128]{3,2,1,0:T(8,128)} %x_ref.1, f32[2,128,128]{2,1,0:T(8,128)} %a_ref.1), custom_call_target="tpu_custom_call" | custom-call | tf_op jit(solution)/shard_map/bands/pallas_call | solution.py:556
  1.2 27.0 %all_to_all.95 = f32[16,4,2,8,128]{4,3,2,1,0:T(8,128)S(1)} all-to-all(f32[16,4,2,8,128]{4,3,2,1,0:T(8,128)S(1)} %get-tuple-element.176), channel_id=1, replica_groups=mesh['z'=8,'core'=2,'y'=4,'x'=4] {'z','core'}, dimensions={0} | all-to-all | bytes 1048576 | tf_op jit(solution)/shard_map/all_to_all | solution.py:530
  28.1 0.2 forward.1
  28.4 20.7 %all_to_all.96 = f32[32,6,8,128]{3,2,1,0:T(8,128)S(1)} all-to-all(f32[32,6,8,128]{3,2,1,0:T(8,128)S(1)} %forward.1), channel_id=1, replica_groups=mesh['z'=8,'core'=2,'y'=4,'x'=4] {'core','y','x'}, dimensions={0} | all-to-all | bytes 1572864 | tf_op jit(solution)/shard_map/all_to_all | solution.py:530
  49.0 0.0 copy-start
  49.0 0.1 edges.1
  49.1 1.3 %collective-permute-start.4 = (f32[2,16,2,8,128]{4,3,2,1,0:T(8,128)S(1)}, f32[2,16,2,8,128]{4,3,2,1,0:T(8,128)S(1)}, u32[]{:S(2)}, u32[]{:S(2)}) collective-permute-start(f32[2,16,2,8,128]{4,3,2,1,0:T(8,128)S(1)} %get-tuple-element.180), channel_id=1, source_target_pairs={{0,16},{16,0},{1,17},{17,1},{2,18},{18,2},{3,19},{19,3},{4,20},{20... | collective-permute-start | bytes 786440 | tf_op jit(solution)/shard_map/ppermute | solution.py:585
  50.5 1.3 %collective-permute-start.2 = (f32[16,24,128]{2,1,0:T(8,128)S(1)}, f32[16,24,128]{2,1,0:T(8,128)S(1)}, u32[]{:S(2)}, u32[]{:S(2)}) collective-permute-start(f32[16,24,128]{2,1,0:T(8,128)S(1)} %get-tuple-element.178), channel_id=1, source_target_pairs={{0,32},{32,64},{64,96},{96,128},{128,160},{160,192},{192,224},{48,... | collective-permute-start | bytes 589832 | tf_op jit(solution)/shard_map/ppermute | solution.py:586
  51.7 4.0 %collective-permute-start.3 = (f32[16,24,128]{2,1,0:T(8,128)S(1)}, f32[16,24,128]{2,1,0:T(8,128)S(1)}, u32[]{:S(2)}, u32[]{:S(2)}) collective-permute-start(f32[16,24,128]{2,1,0:T(8,128)S(1)} %get-tuple-element.179), channel_id=1, source_target_pairs={{32,0},{64,32},{96,64},{128,96},{160,128},{192,160},{224,192},{16,... | collective-permute-start | bytes 589832 | tf_op jit(solution)/shard_map/ppermute | solution.py:587
  55.7 0.0 collective-permute-done.4.swap_ref
  55.8 0.3 inverses.1
  56.1 1.3 %collective-permute-done.2.first_ref = f32[16,24,128]{2,1,0:T(8,128)S(1)} collective-permute-done((f32[16,24,128]{2,1,0:T(8,128)S(1)}, f32[16,24,128]{2,1,0:T(8,128)S(1)}, u32[]{:S(2)}, u32[]{:S(2)}) %collective-permute-start.2) | collective-permute-done | bytes 196640 | tf_op jit(solution)/shard_map/ppermute | solution.py:586
  57.5 0.9 collective-permute-done.3.second_ref
  58.3 5.1 %basis.1 = (f32[5,2,2,16,2,8,128]{6,5,4,3,2,1,0:T(8,128)S(1)}, f32[8,8,128]{2,1,0:T(8,128)S(1)}) custom-call(f32[2,16,6,8,128]{4,3,2,1,0:T(8,128)S(1)} %bitcast.87, f32[16,24,128]{2,1,0:T(8,128)S(1)} %collective-permute-done.2.first_ref, f32[16,24,128]{2,1,0:T(8,128)S(1)} %collective-permute-done.3.second_ref, ...), custom_call_target="tpu_custom_call" | custom-call | tf_op jit(solution)/shard_map/basis/pallas_call | solution.py:597
  63.5 13.4 %all_to_all.97.part_ref = f32[8,8,128]{2,1,0:T(8,128)S(1)} all-to-all(f32[8,8,128]{2,1,0:T(8,128)S(1)} %get-tuple-element.183), channel_id=1, replica_groups=mesh['z'=8,'core'=2,'y'=4,'x'=4] {'z'}, dimensions={0} | all-to-all | bytes 65536 | tf_op jit(solution)/shard_map/all_to_all | solution.py:530
  76.8 0.0 copy-done
  76.8 0.9 combine.1
  77.8 15.0 %all_to_all.98.s_ref = f32[32,2,2,8,128]{4,3,2,1,0:T(8,128)S(1)} all-to-all(f32[32,2,2,8,128]{4,3,2,1,0:T(8,128)S(1)} %combine.1), channel_id=1, replica_groups=mesh['z'=8,'core'=2,'y'=4,'x'=4] {'core','y','x'}, dimensions={0} | all-to-all | bytes 1048576 | tf_op jit(solution)/shard_map/all_to_all | solution.py:530
  92.7 0.3 inverse.1
  93.1 21.1 %conditional.1 = (f32[4,2,128,128]{3,2,1,0:T(8,128)S(1)}) conditional(s32[]{:T(128)} %bitcast.35, f32[64,2,8,128]{3,2,1,0:T(8,128)S(1)} %get-tuple-element.187, (f32[4,2,128,128]{3,2,1,0:T(8,128)}, f32[2,128,128]{2,1,0:T(8,128)}, s32[64]{0:T(128)S(1)}) %tuple.72), branch_computations={%region_0.0_spmd, %region_1.9_spmd} | conditional | flops 413107744 | bytes 59532052 | solution.py:658
  93.1 20.8 %all_to_all.92 = f32[16,4,2,8,128]{4,3,2,1,0:T(8,128)S(1)} all-to-all(f32[16,4,2,8,128]{4,3,2,1,0:T(8,128)S(1)} %bitcast.90), channel_id=1, replica_groups=mesh['z'=8,'core'=2,'y'=4,'x'=4] {'z','core'}, dimensions={0} | all-to-all | bytes 1048576 | tf_op jit(solution)/shard_map/cond/branch_0_fun/all_to_all | solution.py:530
  114.2 0.0 copy-start.1
  114.2 0.8 copy-done.1
  (1 shorter events, 0.0 us)
Async XLA Ops:
  49.0 27.8 %copy-start = (s32[64]{0:T(128)S(1)}, s32[64]{0:T(128)}, u32[]{:S(2)}) copy-start(s32[64]{0:T(128)} %param.9) | copy-start | bytes 772
  49.1 6.6 %collective-permute-start.4 = (f32[2,16,2,8,128]{4,3,2,1,0:T(8,128)S(1)}, f32[2,16,2,8,128]{4,3,2,1,0:T(8,128)S(1)}, u32[]{:S(2)}, u32[]{:S(2)}) collective-permute-start(f32[2,16,2,8,128]{4,3,2,1,0:T(8,128)S(1)} %get-tuple-element.180), channel_id=1, source_target_pairs={{0,16},{16,0},{1,17},{17,1},{2,18},{18,2},{3,19},{19,3},{4,20},{20... | collective-permute-start | bytes 786440 | tf_op jit(solution)/shard_map/ppermute | solution.py:585
  50.5 7.0 %collective-permute-start.2 = (f32[16,24,128]{2,1,0:T(8,128)S(1)}, f32[16,24,128]{2,1,0:T(8,128)S(1)}, u32[]{:S(2)}, u32[]{:S(2)}) collective-permute-start(f32[16,24,128]{2,1,0:T(8,128)S(1)} %get-tuple-element.178), channel_id=1, source_target_pairs={{0,32},{32,64},{64,96},{96,128},{128,160},{160,192},{192,224},{48,... | collective-permute-start | bytes 589832 | tf_op jit(solution)/shard_map/ppermute | solution.py:586
  51.7 6.6 %collective-permute-start.3 = (f32[16,24,128]{2,1,0:T(8,128)S(1)}, f32[16,24,128]{2,1,0:T(8,128)S(1)}, u32[]{:S(2)}, u32[]{:S(2)}) collective-permute-start(f32[16,24,128]{2,1,0:T(8,128)S(1)} %get-tuple-element.179), channel_id=1, source_target_pairs={{32,0},{64,32},{96,64},{128,96},{160,128},{192,160},{224,192},{16,... | collective-permute-start | bytes 589832 | tf_op jit(solution)/shard_map/ppermute | solution.py:587
  114.2 0.8 copy-start.1

commit v9 on v8

--- a/solution.py
+++ b/solution.py
@@ -12,6 +12,7 @@
 L = 64
 STEPS = 6
 HALO = 6
+BOTH = 4
 NX = 128
 NZ = 32
 PAIRS = L // 2
@@ -25,7 +26,7 @@
 highest = lax.Precision.HIGHEST
 decay = wrap_factor ** (1.0 / L)
 
-gram_rounding = 1e-6
+gram_rounding = 1.5e-6
 error_allowed = 1.5e-4
 
 
@@ -279,10 +280,12 @@
 
 def inverses_kernel(own_ref, swap_ref, inv_ref, edge_inv_ref):
     slot, z, core = lax.axis_index(SLOTS), lax.axis_index("z"), lax.axis_index("core")
+    upper = lax.broadcasted_iota(jnp.int32, (8, 128), 0) < 4
     shifts_here = slot_shifts()
     shift_a, shift_b, shift_im = (pick(slot, shifts_here[:, i]) for i in range(3))
 
     def prepare(sp, _):
+        edges = {}
         for tile in range(4):
             for zz in range(2):
                 mine, other = own_ref[tile // 2, sp, 4 + zz], swap_ref[tile // 2, sp, zz]
@@ -296,7 +299,11 @@
                 else:
                     inside = z > 0 if tile == 0 else z < lax.axis_size("z") - 1
                     for i in range(3):
-                        edge_inv_ref[i, tile // 3, sp, zz] = jnp.where(inside, found[i], 0.0)
+                        edges[tile, zz, i] = jnp.where(inside, found[i], 0.0)
+                        edge_inv_ref[i, tile // 3, sp, zz] = edges[tile, zz, i]
+        for zz in range(2):
+            for i in range(3):
+                edge_inv_ref[i, 2, sp, zz] = jnp.where(upper, edges[3, zz, i], edges[0, zz, i])
         return 0
 
     lax.fori_loop(0, NZ // 2, prepare, 0, unroll=4)
@@ -306,6 +313,7 @@
     core = lax.axis_index("core")
     lanes = lax.broadcasted_iota(jnp.int32, (8, 128), 1)
     first_lane, last_lane = lanes == 0, lanes == 127
+    upper = lax.broadcasted_iota(jnp.int32, (8, 128), 0) < 4
     blank = jnp.zeros((8, 128), jnp.float32)
 
     for turn in range(2):
@@ -314,10 +322,12 @@
                 u[turn, part, 0, pl.ds(row, 8), :] = blank
                 u[turn, part, NZ + 1, pl.ds(row, 8), :] = blank
 
-    def put(turn, tile, layer, inverse, re, im):
+    def put(turn, tiles, layer, inverse, re, im):
         a, b, c = inverse
-        u[turn, 0, layer, pl.ds(8 + 8 * tile, 8), :] = a * re - c * im
-        u[turn, 1, layer, pl.ds(8 + 8 * tile, 8), :] = b * im + c * re
+        pair = a * re - c * im, b * im + c * re
+        for tile in tiles:
+            for part in range(2):
+                u[turn, part, layer, pl.ds(8 + 8 * tile, 8), :] = pair[part]
 
     def prepare(sp, _):
         for turn in range(2):
@@ -342,7 +352,7 @@
                         shift = (start - wanted) % 8
                         pair.append(pltpu.roll(rows, shift, 0) if shift else rows)
                     re, im = pair
-                put(0, tile, 2 * sp + zz + 1, found, re, im)
+                put(0, (tile,), 2 * sp + zz + 1, found, re, im)
         return 0
 
     lax.fori_loop(0, NZ // 2, prepare, 0, unroll=4)
@@ -352,27 +362,34 @@
             return [own_ref[side, sp, 2 * part + zz] for part in range(2)]
         return [v_ref[j - 1, part, side, sp, zz] for part in range(2)]
 
+    def nearby(old, tile, layer, j):
+        def rows(z_off, x_off):
+            before, behind = (old[layer + z_off, pl.ds(row + x_off, 8), :] for row in (8, 32))
+            if j == 1:
+                return jnp.where(upper, behind, before)
+            return behind if x_off < 0 else before
+
+        if tile != BOTH:
+            def rows(z_off, x_off):
+                return old[layer + z_off, pl.ds(8 + 8 * tile + x_off, 8), :]
+
+        here = rows(0, 0)
+        total = (rows(-1, 0) + rows(1, 0)) + (rows(0, -1) + rows(0, 1))
+        return total + (
+            jnp.where(first_lane, 0.0, pltpu.roll(here, 1, 1)) + jnp.where(last_lane, 0.0, pltpu.roll(here, 127, 1))
+        )
+
     for j in range(STEPS):
+        tiles = (0, 1, 2, 3) if j == 0 else (1, 2, BOTH) if j < STEPS - 1 else (1, 2)
         names = [name for name in entry if name[2] == j + 1 or (j == 0 and name[2] == 0)]
 
-        def step(group, totals, j=j, names=names):
-            by_layer = []
+        def step(group, totals, j=j, names=names, tiles=tiles):
+            found = {}
             for sp in [4 * group + s for s in range(4)]:
-                found = {name: [] for name in names}
                 for zz in range(2):
-                    for tile in range(4) if j < STEPS - 1 else (1, 2):
-                        layer, row = 2 * sp + zz + 1, 8 + 8 * tile
-                        pair = []
-                        for part in range(2):
-                            old = u.at[j % 2, part]
-                            here = old[layer, pl.ds(row, 8), :]
-                            total = old[layer - 1, pl.ds(row, 8), :] + old[layer + 1, pl.ds(row, 8), :]
-                            total = total + (old[layer, pl.ds(row - 1, 8), :] + old[layer, pl.ds(row + 1, 8), :])
-                            total = total + (
-                                jnp.where(first_lane, 0.0, pltpu.roll(here, 1, 1))
-                                + jnp.where(last_lane, 0.0, pltpu.roll(here, 127, 1))
-                            )
-                            pair.append(total)
+                    for tile in tiles:
+                        layer = 2 * sp + zz + 1
+                        pair = [nearby(u.at[j % 2, part], tile, layer, j) for part in range(2)]
                         if tile in (1, 2):
                             side = tile - 1
                             if j < STEPS - 1:
@@ -382,18 +399,19 @@
                             for kind, i, k in names:
                                 a, b = known[i], known[k]
                                 if kind == "x":
-                                    found[kind, i, k].append(a[0] * b[1] - a[1] * b[0])
+                                    product = a[0] * b[1] - a[1] * b[0]
                                 else:
                                     part = ("re", "im").index(kind)
-                                    found[kind, i, k].append(a[part] * b[part])
+                                    product = a[part] * b[part]
+                                name = kind, i, k
+                                found[name] = found[name] + product if name in found else product
                         if j < STEPS - 1:
                             if tile in (1, 2):
                                 inverse = [inv_ref[i, tile - 1, sp, zz] for i in range(3)]
                             else:
-                                inverse = [edge_inv[i, tile // 3, sp, zz] for i in range(3)]
-                            put((j + 1) % 2, tile, layer, inverse, *pair)
-                by_layer.append([tree_sum(found[name]) for name in names])
-            return tuple(t + tree_sum(list(parts)) for t, parts in zip(totals, zip(*by_layer)))
+                                inverse = [edge_inv[i, (0, None, None, 1, 2)[tile], sp, zz] for i in range(3)]
+                            put((j + 1) % 2, (0, 3) if tile == BOTH else (tile,), layer, inverse, *pair)
+            return tuple(t + found[name] for t, name in zip(totals, names))
 
         totals = lax.fori_loop(0, NZ // 8, step, tuple(blank for _ in names), unroll=2)
         for name, total in zip(names, totals):
@@ -587,7 +605,7 @@
     second = lax.ppermute(second, TM, downs[0] + ups[1])
     inverses, edge_inverses = pl.pallas_call(
         inverses_kernel,
-        out_shape=(f32(3, 2, 16, 2, 8, 128), f32(3, 2, 16, 2, 8, 128)),
+        out_shape=(f32(3, 2, 16, 2, 8, 128), f32(3, 3, 16, 2, 8, 128)),
         in_specs=[VMEM, VMEM],
         out_specs=(VMEM, VMEM),
         compiler_params=room(2),

time: 115 us -> 115 us (level)
  no operation moved by 1% of the time
where the time goes in v9:
time: 115 us; the launch traced here: 114 us
  blocking collectives  96.8 us (84%)
  Pallas kernels  7.56 us (7%)
  starting transfers between devices  6.63 us (6%)
  waiting for transfers between devices  2.21 us (2%)
    all_to_all x5, blocking collectives, exchanged(): return lax.all_to_all(blocks, axes, split_axis=0, concat_axis=0, tiled=True)  96.8 us
    pallas_call x1, Pallas kernels, together(): pl.pallas_call(basis_kernel, out_shape=(f32(STEPS - 1, 2, 2, 16, 2, 8, 12...  4.51 us
    ppermute x1, starting transfers between devices, together(): second = lax.ppermute(second, TM, downs[0] + ups[1])  4 us
  transfers between devices with their start and end apart: 3, of which 2 were waited for; matrix products, arithmetic and copies ran while one was open for 0% of the time, Pallas kernels for 0%

profile of v9, /device:TPU:1, one launch (start us, length us, event | category | flops | bytes accessed | tf_op | source)
XLA Modules:
  0.0 114.3 jit_solution(5029703221057275778)
XLA Ops:
  0.0 1.2 %bands.1 = (f32[16,4,2,8,128]{4,3,2,1,0:T(8,128)S(1)}, f32[2,2,8,128]{3,2,1,0:T(8,128)S(1)}) custom-call(f32[4,2,128,128]{3,2,1,0:T(8,128)} %x_ref.1, f32[2,128,128]{2,1,0:T(8,128)} %a_ref.1), custom_call_target="tpu_custom_call" | custom-call | tf_op jit(solution)/shard_map/bands/pallas_call | solution.py:574
  1.2 27.0 %all_to_all.95 = f32[16,4,2,8,128]{4,3,2,1,0:T(8,128)S(1)} all-to-all(f32[16,4,2,8,128]{4,3,2,1,0:T(8,128)S(1)} %get-tuple-element.176), channel_id=1, replica_groups=mesh['z'=8,'core'=2,'y'=4,'x'=4] {'z','core'}, dimensions={0} | all-to-all | bytes 1048576 | tf_op jit(solution)/shard_map/all_to_all | solution.py:548
  28.1 0.2 forward.1
  28.4 20.7 %all_to_all.96 = f32[32,6,8,128]{3,2,1,0:T(8,128)S(1)} all-to-all(f32[32,6,8,128]{3,2,1,0:T(8,128)S(1)} %forward.1), channel_id=1, replica_groups=mesh['z'=8,'core'=2,'y'=4,'x'=4] {'core','y','x'}, dimensions={0} | all-to-all | bytes 1572864 | tf_op jit(solution)/shard_map/all_to_all | solution.py:548
  49.0 0.1 edges.1
  49.1 0.0 copy-start
  49.1 1.3 %collective-permute-start.4 = (f32[2,16,2,8,128]{4,3,2,1,0:T(8,128)S(1)}, f32[2,16,2,8,128]{4,3,2,1,0:T(8,128)S(1)}, u32[]{:S(2)}, u32[]{:S(2)}) collective-permute-start(f32[2,16,2,8,128]{4,3,2,1,0:T(8,128)S(1)} %get-tuple-element.180), channel_id=1, source_target_pairs={{0,16},{16,0},{1,17},{17,1},{2,18},{18,2},{3,19},{19,3},{4,20},{20... | collective-permute-start | bytes 786440 | tf_op jit(solution)/shard_map/ppermute | solution.py:603
  50.5 1.3 %collective-permute-start.2 = (f32[16,24,128]{2,1,0:T(8,128)S(1)}, f32[16,24,128]{2,1,0:T(8,128)S(1)}, u32[]{:S(2)}, u32[]{:S(2)}) collective-permute-start(f32[16,24,128]{2,1,0:T(8,128)S(1)} %get-tuple-element.178), channel_id=1, source_target_pairs={{0,32},{32,64},{64,96},{96,128},{128,160},{160,192},{192,224},{48,... | collective-permute-start | bytes 589832 | tf_op jit(solution)/shard_map/ppermute | solution.py:604
  51.7 4.0 %collective-permute-start.3 = (f32[16,24,128]{2,1,0:T(8,128)S(1)}, f32[16,24,128]{2,1,0:T(8,128)S(1)}, u32[]{:S(2)}, u32[]{:S(2)}) collective-permute-start(f32[16,24,128]{2,1,0:T(8,128)S(1)} %get-tuple-element.179), channel_id=1, source_target_pairs={{32,0},{64,32},{96,64},{128,96},{160,128},{192,160},{224,192},{16,... | collective-permute-start | bytes 589832 | tf_op jit(solution)/shard_map/ppermute | solution.py:605
  55.8 0.0 collective-permute-done.4.swap_ref
  55.8 0.4 inverses.1
  56.1 1.3 %collective-permute-done.2.first_ref = f32[16,24,128]{2,1,0:T(8,128)S(1)} collective-permute-done((f32[16,24,128]{2,1,0:T(8,128)S(1)}, f32[16,24,128]{2,1,0:T(8,128)S(1)}, u32[]{:S(2)}, u32[]{:S(2)}) %collective-permute-start.2) | collective-permute-done | bytes 196640 | tf_op jit(solution)/shard_map/ppermute | solution.py:604
  57.5 0.9 collective-permute-done.3.second_ref
  58.3 4.5 %basis.1 = (f32[5,2,2,16,2,8,128]{6,5,4,3,2,1,0:T(8,128)S(1)}, f32[8,8,128]{2,1,0:T(8,128)S(1)}) custom-call(f32[2,16,6,8,128]{4,3,2,1,0:T(8,128)S(1)} %bitcast.87, f32[16,24,128]{2,1,0:T(8,128)S(1)} %collective-permute-done.2.first_ref, f32[16,24,128]{2,1,0:T(8,128)S(1)} %collective-permute-done.3.second_ref, ...), custom_call_target="tpu_custom_call" | custom-call | tf_op jit(solution)/shard_map/basis/pallas_call | solution.py:615
  62.8 13.4 %all_to_all.97.part_ref = f32[8,8,128]{2,1,0:T(8,128)S(1)} all-to-all(f32[8,8,128]{2,1,0:T(8,128)S(1)} %get-tuple-element.183), channel_id=1, replica_groups=mesh['z'=8,'core'=2,'y'=4,'x'=4] {'z'}, dimensions={0} | all-to-all | bytes 65536 | tf_op jit(solution)/shard_map/all_to_all | solution.py:548
  76.2 0.0 copy-done
  76.2 0.9 combine.1
  77.1 15.0 %all_to_all.98.s_ref = f32[32,2,2,8,128]{4,3,2,1,0:T(8,128)S(1)} all-to-all(f32[32,2,2,8,128]{4,3,2,1,0:T(8,128)S(1)} %combine.1), channel_id=1, replica_groups=mesh['z'=8,'core'=2,'y'=4,'x'=4] {'core','y','x'}, dimensions={0} | all-to-all | bytes 1048576 | tf_op jit(solution)/shard_map/all_to_all | solution.py:548
  92.1 0.3 inverse.1
  92.5 21.1 %conditional.1 = (f32[4,2,128,128]{3,2,1,0:T(8,128)S(1)}) conditional(s32[]{:T(128)} %bitcast.35, f32[64,2,8,128]{3,2,1,0:T(8,128)S(1)} %get-tuple-element.187, (f32[4,2,128,128]{3,2,1,0:T(8,128)}, f32[2,128,128]{2,1,0:T(8,128)}, s32[64]{0:T(128)S(1)}) %tuple.72), branch_computations={%region_0.0_spmd, %region_1.9_spmd} | conditional | flops 413107744 | bytes 59532052 | solution.py:676
  92.5 20.8 %all_to_all.92 = f32[16,4,2,8,128]{4,3,2,1,0:T(8,128)S(1)} all-to-all(f32[16,4,2,8,128]{4,3,2,1,0:T(8,128)S(1)} %bitcast.90), channel_id=1, replica_groups=mesh['z'=8,'core'=2,'y'=4,'x'=4] {'z','core'}, dimensions={0} | all-to-all | bytes 1048576 | tf_op jit(solution)/shard_map/cond/branch_0_fun/all_to_all | solution.py:548
  113.5 0.0 copy-start.1
  113.5 0.8 copy-done.1
  (1 shorter events, 0.0 us)
Async XLA Ops:
  49.1 27.1 %copy-start = (s32[64]{0:T(128)S(1)}, s32[64]{0:T(128)}, u32[]{:S(2)}) copy-start(s32[64]{0:T(128)} %param.9) | copy-start | bytes 772
  49.1 6.6 %collective-permute-start.4 = (f32[2,16,2,8,128]{4,3,2,1,0:T(8,128)S(1)}, f32[2,16,2,8,128]{4,3,2,1,0:T(8,128)S(1)}, u32[]{:S(2)}, u32[]{:S(2)}) collective-permute-start(f32[2,16,2,8,128]{4,3,2,1,0:T(8,128)S(1)} %get-tuple-element.180), channel_id=1, source_target_pairs={{0,16},{16,0},{1,17},{17,1},{2,18},{18,2},{3,19},{19,3},{4,20},{20... | collective-permute-start | bytes 786440 | tf_op jit(solution)/shard_map/ppermute | solution.py:603
  50.5 7.0 %collective-permute-start.2 = (f32[16,24,128]{2,1,0:T(8,128)S(1)}, f32[16,24,128]{2,1,0:T(8,128)S(1)}, u32[]{:S(2)}, u32[]{:S(2)}) collective-permute-start(f32[16,24,128]{2,1,0:T(8,128)S(1)} %get-tuple-element.178), channel_id=1, source_target_pairs={{0,32},{32,64},{64,96},{96,128},{128,160},{160,192},{192,224},{48,... | collective-permute-start | bytes 589832 | tf_op jit(solution)/shard_map/ppermute | solution.py:604
  51.7 6.6 %collective-permute-start.3 = (f32[16,24,128]{2,1,0:T(8,128)S(1)}, f32[16,24,128]{2,1,0:T(8,128)S(1)}, u32[]{:S(2)}, u32[]{:S(2)}) collective-permute-start(f32[16,24,128]{2,1,0:T(8,128)S(1)} %get-tuple-element.179), channel_id=1, source_target_pairs={{32,0},{64,32},{96,64},{128,96},{160,128},{192,160},{224,192},{16,... | collective-permute-start | bytes 589832 | tf_op jit(solution)/shard_map/ppermute | solution.py:605
  113.5 0.8 copy-start.1

commit v10 on v9

--- a/solution.py
+++ b/solution.py
@@ -475,7 +475,6 @@
         if m == STEPS - 1:
             break
         rest = (1.0 - coef[0], -coef[1])
-        padded = [None] + poly + [None]
         following = []
         for j in range(len(poly) + 1):
             kept = multiplied(rest, poly[j]) if j < len(poly) else (none, none)
@@ -600,9 +599,9 @@
     )(own)
     ups = [[(2 * i + core, 2 * i + 2 + core) for i in range(chips - 1)] for core in range(2)]
     downs = [[(b, a) for a, b in pairs] for pairs in ups]
-    swap = lax.ppermute(swap, "core", [(0, 1), (1, 0)])
     first = lax.ppermute(first, TM, ups[0] + downs[1])
     second = lax.ppermute(second, TM, downs[0] + ups[1])
+    swap = lax.ppermute(swap, "core", [(0, 1), (1, 0)])
     inverses, edge_inverses = pl.pallas_call(
         inverses_kernel,
         out_shape=(f32(3, 2, 16, 2, 8, 128), f32(3, 3, 16, 2, 8, 128)),
@@ -666,19 +665,19 @@
     )(*(in_hbm(a) for a in arrays))
 
 
-def to_steps(values, shape):
-    bands = exchanged(values.reshape(16, 4, 2, 8, 128), TM)
-    return bands.transpose(1, 2, 0, 3, 4).reshape(shape)
+def to_bands(steps):
+    return steps.reshape(4, 2, 16, 8, 128).transpose(2, 0, 1, 3, 4)
 
 
 def body(residual, absorption, counts):
     values, failed, arguments = together(residual, absorption, counts)
-    return lax.cond(
+    bands = lax.cond(
         failed[0] > 0,
-        lambda r, a, c, v: stepwise(*taken(r, a), c),
-        lambda r, a, c, v: to_steps(v, r.shape),
+        lambda r, a, c, v: to_bands(stepwise(*taken(r, a), c)),
+        lambda r, a, c, v: exchanged(v.reshape(16, 4, 2, 8, 128), TM),
         *arguments, values,
     )
+    return bands.transpose(1, 2, 0, 3, 4).reshape(residual.shape)
 
 
 def solution(mesh):

time: 115 us -> 115 us (level)
  no operation moved by 1% of the time
where the time goes in v10:
time: 115 us
  blocking collectives  96.8 us (84%)
  Pallas kernels  7.56 us (7%)
  starting transfers between devices  6.63 us (6%)
  waiting for transfers between devices  2.21 us (2%)
    all_to_all x5, blocking collectives, exchanged(): return lax.all_to_all(blocks, axes, split_axis=0, concat_axis=0, tiled=True)  96.8 us
    pallas_call x1, Pallas kernels, together(): pl.pallas_call(basis_kernel, out_shape=(f32(STEPS - 1, 2, 2, 16, 2, 8, 12...  4.51 us
    ppermute x1, starting transfers between devices, together(): second = lax.ppermute(second, TM, downs[0] + ups[1])  4 us
  transfers between devices with their start and end apart: 3, of which 2 were waited for; matrix products, arithmetic and copies ran while one was open for 0% of the time, Pallas kernels for 0%

profile of v10, /device:TPU:1, one launch (start us, length us, event | category | flops | bytes accessed | tf_op | source)
XLA Modules:
  0.0 114.6 jit_solution(169374423679466215)
XLA Ops:
  0.0 1.2 %bands.1 = (f32[16,4,2,8,128]{4,3,2,1,0:T(8,128)S(1)}, f32[2,2,8,128]{3,2,1,0:T(8,128)S(1)}) custom-call(f32[4,2,128,128]{3,2,1,0:T(8,128)} %x_ref.1, f32[2,128,128]{2,1,0:T(8,128)} %a_ref.1), custom_call_target="tpu_custom_call" | custom-call | tf_op jit(solution)/shard_map/bands/pallas_call | solution.py:573
  1.2 27.0 %all_to_all.91 = f32[16,4,2,8,128]{4,3,2,1,0:T(8,128)S(1)} all-to-all(f32[16,4,2,8,128]{4,3,2,1,0:T(8,128)S(1)} %get-tuple-element.176), channel_id=1, replica_groups=mesh['z'=8,'core'=2,'y'=4,'x'=4] {'z','core'}, dimensions={0} | all-to-all | bytes 1048576 | tf_op jit(solution)/shard_map/all_to_all | solution.py:547
  28.1 0.2 forward.1
  28.4 20.7 %all_to_all.92 = f32[32,6,8,128]{3,2,1,0:T(8,128)S(1)} all-to-all(f32[32,6,8,128]{3,2,1,0:T(8,128)S(1)} %forward.1), channel_id=1, replica_groups=mesh['z'=8,'core'=2,'y'=4,'x'=4] {'core','y','x'}, dimensions={0} | all-to-all | bytes 1572864 | tf_op jit(solution)/shard_map/all_to_all | solution.py:547
  49.0 0.1 edges.1
  49.1 0.0 copy-start
  49.1 1.3 %collective-permute-start.4 = (f32[2,16,2,8,128]{4,3,2,1,0:T(8,128)S(1)}, f32[2,16,2,8,128]{4,3,2,1,0:T(8,128)S(1)}, u32[]{:S(2)}, u32[]{:S(2)}) collective-permute-start(f32[2,16,2,8,128]{4,3,2,1,0:T(8,128)S(1)} %get-tuple-element.180), channel_id=1, source_target_pairs={{0,16},{16,0},{1,17},{17,1},{2,18},{18,2},{3,19},{19,3},{4,20},{20... | collective-permute-start | bytes 786440 | tf_op jit(solution)/shard_map/ppermute | solution.py:604
  50.5 1.3 %collective-permute-start.2 = (f32[16,24,128]{2,1,0:T(8,128)S(1)}, f32[16,24,128]{2,1,0:T(8,128)S(1)}, u32[]{:S(2)}, u32[]{:S(2)}) collective-permute-start(f32[16,24,128]{2,1,0:T(8,128)S(1)} %get-tuple-element.178), channel_id=1, source_target_pairs={{0,32},{32,64},{64,96},{96,128},{128,160},{160,192},{192,224},{48,... | collective-permute-start | bytes 589832 | tf_op jit(solution)/shard_map/ppermute | solution.py:602
  51.7 4.0 %collective-permute-start.3 = (f32[16,24,128]{2,1,0:T(8,128)S(1)}, f32[16,24,128]{2,1,0:T(8,128)S(1)}, u32[]{:S(2)}, u32[]{:S(2)}) collective-permute-start(f32[16,24,128]{2,1,0:T(8,128)S(1)} %get-tuple-element.179), channel_id=1, source_target_pairs={{32,0},{64,32},{96,64},{128,96},{160,128},{192,160},{224,192},{16,... | collective-permute-start | bytes 589832 | tf_op jit(solution)/shard_map/ppermute | solution.py:603
  55.8 0.0 collective-permute-done.4.swap_ref
  55.8 0.4 inverses.1
  56.1 1.3 %collective-permute-done.2.first_ref = f32[16,24,128]{2,1,0:T(8,128)S(1)} collective-permute-done((f32[16,24,128]{2,1,0:T(8,128)S(1)}, f32[16,24,128]{2,1,0:T(8,128)S(1)}, u32[]{:S(2)}, u32[]{:S(2)}) %collective-permute-start.2) | collective-permute-done | bytes 196640 | tf_op jit(solution)/shard_map/ppermute | solution.py:602
  57.5 0.9 collective-permute-done.3.second_ref
  58.3 4.5 %basis.1 = (f32[5,2,2,16,2,8,128]{6,5,4,3,2,1,0:T(8,128)S(1)}, f32[8,8,128]{2,1,0:T(8,128)S(1)}) custom-call(f32[2,16,6,8,128]{4,3,2,1,0:T(8,128)S(1)} %bitcast.82, f32[16,24,128]{2,1,0:T(8,128)S(1)} %collective-permute-done.2.first_ref, f32[16,24,128]{2,1,0:T(8,128)S(1)} %collective-permute-done.3.second_ref, ...), custom_call_target="tpu_custom_call" | custom-call | tf_op jit(solution)/shard_map/basis/pallas_call | solution.py:614
  62.8 13.4 %all_to_all.93.part_ref = f32[8,8,128]{2,1,0:T(8,128)S(1)} all-to-all(f32[8,8,128]{2,1,0:T(8,128)S(1)} %get-tuple-element.183), channel_id=1, replica_groups=mesh['z'=8,'core'=2,'y'=4,'x'=4] {'z'}, dimensions={0} | all-to-all | bytes 65536 | tf_op jit(solution)/shard_map/all_to_all | solution.py:547
  76.2 0.0 copy-done
  76.2 0.9 combine.1
  77.1 15.0 %all_to_all.94.s_ref = f32[32,2,2,8,128]{4,3,2,1,0:T(8,128)S(1)} all-to-all(f32[32,2,2,8,128]{4,3,2,1,0:T(8,128)S(1)} %combine.1), channel_id=1, replica_groups=mesh['z'=8,'core'=2,'y'=4,'x'=4] {'core','y','x'}, dimensions={0} | all-to-all | bytes 1048576 | tf_op jit(solution)/shard_map/all_to_all | solution.py:547
  92.1 0.3 inverse.1
  92.5 21.3 %conditional.1 = (f32[16,4,2,8,128]{4,3,2,1,0:T(8,128)S(1)}) conditional(s32[]{:T(128)} %bitcast.31, f32[64,2,8,128]{3,2,1,0:T(8,128)S(1)} %get-tuple-element.187, (f32[4,2,128,128]{3,2,1,0:T(8,128)}, f32[2,128,128]{2,1,0:T(8,128)}, s32[64]{0:T(128)S(1)}) %tuple.70), branch_computations={%region_0.0_spmd, %region_1.9_spmd} | conditional | flops 413107744 | bytes 58483476 | solution.py:674
  92.5 0.2 copy.58
  92.7 20.8 %all_to_all.88 = f32[16,4,2,8,128]{4,1,3,2,0:T(4,128)S(1)} all-to-all(f32[16,4,2,8,128]{4,1,3,2,0:T(4,128)S(1)} %copy.58), channel_id=1, replica_groups=mesh['z'=8,'core'=2,'y'=4,'x'=4] {'z','core'}, dimensions={0} | all-to-all | bytes 1048576 | tf_op jit(solution)/shard_map/cond/branch_0_fun/all_to_all | solution.py:547
  113.8 0.8 copy_bitcast_fusion.3
  (1 shorter events, 0.0 us)
Async XLA Ops:
  49.1 27.1 %copy-start = (s32[64]{0:T(128)S(1)}, s32[64]{0:T(128)}, u32[]{:S(2)}) copy-start(s32[64]{0:T(128)} %param.9) | copy-start | bytes 772
  49.1 6.6 %collective-permute-start.4 = (f32[2,16,2,8,128]{4,3,2,1,0:T(8,128)S(1)}, f32[2,16,2,8,128]{4,3,2,1,0:T(8,128)S(1)}, u32[]{:S(2)}, u32[]{:S(2)}) collective-permute-start(f32[2,16,2,8,128]{4,3,2,1,0:T(8,128)S(1)} %get-tuple-element.180), channel_id=1, source_target_pairs={{0,16},{16,0},{1,17},{17,1},{2,18},{18,2},{3,19},{19,3},{4,20},{20... | collective-permute-start | bytes 786440 | tf_op jit(solution)/shard_map/ppermute | solution.py:604
  50.5 7.0 %collective-permute-start.2 = (f32[16,24,128]{2,1,0:T(8,128)S(1)}, f32[16,24,128]{2,1,0:T(8,128)S(1)}, u32[]{:S(2)}, u32[]{:S(2)}) collective-permute-start(f32[16,24,128]{2,1,0:T(8,128)S(1)} %get-tuple-element.178), channel_id=1, source_target_pairs={{0,32},{32,64},{64,96},{96,128},{128,160},{160,192},{192,224},{48,... | collective-permute-start | bytes 589832 | tf_op jit(solution)/shard_map/ppermute | solution.py:602
  51.7 6.6 %collective-permute-start.3 = (f32[16,24,128]{2,1,0:T(8,128)S(1)}, f32[16,24,128]{2,1,0:T(8,128)S(1)}, u32[]{:S(2)}, u32[]{:S(2)}) collective-permute-start(f32[16,24,128]{2,1,0:T(8,128)S(1)} %get-tuple-element.179), channel_id=1, source_target_pairs={{32,0},{64,32},{96,64},{128,96},{160,128},{192,160},{224,192},{16,... | collective-permute-start | bytes 589832 | tf_op jit(solution)/shard_map/ppermute | solution.py:603
